TPU v7x, 256 devices: a whole 4x4x8 slice. The times are simulated.
256 devices in a mesh: gx: 4 (over z_lo), gy: 8 (over x, core), tracer: 8 (over z_hi, y).
Axes of the slice: x: 4, y: 4, z: 8 (z_hi: 2, z_lo: 4; z = z_hi * 4 + z_lo), core: 2. Of those that a mesh axis runs over, the one named last changes fastest.
Arguments:
- biology_concentration: float32 [24, 8, 512, 512], P('tracer', None, 'gy', 'gx'), may hold values from 0.1 to 2
- flow_vectors: float32 [2, 8, 512, 512], P(None, 'tracer', 'gy', 'gx'), may hold values from -0.25 to 0.25
- thermal_anomaly: float32 [8, 512, 512], P('tracer', 'gy', 'gx'), may hold values from -6 to 6
- diffusivity_profile: float32 [8, 512, 512], P(None, 'gy', 'gx'), may hold values from 0.02 to 0.24
- solar_flux_field: float32 [512, 512], P('gy', 'gx'), may hold values from 0.5 to 2
- ecosystem_coefficients: float32 [24], P('tracer'), may hold values from 0.05 to 0.5
- ocean_indicator: int32 [512, 512], P('gy', 'gx'), may hold values 0 or 1
- floor_tier_number: int32 [512, 512], P('gy', 'gx'), may hold values from 1 to 8
Outputs:
- tracers_out: float32 [24, 8, 512, 512], P('tracer', None, 'gy', 'gx')
- currents_out: float32 [2, 8, 512, 512], P(None, 'tracer', 'gy', 'gx')
- temperature_out: float32 [8, 512, 512], P('tracer', 'gy', 'gx')
All inputs are finite; a program needn't handle non-finite values. No bound on the sum of `ocean_indicator` on one device may be relied on, other than what follows from the above.
Results may differ from a plain program's by a relative error of at most 0.0003.
Values sent between devices are 32-bit elements; how exact they have to be, the bound alone decides.
No kernel may reach another device: no remote copies, remote signals or barrier semaphores. Data moves between devices by JAX's collectives and lax.ppermute only.
A program may use at most 64 MiB of HBM per device.

v0:
```python
import jax
import jax.numpy as jnp
from jax import lax
from jax.sharding import PartitionSpec as P

STEPS = 2


viscosity = 0.2
water_absorb = 0.04
plankton_absorb = 0.03
heat_share = 0.5
light_half = 0.3
nutrient_half = 0.5


def padded_2(value, sides, width):
    edges = {}
    for axis, dim in sides:
        devices, length = (lax.axis_size(axis), value.shape[dim])
        up = [(i, (i + 1) % devices) for i in range(devices - 1)]
        last = lax.slice_in_dim(value, length - width, length, axis=dim)
        leading = lax.slice_in_dim(value, 0, width, axis=dim)
        edges[dim] = (
            lax.ppermute(last, axis, up),
            lax.ppermute(leading, axis, [(b, a) for a, b in up]),
        )
    done = []
    for _, dim in sides:
        low, high = edges[dim]
        around = [(width, width) if d in done else (0, 0) for d in range(value.ndim)]
        value = jnp.concatenate([jnp.pad(low, around), value, jnp.pad(high, around)], axis=dim)
        done.append(dim)
    return value


def from_everyone(value, axis):
    devices = lax.axis_size(axis)
    return lax.all_to_all(
        jnp.broadcast_to(value[None], (devices, *value.shape)), axis, 0, 0, tiled=True
    )


def over_copies(value, axis):
    return from_everyone(value, axis).sum(axis=0)


def laid_out(parts, dim):
    parts = jnp.moveaxis(parts, 0, dim)
    shape = parts.shape
    return parts.reshape(*shape[:dim], shape[dim] * shape[dim + 1], *shape[dim + 2 :])


def collect(value, axis, dim):
    parts = from_everyone(value, axis)
    return laid_out(parts, dim)


def shift_left(values):
    return jnp.concatenate([values[..., 1:], jnp.zeros_like(values[..., :1])], -1)


def shift_up(values):
    return jnp.concatenate([values[..., 1:, :], jnp.zeros_like(values[..., :1, :])], -2)


def minmod(former, latter):
    return (
        0.5 * (jnp.sign(former) + jnp.sign(latter)) * jnp.minimum(jnp.abs(former), jnp.abs(latter))
    )


def limited(behind, center, ahead_one, beyond, velocity):
    slope_mid = ahead_one - center
    forward = velocity * (center + 0.5 * (1.0 - velocity) * minmod(slope_mid, center - behind))
    backward = velocity * (
        ahead_one - 0.5 * (1.0 + velocity) * minmod(slope_mid, beyond - ahead_one)
    )
    return jnp.where(velocity >= 0.0, forward, backward)


def advect_padded(padded, east_pad, north_pad):
    water_span_tiers = padded.shape[-2] - 4
    width_cells = padded.shape[-1] - 4
    row_band = padded[..., 2 : water_span_tiers + 2, :]
    flux_x = limited(
        row_band[..., 0 : width_cells + 1],
        row_band[..., 1 : width_cells + 2],
        row_band[..., 2 : width_cells + 3],
        row_band[..., 3 : width_cells + 4],
        east_pad[:, 2 : water_span_tiers + 2, 1 : width_cells + 2],
    )
    col_band = padded[..., 2 : width_cells + 2]
    flux_y = limited(
        col_band[..., 0 : water_span_tiers + 1, :],
        col_band[..., 1 : water_span_tiers + 2, :],
        col_band[..., 2 : water_span_tiers + 3, :],
        col_band[..., 3 : water_span_tiers + 4, :],
        north_pad[:, 1 : water_span_tiers + 2, 2 : width_cells + 2],
    )
    inner_cells = padded[..., 2 : water_span_tiers + 2, 2 : width_cells + 2]
    return (
        inner_cells
        - (flux_x[..., 1:] - flux_x[..., :-1])
        - (flux_y[..., 1:, :] - flux_y[..., :-1, :])
    )


def vertical_mix(tracer_field, coupling):
    level_below = jnp.concatenate([tracer_field[:, 1:], jnp.zeros_like(tracer_field[:, :1])], 1)
    level_above = jnp.concatenate([jnp.zeros_like(tracer_field[:, :1]), tracer_field[:, :-1]], 1)
    coupling_above = jnp.concatenate([jnp.zeros_like(coupling[:1]), coupling[:-1]], 0)
    return (
        tracer_field
        + coupling * (level_below - tracer_field)
        - coupling_above * (tracer_field - level_above)
    )


def light_fields(absorb, solar_flux_field):
    attenuation = water_absorb + plankton_absorb * absorb
    depth_top = jnp.cumsum(attenuation, 0) - attenuation
    light_mid = solar_flux_field * jnp.exp(-depth_top - 0.5 * attenuation)
    heating = (
        heat_share * solar_flux_field * (jnp.exp(-depth_top) - jnp.exp(-depth_top - attenuation))
    )
    return (light_mid, heating)


def biology(tracer_field, light_mid, rate_values, wet_full):
    tracer_count = tracer_field.shape[0]
    triples = tracer_field.reshape((tracer_count // 3, 3) + tracer_field.shape[1:])
    rate_sets = rate_values.reshape(tracer_count // 3, 3)
    nutrient, plankton, detritus = (triples[:, 0], triples[:, 1], triples[:, 2])
    growth = rate_sets[:, 0][:, None, None, None]
    mortal = rate_sets[:, 1][:, None, None, None]
    recycle_rate = rate_sets[:, 2][:, None, None, None]
    uptake = (
        growth
        * (light_mid / (light_mid + light_half))
        * plankton
        * nutrient
        / (jnp.abs(nutrient) + nutrient_half)
    )
    mortality = mortal * plankton
    recycled = recycle_rate * detritus
    result = jnp.stack(
        [
            nutrient - uptake + recycled,
            plankton + uptake - mortality,
            detritus + mortality - recycled,
        ],
        1,
    )
    return result.reshape(tracer_field.shape) * wet_full


def flux_pieces(east_pad, north_pad):
    return jnp.stack([east_pad, north_pad])


def ocean_step(currents_now, wet_pad, coriolis):
    padded = padded_2(currents_now, (("gx", 3), ("gy", 2)), 1)
    open_east = wet_pad * shift_left(wet_pad)
    open_north = wet_pad * shift_up(wet_pad)
    east_pad = open_east * padded[0]
    north_pad = open_north * padded[1]
    center = padded[..., 1:-1, 1:-1]
    laplace_sum = (
        padded[..., 1:-1, 2:]
        + padded[..., 1:-1, :-2]
        + padded[..., 2:, 1:-1]
        + padded[..., :-2, 1:-1]
        - 4.0 * center
    )
    next_east = open_east[:, 1:-1, 1:-1] * (
        center[0] + coriolis * center[1] + viscosity * laplace_sum[0]
    )
    next_north = open_north[:, 1:-1, 1:-1] * (
        center[1] - coriolis * center[0] + viscosity * laplace_sum[1]
    )
    return (jnp.stack([next_east, next_north]), east_pad, north_pad)


def heat_step(warming_forcing, east_pad, north_pad, heating, wet_own):
    padded = padded_2(warming_forcing, (("gx", 2), ("gy", 1)), 1)
    water_span_tiers = warming_forcing.shape[1]
    width_cells = warming_forcing.shape[2]
    speed_x = east_pad[:, 1 : water_span_tiers + 1, 0 : width_cells + 1]
    eastward = (
        jnp.maximum(speed_x, 0.0) * padded[:, 1 : water_span_tiers + 1, 0 : width_cells + 1]
        + jnp.minimum(speed_x, 0.0) * padded[:, 1 : water_span_tiers + 1, 1 : width_cells + 2]
    )
    speed_y = north_pad[:, 0 : water_span_tiers + 1, 1 : width_cells + 1]
    northward = (
        jnp.maximum(speed_y, 0.0) * padded[:, 0 : water_span_tiers + 1, 1 : width_cells + 1]
        + jnp.minimum(speed_y, 0.0) * padded[:, 1 : water_span_tiers + 2, 1 : width_cells + 1]
    )
    change = (
        eastward[..., 1:] - eastward[..., :-1] + (northward[..., 1:, :] - northward[..., :-1, :])
    )
    return wet_own * (warming_forcing - change + heating)


def tracer_step(
    tracer_field,
    fluxes,
    coupling,
    wet_inner,
    solar_flux_field,
    ecosystem_coefficients,
    level_start,
    vertical_tier_total,
):
    tracer_count = tracer_field.shape[0]
    padded = padded_2(tracer_field, (("gx", 3), ("gy", 2)), 2)
    widen = ((0, 0), (1, 1), (1, 1))
    east_wide = jnp.pad(fluxes[0], widen)
    north_wide = jnp.pad(fluxes[1], widen)
    tracer_field = advect_padded(padded, east_wide, north_wide) * wet_inner
    tracer_field = vertical_mix(tracer_field, coupling)
    absorb = jnp.sum(tracer_field.reshape((tracer_count // 3, 3) + tracer_field.shape[1:])[:, 1], 0)
    absorb_total = over_copies(absorb, "tracer")
    light_mid, heating = light_fields(absorb_total, solar_flux_field)
    heating = lax.dynamic_slice_in_dim(heating, level_start, vertical_tier_total, 0)
    tracer_field = biology(tracer_field, light_mid, ecosystem_coefficients, wet_inner)
    return (tracer_field, heating)


def per_device(
    biology_concentration,
    flow_vectors,
    thermal_anomaly,
    diffusivity_profile,
    solar_flux_field,
    ecosystem_coefficients,
    ocean_indicator,
    floor_tier_number,
):
    depth_layers = diffusivity_profile.shape[0]
    vertical_tier_total = thermal_anomaly.shape[0]
    level_start = lax.axis_index("tracer") * vertical_tier_total
    water_span_tiers = thermal_anomaly.shape[1]
    depth_pad = padded_2(jnp.stack([ocean_indicator, floor_tier_number]), (("gx", 2), ("gy", 1)), 1)
    depth_index = jnp.arange(depth_layers, dtype=jnp.int32)[:, None, None]
    wet_pad = (depth_pad[0][None] * (depth_index < depth_pad[1][None]).astype(jnp.int32)).astype(
        jnp.float32
    )
    wet_inner = wet_pad[:, 1:-1, 1:-1]
    wet_below = jnp.concatenate([wet_inner[1:], jnp.zeros_like(wet_inner[:1])], 0)
    coupling = diffusivity_profile * wet_inner * wet_below
    wet_own_pad = lax.dynamic_slice_in_dim(wet_pad, level_start, vertical_tier_total, 0)
    wet_own = wet_own_pad[:, 1:-1, 1:-1]
    grid_rows = water_span_tiers * lax.axis_size("gy")
    row_index = lax.axis_index("gy") * water_span_tiers + jnp.arange(
        water_span_tiers, dtype=jnp.int32
    )
    coriolis = (0.1 + 0.1 * row_index.astype(jnp.float32) / grid_rows)[:, None]
    tracer_field = biology_concentration
    warming_forcing = thermal_anomaly
    currents_now = collect(flow_vectors, "tracer", 1)
    for repeat in range(STEPS):
        currents_next, east_pad, north_pad = ocean_step(currents_now, wet_pad, coriolis)
        fluxes = flux_pieces(east_pad, north_pad)
        tracer_field, heating = tracer_step(
            tracer_field,
            fluxes,
            coupling,
            wet_inner,
            solar_flux_field,
            ecosystem_coefficients,
            level_start,
            vertical_tier_total,
        )
        east_own = lax.dynamic_slice_in_dim(east_pad, level_start, vertical_tier_total, 0)
        north_own = lax.dynamic_slice_in_dim(north_pad, level_start, vertical_tier_total, 0)
        warming_forcing = heat_step(warming_forcing, east_own, north_own, heating, wet_own)
        currents_now = currents_next
    currents_final = lax.dynamic_slice_in_dim(currents_now, level_start, vertical_tier_total, 1)
    return (tracer_field, currents_final, warming_forcing)


def solution(mesh):
    in_specs = (
        P("tracer", None, "gy", "gx"),
        P(None, "tracer", "gy", "gx"),
        P("tracer", "gy", "gx"),
        P(None, "gy", "gx"),
        P("gy", "gx"),
        P("tracer"),
        P("gy", "gx"),
        P("gy", "gx"),
    )
    out_specs = (
        P("tracer", None, "gy", "gx"),
        P(None, "tracer", "gy", "gx"),
        P("tracer", "gy", "gx"),
    )
    return jax.shard_map(
        per_device, mesh=mesh, in_specs=in_specs, out_specs=out_specs, check_vma=False
    )
```

profile of v0, /device:TPU:225, one launch (start us, length us, event | category | flops | bytes accessed | tf_op | source)
XLA Modules:
  0.0 267.2 jit_solution(14098092342450380989)
XLA Ops:
  1.5 3.7 %collective-permute-start = (s32[2,1,128]{2,1,0:T(1,128)S(1)}, s32[2,1,128]{2,1,0:T(1,128)S(1)}, u32[]{:S(2)}, u32[]{:S(2)}) collective-permute-start(s32[2,1,128]{2,1,0:T(1,128)S(1)} %get-tuple-element.67), channel_id=1, source_target_pairs={{0,8},{8,16},{16,24},{24,32},{32,40},{40,48},{48,56},{1,9},{9,17},... | collective-permute-start | bytes 3080 | tf_op jit(solution)/shard_map/ppermute | solution.py:25
  5.1 1.9 collective-permute-start.3
  7.1 1.6 fusion.88
  8.6 3.6 %collective-permute-start.10 = (f32[3,8,2,128]{3,2,1,0:T(2,128)}, f32[3,8,2,128]{3,2,1,0:T(2,128)}, u32[]{:S(2)}, u32[]{:S(2)}) collective-permute-start(f32[3,8,2,128]{3,2,1,0:T(2,128)} %get-tuple-element.35), channel_id=1, source_target_pairs={{0,8},{8,16},{16,24},{24,32},{32,40},{40,48},{48,56},{1,9},{9,17},... | collective-permute-start | bytes 73736 | tf_op jit(solution)/shard_map/ppermute | solution.py:25
  13.2 1.3 collective-permute-start.1
  14.5 4.0 %collective-permute-start.2 = (s32[2,64,1]{2,1,0:T(8,128)S(1)}, s32[2,64,1]{2,1,0:T(8,128)S(1)}, u32[]{:S(2)}, u32[]{:S(2)}) collective-permute-start(s32[2,64,1]{2,1,0:T(8,128)S(1)} %get-tuple-element.66), channel_id=1, source_target_pairs={{64,0},{128,64},{192,128},{65,1},{129,65},{193,129},{66,2},{130,66... | collective-permute-start | bytes 1544 | tf_op jit(solution)/shard_map/ppermute | solution.py:26
  18.5 1.7 broadcast_in_dim.27
  20.2 9.3 %all-to-all-start = ((f32[8,2,1,64,128]{4,3,2,1,0:T(8,128)}), f32[8,2,1,64,128]{4,3,2,1,0:T(8,128)}, u32[]{:S(2)}, u32[]{:S(2)}) async-start(f32[8,2,1,64,128]{4,3,2,1,0:T(8,128)} %broadcast_in_dim.27), calls=%async_computation | async-start | bytes 1048576 | tf_op jit(solution)/shard_map/all_to_all | solution.py:39
  30.4 2.4 collective-permute-start.11
  32.8 2.6 collective-permute-start.9
  35.5 1.3 collective-permute-start.8
  38.9 1.0 slice.523
  40.7 2.2 collective-permute-done.8
  43.5 1.1 copy.54
  44.9 3.4 %collective-permute-start.4 = (f32[2,8,1,128]{3,2,1,0:T(1,128)S(1)}, f32[2,8,1,128]{3,2,1,0:T(1,128)S(1)}, u32[]{:S(2)}, u32[]{:S(2)}) collective-permute-start(f32[2,8,1,128]{3,2,1,0:T(1,128)S(1)} %get-tuple-element.59), channel_id=1, source_target_pairs={{0,8},{8,16},{16,24},{24,32},{32,40},{40,48},{48,56},{1,9},{9,17},... | collective-permute-start | bytes 24584 | tf_op jit(solution)/shard_map/ppermute | solution.py:25
  48.3 1.9 collective-permute-start.7
  50.2 1.3 collective-permute-start.5
  51.6 4.0 %collective-permute-start.6 = (f32[2,8,64,1]{3,2,1,0:T(8,128)S(1)}, f32[2,8,64,1]{3,2,1,0:T(8,128)S(1)}, u32[]{:S(2)}, u32[]{:S(2)}) collective-permute-start(f32[2,8,64,1]{3,2,1,0:T(8,128)S(1)} %get-tuple-element.62), channel_id=1, source_target_pairs={{64,0},{128,64},{192,128},{65,1},{129,65},{193,129},{66,2},{130,66... | collective-permute-start | bytes 12296 | tf_op jit(solution)/shard_map/ppermute | solution.py:26
  55.6 2.2 select_maximum_fusion.3
  58.1 6.5 %collective-permute-done.5 = f32[2,8,64,1]{3,2,1,0:T(8,128)S(1)} collective-permute-done((f32[2,8,64,1]{3,2,1,0:T(8,128)S(1)}, f32[2,8,64,1]{3,2,1,0:T(8,128)S(1)}, u32[]{:S(2)}, u32[]{:S(2)}) %collective-permute-start.5) | collective-permute-done | bytes 4128 | tf_op jit(solution)/shard_map/ppermute | solution.py:25
  64.6 1.8 collective-permute-done.6
  66.9 1.3 fusion.17
  69.2 2.8 %multiply_select_fusion.1 = f32[3,8,64,129]{3,2,1,0:T(8,128)S(1)} fusion(f32[3,8,64,2]{3,2,1,0:T(8,128)S(1)} %copy.41, f32[3,8,64,128]{3,2,1,0:T(8,128)S(1)} %copy-done, f32[3,8,64,2]{3,2,1,0:T(8,128)S(1)} %copy.39, f32[8,64,129]{2,1,0:T(8,128)S(1)} %get-tuple-element.49, f32[8,64,129]{2,1,0:T(8,128)S(1)} %get-tuple-element.48, ...), kind=kLoop, calls=%fused_computation.19 | loop fusion | flops 5548032 | bytes 2462208 | tf_op jit(solution)/shard_map/jit(_where)/select_n | solution.py:79
  72.0 1.7 multiply_select_fusion.3
  75.3 1.6 broadcast_in_dim.31
  76.9 9.2 %all-to-all-start.1 = ((f32[8,8,64,128]{3,2,1,0:T(8,128)}), f32[8,8,64,128]{3,2,1,0:T(8,128)}, u32[]{:S(2)}, u32[]{:S(2)}) async-start(f32[8,8,64,128]{3,2,1,0:T(8,128)} %broadcast_in_dim.31), calls=%async_computation.1 | async-start | bytes 4194304 | tf_op jit(solution)/shard_map/all_to_all | solution.py:39
  86.2 1.9 fusion.26
  88.0 1.3 fusion.47
  89.4 4.6 %collective-permute-start.12 = (f32[2,8,1,128]{3,2,1,0:T(1,128)S(1)}, f32[2,8,1,128]{3,2,1,0:T(1,128)S(1)}, u32[]{:S(2)}, u32[]{:S(2)}) collective-permute-start(f32[2,8,1,128]{3,2,1,0:T(1,128)S(1)} %get-tuple-element.53), channel_id=1, source_target_pairs={{0,8},{8,16},{16,24},{24,32},{32,40},{40,48},{48,56},{1,9},{9,17},... | collective-permute-start | bytes 24584 | tf_op jit(solution)/shard_map/ppermute | solution.py:25
  94.0 1.9 collective-permute-start.15
  96.1 1.4 collective-permute-start.13
  97.6 4.9 %collective-permute-start.14 = (f32[2,8,64,1]{3,2,1,0:T(8,128)S(1)}, f32[2,8,64,1]{3,2,1,0:T(8,128)S(1)}, u32[]{:S(2)}, u32[]{:S(2)}) collective-permute-start(f32[2,8,64,1]{3,2,1,0:T(8,128)S(1)} %get-tuple-element.56), channel_id=1, source_target_pairs={{64,0},{128,64},{192,128},{65,1},{129,65},{193,129},{66,2},{130,66... | collective-permute-start | bytes 12296 | tf_op jit(solution)/shard_map/ppermute | solution.py:26
  103.4 41.7 %collective-permute-done.13 = f32[2,8,64,1]{3,2,1,0:T(8,128)S(1)} collective-permute-done((f32[2,8,64,1]{3,2,1,0:T(8,128)S(1)}, f32[2,8,64,1]{3,2,1,0:T(8,128)S(1)}, u32[]{:S(2)}, u32[]{:S(2)}) %collective-permute-start.13) | collective-permute-done | bytes 4128 | tf_op jit(solution)/shard_map/ppermute | solution.py:25
  147.5 1.0 broadcast_compare_fusion.2
  149.2 1.0 fusion.91
  150.3 1.3 fusion.90
  151.6 1.7 reduce_sum.16
  153.3 2.2 subtract_add_fusion.1
  155.6 1.3 add_subtract_fusion.3
  159.3 3.2 %collective-permute-start.17 = (f32[3,8,64,2]{2,1,3,0:T(8,128)S(1)}, f32[3,8,64,2]{2,1,3,0:T(8,128)}, u32[]{:S(2)}, u32[]{:S(2)}) collective-permute-start(f32[3,8,64,2]{2,1,3,0:T(8,128)S(1)} %copy.46), channel_id=1, source_target_pairs={{64,0},{128,64},{192,128},{65,1},{129,65},{193,129},{66,2},{130,66... | collective-permute-start | bytes 36872 | tf_op jit(solution)/shard_map/ppermute | solution.py:26
  162.4 1.3 collective-permute-start.16
  164.4 3.2 %collective-permute-start.18 = (f32[3,8,2,128]{3,2,1,0:T(2,128)}, f32[3,8,2,128]{3,2,1,0:T(2,128)S(1)}, u32[]{:S(2)}, u32[]{:S(2)}) collective-permute-start(f32[3,8,2,128]{3,2,1,0:T(2,128)} %get-tuple-element.27), channel_id=1, source_target_pairs={{0,8},{8,16},{16,24},{24,32},{32,40},{40,48},{48,56},{1,9},{9,17},... | collective-permute-start | bytes 73736 | tf_op jit(solution)/shard_map/ppermute | solution.py:25
  167.5 1.9 collective-permute-start.19
  169.8 1.1 copy.47
  170.9 3.9 %multiply_select_fusion = f32[3,8,64,129]{3,2,1,0:T(8,128)S(1)} fusion(f32[3,8,64,2]{3,2,1,0:T(8,128)S(1)} %copy.47, f32[3,8,64,128]{3,2,1,0:T(8,128)S(1)} %fusion.12, f32[3,8,64,2]{3,2,1,0:T(8,128)S(1)} %copy.45, f32[8,64,129]{2,1,0:T(8,128)} %get-tuple-element.41, f32[8,64,129]{2,1,0:T(8,128)} %get-tuple-element.40, f32[8,64,129]{2,1,0:T(8,128)} %get-tuple-element.39, ...), kind=kLoop, calls=%fused_computation.18 | loop fusion | flops 5548032 | bytes 2462208 | tf_op jit(solution)/shard_map/jit(_where)/select_n | solution.py:79
  174.8 2.3 select_maximum_fusion.1
  177.2 1.7 multiply_select_fusion.2
  180.6 1.6 broadcast_in_dim.35
  182.2 9.5 %all-to-all-start.2 = ((f32[8,8,64,128]{3,2,1,0:T(8,128)}), f32[8,8,64,128]{3,2,1,0:T(8,128)}, u32[]{:S(2)}, u32[]{:S(2)}) async-start(f32[8,8,64,128]{3,2,1,0:T(8,128)} %broadcast_in_dim.35), calls=%async_computation.2 | async-start | bytes 4194304 | tf_op jit(solution)/shard_map/all_to_all | solution.py:39
  191.7 4.2 %collective-permute-start.22 = (f32[1,1,128]{2,1,0:T(1,128)S(1)}, f32[1,1,128]{2,1,0:T(1,128)S(1)}, u32[]{:S(2)}, u32[]{:S(2)}) collective-permute-start(f32[1,1,128]{2,1,0:T(1,128)S(1)} %get-tuple-element.73), channel_id=1, source_target_pairs={{0,8},{8,16},{16,24},{24,32},{32,40},{40,48},{48,56},{1,9},{9,17},... | collective-permute-start | bytes 1544 | tf_op jit(solution)/shard_map/ppermute | solution.py:25
  195.9 1.9 collective-permute-start.23
  197.9 1.3 collective-permute-start.20
  199.2 4.9 %collective-permute-start.21 = (f32[1,64,1]{2,1,0:T(8,128)S(1)}, f32[1,64,1]{2,1,0:T(8,128)S(1)}, u32[]{:S(2)}, u32[]{:S(2)}) collective-permute-start(f32[1,64,1]{2,1,0:T(8,128)S(1)} %get-tuple-element.76), channel_id=1, source_target_pairs={{64,0},{128,64},{192,128},{65,1},{129,65},{193,129},{66,2},{130,66... | collective-permute-start | bytes 776 | tf_op jit(solution)/shard_map/ppermute | solution.py:26
  204.1 35.4 %collective-permute-done.20 = f32[1,64,1]{2,1,0:T(8,128)S(1)} collective-permute-done((f32[1,64,1]{2,1,0:T(8,128)S(1)}, f32[1,64,1]{2,1,0:T(8,128)S(1)}, u32[]{:S(2)}, u32[]{:S(2)}) %collective-permute-start.20) | collective-permute-done | bytes 288 | tf_op jit(solution)/shard_map/ppermute | solution.py:25
  239.5 1.0 fusion.63
  242.3 1.5 fusion.40
  245.5 1.3 collective-permute-start.24
  246.8 4.0 %collective-permute-start.25 = (f32[1,64,1]{2,1,0:T(8,128)S(1)}, f32[1,64,1]{2,1,0:T(8,128)S(1)}, u32[]{:S(2)}, u32[]{:S(2)}) collective-permute-start(f32[1,64,1]{2,1,0:T(8,128)S(1)} %get-tuple-element.72), channel_id=1, source_target_pairs={{64,0},{128,64},{192,128},{65,1},{129,65},{193,129},{66,2},{130,66... | collective-permute-start | bytes 776 | tf_op jit(solution)/shard_map/ppermute | solution.py:26
  250.8 4.3 %collective-permute-start.26 = (f32[1,1,128]{2,1,0:T(1,128)S(1)}, f32[1,1,128]{2,1,0:T(1,128)S(1)}, u32[]{:S(2)}, u32[]{:S(2)}) collective-permute-start(f32[1,1,128]{2,1,0:T(1,128)S(1)} %get-tuple-element.69), channel_id=1, source_target_pairs={{0,8},{8,16},{16,24},{24,32},{32,40},{40,48},{48,56},{1,9},{9,17},... | collective-permute-start | bytes 1544 | tf_op jit(solution)/shard_map/ppermute | solution.py:25
  255.0 1.9 collective-permute-start.27
  258.0 1.9 collective-permute-done.27
  260.9 1.7 reduce_sum.20
  262.7 1.5 subtract_add_fusion
  264.2 1.3 add_subtract_fusion.1
  (189 shorter events, 26.0 us)
Async XLA Ops:
  0.6 28.8 %copy-start = (f32[3,8,64,128]{3,2,1,0:T(8,128)S(1)}, f32[3,8,64,128]{3,2,1,0:T(8,128)}, u32[]{:S(2)}) copy-start(f32[3,8,64,128]{3,2,1,0:T(8,128)} %param.8) | copy-start | bytes 2359300
  1.5 34.0 %collective-permute-start = (s32[2,1,128]{2,1,0:T(1,128)S(1)}, s32[2,1,128]{2,1,0:T(1,128)S(1)}, u32[]{:S(2)}, u32[]{:S(2)}) collective-permute-start(s32[2,1,128]{2,1,0:T(1,128)S(1)} %get-tuple-element.67), channel_id=1, source_target_pairs={{0,8},{8,16},{16,24},{24,32},{32,40},{40,48},{48,56},{1,9},{9,17},... | collective-permute-start | bytes 3080 | tf_op jit(solution)/shard_map/ppermute | solution.py:25
  5.1 31.6 %collective-permute-start.3 = (s32[2,1,128]{2,1,0:T(1,128)S(1)}, s32[2,1,128]{2,1,0:T(1,128)S(1)}, u32[]{:S(2)}, u32[]{:S(2)}) collective-permute-start(s32[2,1,128]{2,1,0:T(1,128)S(1)} %get-tuple-element.68), channel_id=1, source_target_pairs={{8,0},{16,8},{24,16},{32,24},{40,32},{48,40},{56,48},{9,1},{17,9},... | collective-permute-start | bytes 3080 | tf_op jit(solution)/shard_map/ppermute | solution.py:26
  8.6 42.9 %collective-permute-start.10 = (f32[3,8,2,128]{3,2,1,0:T(2,128)}, f32[3,8,2,128]{3,2,1,0:T(2,128)}, u32[]{:S(2)}, u32[]{:S(2)}) collective-permute-start(f32[3,8,2,128]{3,2,1,0:T(2,128)} %get-tuple-element.35), channel_id=1, source_target_pairs={{0,8},{8,16},{16,24},{24,32},{32,40},{40,48},{48,56},{1,9},{9,17},... | collective-permute-start | bytes 73736 | tf_op jit(solution)/shard_map/ppermute | solution.py:25
  13.2 17.2 %collective-permute-start.1 = (s32[2,64,1]{2,1,0:T(8,128)S(1)}, s32[2,64,1]{2,1,0:T(8,128)S(1)}, u32[]{:S(2)}, u32[]{:S(2)}) collective-permute-start(s32[2,64,1]{2,1,0:T(8,128)S(1)} %get-tuple-element.65), channel_id=1, source_target_pairs={{0,64},{64,128},{128,192},{1,65},{65,129},{129,193},{2,66},{66,130... | collective-permute-start | bytes 1544 | tf_op jit(solution)/shard_map/ppermute | solution.py:25
  14.5 18.3 %collective-permute-start.2 = (s32[2,64,1]{2,1,0:T(8,128)S(1)}, s32[2,64,1]{2,1,0:T(8,128)S(1)}, u32[]{:S(2)}, u32[]{:S(2)}) collective-permute-start(s32[2,64,1]{2,1,0:T(8,128)S(1)} %get-tuple-element.66), channel_id=1, source_target_pairs={{64,0},{128,64},{192,128},{65,1},{129,65},{193,129},{66,2},{130,66... | collective-permute-start | bytes 1544 | tf_op jit(solution)/shard_map/ppermute | solution.py:26
  20.2 23.3 %all-to-all-start = ((f32[8,2,1,64,128]{4,3,2,1,0:T(8,128)}), f32[8,2,1,64,128]{4,3,2,1,0:T(8,128)}, u32[]{:S(2)}, u32[]{:S(2)}) async-start(f32[8,2,1,64,128]{4,3,2,1,0:T(8,128)} %broadcast_in_dim.27), calls=%async_computation | async-start | bytes 1048576 | tf_op jit(solution)/shard_map/all_to_all | solution.py:39
  29.8 7.0 %copy-start.38 = (s32[64,128]{1,0:T(8,128)S(1)}, s32[64,128]{1,0:T(8,128)}, u32[]{:S(2)}) copy-start(s32[64,128]{1,0:T(8,128)} %param.15) | copy-start | bytes 98308
  29.8 7.0 %copy-start.39 = (s32[64,128]{1,0:T(8,128)S(1)}, s32[64,128]{1,0:T(8,128)}, u32[]{:S(2)}) copy-start(s32[64,128]{1,0:T(8,128)} %param.14) | copy-start | bytes 98308
  29.8 7.4 %copy-start.41 = (f32[8,64,128]{2,1,0:T(8,128)S(1)}, f32[8,64,128]{2,1,0:T(8,128)}, u32[]{:S(2)}) copy-start(f32[8,64,128]{2,1,0:T(8,128)} %param.11) | copy-start | bytes 786436
  30.4 25.2 %collective-permute-start.11 = (f32[3,8,2,128]{3,2,1,0:T(2,128)}, f32[3,8,2,128]{3,2,1,0:T(2,128)}, u32[]{:S(2)}, u32[]{:S(2)}) collective-permute-start(f32[3,8,2,128]{3,2,1,0:T(2,128)} %get-tuple-element.36), channel_id=1, source_target_pairs={{8,0},{16,8},{24,16},{32,24},{40,32},{48,40},{56,48},{9,1},{17,9},... | collective-permute-start | bytes 73736 | tf_op jit(solution)/shard_map/ppermute | solution.py:26
  32.8 10.4 %collective-permute-start.9 = (f32[3,8,64,2]{2,1,3,0:T(8,128)S(1)}, f32[3,8,64,2]{2,1,3,0:T(8,128)S(1)}, u32[]{:S(2)}, u32[]{:S(2)}) collective-permute-start(f32[3,8,64,2]{2,1,3,0:T(8,128)S(1)} %copy.51), channel_id=1, source_target_pairs={{64,0},{128,64},{192,128},{65,1},{129,65},{193,129},{66,2},{130,66... | collective-permute-start | bytes 36872 | tf_op jit(solution)/shard_map/ppermute | solution.py:26
  35.5 7.4 %collective-permute-start.8 = (f32[3,8,64,2]{2,1,3,0:T(8,128)S(1)}, f32[3,8,64,2]{2,1,3,0:T(8,128)S(1)}, u32[]{:S(2)}, u32[]{:S(2)}) collective-permute-start(f32[3,8,64,2]{2,1,3,0:T(8,128)S(1)} %copy.50), channel_id=1, source_target_pairs={{0,64},{64,128},{128,192},{1,65},{65,129},{129,193},{2,66},{66,130... | collective-permute-start | bytes 36872 | tf_op jit(solution)/shard_map/ppermute | solution.py:25
  36.9 2.0 copy-start.35
  38.0 2.7 %copy-start.9 = (f32[8,64,128]{2,1,0:T(8,128)}, f32[8,64,128]{2,1,0:T(8,128)S(1)}, u32[]{:S(2)}) copy-start(f32[8,64,128]{2,1,0:T(8,128)S(1)} %get-tuple-element.45) | copy-start | bytes 786436
  44.9 13.0 %collective-permute-start.4 = (f32[2,8,1,128]{3,2,1,0:T(1,128)S(1)}, f32[2,8,1,128]{3,2,1,0:T(1,128)S(1)}, u32[]{:S(2)}, u32[]{:S(2)}) collective-permute-start(f32[2,8,1,128]{3,2,1,0:T(1,128)S(1)} %get-tuple-element.59), channel_id=1, source_target_pairs={{0,8},{8,16},{16,24},{24,32},{32,40},{40,48},{48,56},{1,9},{9,17},... | collective-permute-start | bytes 24584 | tf_op jit(solution)/shard_map/ppermute | solution.py:25
  48.3 9.6 %collective-permute-start.7 = (f32[2,8,1,128]{3,2,1,0:T(1,128)S(1)}, f32[2,8,1,128]{3,2,1,0:T(1,128)S(1)}, u32[]{:S(2)}, u32[]{:S(2)}) collective-permute-start(f32[2,8,1,128]{3,2,1,0:T(1,128)S(1)} %get-tuple-element.60), channel_id=1, source_target_pairs={{8,0},{16,8},{24,16},{32,24},{40,32},{48,40},{56,48},{9,1},{17,9},... | collective-permute-start | bytes 24584 | tf_op jit(solution)/shard_map/ppermute | solution.py:26
  50.2 14.3 %collective-permute-start.5 = (f32[2,8,64,1]{3,2,1,0:T(8,128)S(1)}, f32[2,8,64,1]{3,2,1,0:T(8,128)S(1)}, u32[]{:S(2)}, u32[]{:S(2)}) collective-permute-start(f32[2,8,64,1]{3,2,1,0:T(8,128)S(1)} %get-tuple-element.61), channel_id=1, source_target_pairs={{0,64},{64,128},{128,192},{1,65},{65,129},{129,193},{2,66},{66,130... | collective-permute-start | bytes 12296 | tf_op jit(solution)/shard_map/ppermute | solution.py:25
  51.6 14.8 %collective-permute-start.6 = (f32[2,8,64,1]{3,2,1,0:T(8,128)S(1)}, f32[2,8,64,1]{3,2,1,0:T(8,128)S(1)}, u32[]{:S(2)}, u32[]{:S(2)}) collective-permute-start(f32[2,8,64,1]{3,2,1,0:T(8,128)S(1)} %get-tuple-element.62), channel_id=1, source_target_pairs={{64,0},{128,64},{192,128},{65,1},{129,65},{193,129},{66,2},{130,66... | collective-permute-start | bytes 12296 | tf_op jit(solution)/shard_map/ppermute | solution.py:26
  57.8 9.1 %copy-start.14 = (f32[8,65,130]{2,1,0:T(8,128)S(1)}, f32[8,65,130]{2,1,0:T(8,128)}, u32[]{:S(2)}) copy-start(f32[8,65,130]{2,1,0:T(8,128)} %slice.536) | copy-start | bytes 811204
  57.8 9.1 %copy-start.15 = (f32[8,66,129]{2,1,0:T(8,128)S(1)}, f32[8,66,129]{2,1,0:T(8,128)}, u32[]{:S(2)}) copy-start(f32[8,66,129]{2,1,0:T(8,128)} %slice.523) | copy-start | bytes 817348
  57.8 9.1 %copy-start.36 = (s32[66,130]{1,0:T(8,128)S(1)}, s32[66,130]{1,0:T(8,128)}, u32[]{:S(2)}) copy-start(s32[66,130]{1,0:T(8,128)} %copy-done.35) | copy-start | bytes 102964
  58.0 10.2 %copy-start.44 = (f32[2,8,1,130]{3,2,1,0:T(1,128)}, f32[2,8,1,130]{3,2,1,0:T(1,128)S(1)}, u32[]{:S(2)}) copy-start(f32[2,8,1,130]{3,2,1,0:T(1,128)S(1)} %pad.61) | copy-start | bytes 24964
  58.1 10.1 %copy-start.46 = (f32[2,8,1,130]{3,2,1,0:T(1,128)}, f32[2,8,1,130]{3,2,1,0:T(1,128)S(1)}, u32[]{:S(2)}) copy-start(f32[2,8,1,130]{3,2,1,0:T(1,128)S(1)} %pad.62) | copy-start | bytes 24964
  64.6 3.6 %copy-start.28 = (f32[2,8,64,1]{3,2,1,0:T(8,128)}, f32[2,8,64,1]{3,2,1,0:T(8,128)S(1)}, u32[]{:S(2)}) copy-start(f32[2,8,64,1]{3,2,1,0:T(8,128)S(1)} %collective-permute-done.5) | copy-start | bytes 12292
  66.4 2.3 copy-start.30
  76.9 9.2 %copy-start.29 = (f32[2,8,64,1]{3,2,1,0:T(8,128)S(1)}, f32[2,8,64,1]{3,2,1,0:T(8,128)}, u32[]{:S(2)}) copy-start(f32[2,8,64,1]{3,2,1,0:T(8,128)} %copy-done.28) | copy-start | bytes 12292
  76.9 9.2 %copy-start.45 = (f32[2,8,1,130]{3,2,1,0:T(1,128)S(1)}, f32[2,8,1,130]{3,2,1,0:T(1,128)}, u32[]{:S(2)}) copy-start(f32[2,8,1,130]{3,2,1,0:T(1,128)} %copy-done.44) | copy-start | bytes 24964
  76.9 9.2 %copy-start.47 = (f32[2,8,1,130]{3,2,1,0:T(1,128)S(1)}, f32[2,8,1,130]{3,2,1,0:T(1,128)}, u32[]{:S(2)}) copy-start(f32[2,8,1,130]{3,2,1,0:T(1,128)} %copy-done.46) | copy-start | bytes 24964
  76.9 74.7 %all-to-all-start.1 = ((f32[8,8,64,128]{3,2,1,0:T(8,128)}), f32[8,8,64,128]{3,2,1,0:T(8,128)}, u32[]{:S(2)}, u32[]{:S(2)}) async-start(f32[8,8,64,128]{3,2,1,0:T(8,128)} %broadcast_in_dim.31), calls=%async_computation.1 | async-start | bytes 4194304 | tf_op jit(solution)/shard_map/all_to_all | solution.py:39
  86.1 1.9 copy-start.3
  86.1 3.2 %copy-start.49 = (f32[64]{0:T(128)}, f32[64]{0:T(128)S(1)}, u32[]{:S(2)}) copy-start(f32[64]{0:T(128)S(1)} %multiply_add_fusion.2) | copy-start | bytes 772
  89.4 13.2 %copy-start.48 = (f32[3]{0:T(128)S(1)}, f32[3]{0:T(128)}, u32[]{:S(2)}) copy-start(f32[3]{0:T(128)} %param.13) | copy-start | bytes 40
  89.4 13.8 %collective-permute-start.12 = (f32[2,8,1,128]{3,2,1,0:T(1,128)S(1)}, f32[2,8,1,128]{3,2,1,0:T(1,128)S(1)}, u32[]{:S(2)}, u32[]{:S(2)}) collective-permute-start(f32[2,8,1,128]{3,2,1,0:T(1,128)S(1)} %get-tuple-element.53), channel_id=1, source_target_pairs={{0,8},{8,16},{16,24},{24,32},{32,40},{40,48},{48,56},{1,9},{9,17},... | collective-permute-start | bytes 24584 | tf_op jit(solution)/shard_map/ppermute | solution.py:25
  94.0 9.3 %collective-permute-start.15 = (f32[2,8,1,128]{3,2,1,0:T(1,128)S(1)}, f32[2,8,1,128]{3,2,1,0:T(1,128)S(1)}, u32[]{:S(2)}, u32[]{:S(2)}) collective-permute-start(f32[2,8,1,128]{3,2,1,0:T(1,128)S(1)} %get-tuple-element.54), channel_id=1, source_target_pairs={{8,0},{16,8},{24,16},{32,24},{40,32},{48,40},{56,48},{9,1},{17,9},... | collective-permute-start | bytes 24584 | tf_op jit(solution)/shard_map/ppermute | solution.py:26
  96.1 51.1 %copy-start.4 = (f32[8,66,130]{2,1,0:T(8,128)S(1)}, f32[8,66,130]{2,1,0:T(8,128)}, u32[]{:S(2)}) copy-start(f32[8,66,130]{2,1,0:T(8,128)} %get-tuple-element.16) | copy-start | bytes 823684
  96.1 48.9 %collective-permute-start.13 = (f32[2,8,64,1]{3,2,1,0:T(8,128)S(1)}, f32[2,8,64,1]{3,2,1,0:T(8,128)S(1)}, u32[]{:S(2)}, u32[]{:S(2)}) collective-permute-start(f32[2,8,64,1]{3,2,1,0:T(8,128)S(1)} %get-tuple-element.55), channel_id=1, source_target_pairs={{0,64},{64,128},{128,192},{1,65},{65,129},{129,193},{2,66},{66,130... | collective-permute-start | bytes 12296 | tf_op jit(solution)/shard_map/ppermute | solution.py:25
  97.6 47.5 %collective-permute-start.14 = (f32[2,8,64,1]{3,2,1,0:T(8,128)S(1)}, f32[2,8,64,1]{3,2,1,0:T(8,128)S(1)}, u32[]{:S(2)}, u32[]{:S(2)}) collective-permute-start(f32[2,8,64,1]{3,2,1,0:T(8,128)S(1)} %get-tuple-element.56), channel_id=1, source_target_pairs={{64,0},{128,64},{192,128},{65,1},{129,65},{193,129},{66,2},{130,66... | collective-permute-start | bytes 12296 | tf_op jit(solution)/shard_map/ppermute | solution.py:26
  103.4 48.2 %copy-start.42 = (f32[2,8,1,130]{3,2,1,0:T(1,128)}, f32[2,8,1,130]{3,2,1,0:T(1,128)S(1)}, u32[]{:S(2)}) copy-start(f32[2,8,1,130]{3,2,1,0:T(1,128)S(1)} %pad.66) | copy-start | bytes 24964
  147.5 2.8 %copy-start.6 = (f32[8,66,130]{2,1,0:T(8,128)}, f32[8,66,130]{2,1,0:T(8,128)S(1)}, u32[]{:S(2)}) copy-start(f32[8,66,130]{2,1,0:T(8,128)S(1)} %get-tuple-element.17) | copy-start | bytes 823684
  153.3 3.6 %copy-start.7 = (f32[8,64,128]{2,1,0:T(8,128)}, f32[8,64,128]{2,1,0:T(8,128)S(1)}, u32[]{:S(2)}) copy-start(f32[8,64,128]{2,1,0:T(8,128)S(1)} %reduce_sum.16) | copy-start | bytes 786436
  159.3 10.5 %collective-permute-start.17 = (f32[3,8,64,2]{2,1,3,0:T(8,128)S(1)}, f32[3,8,64,2]{2,1,3,0:T(8,128)}, u32[]{:S(2)}, u32[]{:S(2)}) collective-permute-start(f32[3,8,64,2]{2,1,3,0:T(8,128)S(1)} %copy.46), channel_id=1, source_target_pairs={{64,0},{128,64},{192,128},{65,1},{129,65},{193,129},{66,2},{130,66... | collective-permute-start | bytes 36872 | tf_op jit(solution)/shard_map/ppermute | solution.py:26
  162.4 7.0 %collective-permute-start.16 = (f32[3,8,64,2]{2,1,3,0:T(8,128)}, f32[3,8,64,2]{2,1,3,0:T(8,128)S(1)}, u32[]{:S(2)}, u32[]{:S(2)}) collective-permute-start(f32[3,8,64,2]{2,1,3,0:T(8,128)} %copy.44), channel_id=1, source_target_pairs={{0,64},{64,128},{128,192},{1,65},{65,129},{129,193},{2,66},{66,130... | collective-permute-start | bytes 36872 | tf_op jit(solution)/shard_map/ppermute | solution.py:25
  164.4 10.5 %collective-permute-start.18 = (f32[3,8,2,128]{3,2,1,0:T(2,128)}, f32[3,8,2,128]{3,2,1,0:T(2,128)S(1)}, u32[]{:S(2)}, u32[]{:S(2)}) collective-permute-start(f32[3,8,2,128]{3,2,1,0:T(2,128)} %get-tuple-element.27), channel_id=1, source_target_pairs={{0,8},{8,16},{16,24},{24,32},{32,40},{40,48},{48,56},{1,9},{9,17},... | collective-permute-start | bytes 73736 | tf_op jit(solution)/shard_map/ppermute | solution.py:25
  167.5 7.3 %collective-permute-start.19 = (f32[3,8,2,128]{3,2,1,0:T(2,128)}, f32[3,8,2,128]{3,2,1,0:T(2,128)}, u32[]{:S(2)}, u32[]{:S(2)}) collective-permute-start(f32[3,8,2,128]{3,2,1,0:T(2,128)} %get-tuple-element.28), channel_id=1, source_target_pairs={{8,0},{16,8},{24,16},{32,24},{40,32},{48,40},{56,48},{9,1},{17,9},... | collective-permute-start | bytes 73736 | tf_op jit(solution)/shard_map/ppermute | solution.py:26
  174.8 2.3 copy-start.31
  174.8 2.3 copy-start.32
  174.8 2.3 copy-start.33
  174.8 2.3 copy-start.40
  182.2 9.5 %copy-start.34 = (f32[1,64,128]{2,1,0:T(8,128)S(1)}, f32[1,64,128]{2,1,0:T(8,128)}, u32[]{:S(2)}) copy-start(f32[1,64,128]{2,1,0:T(8,128)} %param.10) | copy-start | bytes 98308
  182.2 59.3 %copy-start.25 = (f32[2,8,64,1]{3,2,1,0:T(8,128)S(1)}, f32[2,8,64,1]{3,2,1,0:T(8,128)}, u32[]{:S(2)}) copy-start(f32[2,8,64,1]{3,2,1,0:T(8,128)} %copy-done.24) | copy-start | bytes 12292
  182.2 59.3 %copy-start.27 = (f32[2,8,64,1]{3,2,1,0:T(8,128)S(1)}, f32[2,8,64,1]{3,2,1,0:T(8,128)}, u32[]{:S(2)}) copy-start(f32[2,8,64,1]{3,2,1,0:T(8,128)} %copy-done.26) | copy-start | bytes 12292
  182.2 59.3 %copy-start.43 = (f32[2,8,1,130]{3,2,1,0:T(1,128)S(1)}, f32[2,8,1,130]{3,2,1,0:T(1,128)}, u32[]{:S(2)}) copy-start(f32[2,8,1,130]{3,2,1,0:T(1,128)} %copy-done.42) | copy-start | bytes 24964
  182.2 78.7 %all-to-all-start.2 = ((f32[8,8,64,128]{3,2,1,0:T(8,128)}), f32[8,8,64,128]{3,2,1,0:T(8,128)}, u32[]{:S(2)}, u32[]{:S(2)}) async-start(f32[8,8,64,128]{3,2,1,0:T(8,128)} %broadcast_in_dim.35), calls=%async_computation.2 | async-start | bytes 4194304 | tf_op jit(solution)/shard_map/all_to_all | solution.py:39
  191.7 50.6 %copy-start.50 = (f32[64]{0:T(128)S(1)}, f32[64]{0:T(128)}, u32[]{:S(2)}) copy-start(f32[64]{0:T(128)} %copy-done.49) | copy-start | bytes 772
  191.7 47.8 %collective-permute-start.22 = (f32[1,1,128]{2,1,0:T(1,128)S(1)}, f32[1,1,128]{2,1,0:T(1,128)S(1)}, u32[]{:S(2)}, u32[]{:S(2)}) collective-permute-start(f32[1,1,128]{2,1,0:T(1,128)S(1)} %get-tuple-element.73), channel_id=1, source_target_pairs={{0,8},{8,16},{16,24},{24,32},{32,40},{40,48},{48,56},{1,9},{9,17},... | collective-permute-start | bytes 1544 | tf_op jit(solution)/shard_map/ppermute | solution.py:25
  195.9 43.6 %collective-permute-start.23 = (f32[1,1,128]{2,1,0:T(1,128)S(1)}, f32[1,1,128]{2,1,0:T(1,128)S(1)}, u32[]{:S(2)}, u32[]{:S(2)}) collective-permute-start(f32[1,1,128]{2,1,0:T(1,128)S(1)} %get-tuple-element.74), channel_id=1, source_target_pairs={{8,0},{16,8},{24,16},{32,24},{40,32},{48,40},{56,48},{9,1},{17,9},... | collective-permute-start | bytes 1544 | tf_op jit(solution)/shard_map/ppermute | solution.py:26
  197.9 41.6 %collective-permute-start.20 = (f32[1,64,1]{2,1,0:T(8,128)S(1)}, f32[1,64,1]{2,1,0:T(8,128)S(1)}, u32[]{:S(2)}, u32[]{:S(2)}) collective-permute-start(f32[1,64,1]{2,1,0:T(8,128)S(1)} %get-tuple-element.75), channel_id=1, source_target_pairs={{0,64},{64,128},{128,192},{1,65},{65,129},{129,193},{2,66},{66,130... | collective-permute-start | bytes 776 | tf_op jit(solution)/shard_map/ppermute | solution.py:25
  199.2 40.3 %collective-permute-start.21 = (f32[1,64,1]{2,1,0:T(8,128)S(1)}, f32[1,64,1]{2,1,0:T(8,128)S(1)}, u32[]{:S(2)}, u32[]{:S(2)}) collective-permute-start(f32[1,64,1]{2,1,0:T(8,128)S(1)} %get-tuple-element.76), channel_id=1, source_target_pairs={{64,0},{128,64},{192,128},{65,1},{129,65},{193,129},{66,2},{130,66... | collective-permute-start | bytes 776 | tf_op jit(solution)/shard_map/ppermute | solution.py:26
  242.3 2.2 copy-start.8
  245.5 11.5 %collective-permute-start.24 = (f32[1,64,1]{2,1,0:T(8,128)S(1)}, f32[1,64,1]{2,1,0:T(8,128)S(1)}, u32[]{:S(2)}, u32[]{:S(2)}) collective-permute-start(f32[1,64,1]{2,1,0:T(8,128)S(1)} %get-tuple-element.71), channel_id=1, source_target_pairs={{0,64},{64,128},{128,192},{1,65},{65,129},{129,193},{2,66},{66,130... | collective-permute-start | bytes 776 | tf_op jit(solution)/shard_map/ppermute | solution.py:25
  246.8 10.2 %collective-permute-start.25 = (f32[1,64,1]{2,1,0:T(8,128)S(1)}, f32[1,64,1]{2,1,0:T(8,128)S(1)}, u32[]{:S(2)}, u32[]{:S(2)}) collective-permute-start(f32[1,64,1]{2,1,0:T(8,128)S(1)} %get-tuple-element.72), channel_id=1, source_target_pairs={{64,0},{128,64},{192,128},{65,1},{129,65},{193,129},{66,2},{130,66... | collective-permute-start | bytes 776 | tf_op jit(solution)/shard_map/ppermute | solution.py:26
  250.8 7.2 %collective-permute-start.26 = (f32[1,1,128]{2,1,0:T(1,128)S(1)}, f32[1,1,128]{2,1,0:T(1,128)S(1)}, u32[]{:S(2)}, u32[]{:S(2)}) collective-permute-start(f32[1,1,128]{2,1,0:T(1,128)S(1)} %get-tuple-element.69), channel_id=1, source_target_pairs={{0,8},{8,16},{16,24},{24,32},{32,40},{40,48},{48,56},{1,9},{9,17},... | collective-permute-start | bytes 1544 | tf_op jit(solution)/shard_map/ppermute | solution.py:25
  255.0 4.9 %collective-permute-start.27 = (f32[1,1,128]{2,1,0:T(1,128)S(1)}, f32[1,1,128]{2,1,0:T(1,128)S(1)}, u32[]{:S(2)}, u32[]{:S(2)}) collective-permute-start(f32[1,1,128]{2,1,0:T(1,128)S(1)} %get-tuple-element.70), channel_id=1, source_target_pairs={{8,0},{16,8},{24,16},{32,24},{40,32},{48,40},{56,48},{9,1},{17,9},... | collective-permute-start | bytes 1544 | tf_op jit(solution)/shard_map/ppermute | solution.py:26
  (18 other events, 22.4 us)
where the time goes:
time: 269 us; the launch traced here: 267 us
  starting transfers between devices  106 us (39%)
  waiting for transfers between devices  89.5 us (33%)
  other arithmetic  48.3 us (18%)
  local copies, waits for them, and re-layouts  21.9 us (8%)
    ppermute x14, waiting for transfers between devices, padded_2(): lax.ppermute(last, axis, up)  85.7 us
    ppermute x14, starting transfers between devices, padded_2(): lax.ppermute(leading, axis, [(b, a) for a, b in up])  41.6 us
    ppermute x14, starting transfers between devices, padded_2(): lax.ppermute(last, axis, up)  36.1 us
    all_to_all x3, starting transfers between devices, from_everyone(): lax.all_to_all(jnp.broadcast_to(value[None], (devices, *value.shape)), ax...  28 us
    select_n x4, other arithmetic, limited(): return jnp.where(velocity >= 0.0, forward, backward)  9.99 us
    concatenate x5, other arithmetic, padded_2(): jnp.concatenate([jnp.pad(low, around), value, jnp.pad(high, around)], axi...  5.66 us
  transfers between devices with their start and end apart: 31, of which 6 were waited for; matrix products, arithmetic and copies ran while one was open for 14% of the time, Pallas kernels for 0%

commit v1 on v0

v1 whole, which is shorter than its diff:
```python
import jax
import jax.numpy as jnp
from jax import lax
from jax.experimental import pallas as pl
from jax.experimental.pallas import tpu as pltpu
from jax.sharding import PartitionSpec as P

NL = 8
R = 64
W = 128
NT = 3
NCH = NT * NL
HY = 16
f32 = jnp.float32
VM = pl.BlockSpec(memory_space=pltpu.VMEM)
SM = pl.BlockSpec(memory_space=pltpu.SMEM)


def call(body, name, outs, n_scalar, scratch=()):
    def run(*args):
        return pl.pallas_call(
            body,
            name=name,
            out_shape=[jax.ShapeDtypeStruct(s, f32) for s in outs],
            in_specs=[SM] * n_scalar + [VM] * (len(args) - n_scalar),
            out_specs=[VM] * len(outs),
            scratch_shapes=[pltpu.VMEM(s, f32) for s in scratch],
            compiler_params=pltpu.CompilerParams(vmem_limit_bytes=40 * 2**20),
        )(*args)

    return run


def lanes(shape):
    return lax.broadcasted_iota(jnp.int32, shape, 1)


def rx(v, k):
    return pltpu.roll(v, k % v.shape[1], 1)


def ry(v, k):
    return pltpu.roll(v, k % v.shape[0], 0)


def aside(v, shift):
    return pltpu.roll(v, shift, 1)


def minmod(a, b):
    return jnp.maximum(jnp.minimum(a, b), 0.0) + jnp.minimum(jnp.maximum(a, b), 0.0)


def coefs(vel):
    up = jnp.maximum(vel, 0.0)
    um = jnp.minimum(vel, 0.0)
    return up, um, 0.5 * up * (1.0 - up), 0.5 * um * (1.0 + um)


def divergence(c, co, roll):
    up, um, a, b = co
    ahead = roll(c, -1)
    d = ahead - c
    s = minmod(d, roll(d, 1))
    flux = up * c + a * s + um * ahead - b * roll(s, -1)
    return flux - roll(flux, 1)


def upwind(c, vel, roll):
    flux = jnp.maximum(vel, 0.0) * c + jnp.minimum(vel, 0.0) * roll(c, -1)
    return flux - roll(flux, 1)


def put_x(acc, value, lane, width):
    at = lanes(acc.shape)
    half = width // 2
    return jnp.where((at >= lane) & (at < lane + width), pltpu.roll(value, lane + half, 1), acc)


def pack_tracers(c_ref, px_ref, pyu_ref, pyd_ref):
    def level(l, carry):
        for t in range(NT):
            ch = t * NL + l
            c = c_ref[t, l]
            px_ref[...] = put_x(px_ref[...], c, 4 * ch, 4)
            pyu_ref[pl.ds(2 * ch, 2), :] = c_ref[t, l, R - 2 : R, :]
            pyd_ref[pl.ds(2 * ch, 2), :] = c_ref[t, l, 0:2, :]
        return carry

    lax.fori_loop(0, NL, level, 0)


def pack_rows(value, row, pyu_ref, pyd_ref):
    pyu_ref[row : row + 1, :] = value[R - 1 : R, :]
    pyd_ref[row : row + 1, :] = value[0:1, :]


def first_pack(c_ref, flow_ref, temp_ref, sea_ref, floor_ref, px_ref, pyu_ref, pyd_ref):
    px_ref[...] = jnp.zeros_like(px_ref)
    pyu_ref[...] = jnp.zeros_like(pyu_ref)
    pyd_ref[...] = jnp.zeros_like(pyd_ref)
    pack_tracers(c_ref, px_ref, pyu_ref, pyd_ref)
    singles = (
        flow_ref[0, 0],
        flow_ref[1, 0],
        temp_ref[0],
        sea_ref[...].astype(f32),
        floor_ref[...].astype(f32),
    )
    acc = px_ref[...]
    for j, value in enumerate(singles):
        acc = put_x(acc, value, 96 + 2 * j, 2)
        pack_rows(value, 48 + j, pyu_ref, pyd_ref)
    px_ref[...] = acc


def join_x(ids_ref, even, odd, left_end=96):
    at = lanes(even.shape)
    half = jnp.where(at < 96, (at >> 1) & 1, jnp.where(at < left_end, 0, at & 1))
    return jnp.where(half == (ids_ref[1] & 1), odd, even)


def edges_y(ids_ref, lo_ref, hi_ref, los_ref, his_ref):
    gy = ids_ref[2]
    los_ref[...] = jnp.where(gy == 0, 0.0, lo_ref[...])
    his_ref[...] = jnp.where(gy == ids_ref[3] - 1, 0.0, hi_ref[...])


def extend_flow(ids_ref, flow_ref, even_ref, odd_ref, lo_ref, hi_ref, e_ref):
    joined = join_x(ids_ref, even_ref[...], odd_ref[...])
    padded = jnp.concatenate([joined, jnp.zeros_like(joined)], 0)
    turned = padded.T
    gy = ids_ref[2]
    e_ref[0:R, :] = flow_ref[0, 0]
    e_ref[R : 2 * R, :] = flow_ref[1, 0]
    e_ref[2 * R : 2 * R + 4, :] = turned[96:100, :]
    lo = jnp.where(gy == 0, 0.0, lo_ref[48:50, :])
    hi = jnp.where(gy == ids_ref[3] - 1, 0.0, hi_ref[48:50, :])
    e_ref[2 * R + 4 : 2 * R + 6, :] = lo
    e_ref[2 * R + 6 : 2 * R + 8, :] = hi


def wet_setup(xh, los_ref, his_ref, sea_ref, floor_ref, wx_ref, wy_ref):
    for k, ref in enumerate((sea_ref, floor_ref)):
        main = ref[...].astype(f32)
        wx_ref[k, :, :W] = main
        wx_ref[k, :, W:] = aside(xh, (127 - (96 + 2 * (3 + k))) % W)
        wy_ref[k, :R, :] = main
        wy_ref[k, R : R + HY, :] = jnp.zeros((HY, W), f32)
        wy_ref[k, R : R + 1, :] = his_ref[51 + k : 52 + k, :]
        wy_ref[k, R + HY - 1 : R + HY, :] = los_ref[51 + k : 52 + k, :]


def wet_of(ref, l):
    return jnp.where(l.astype(f32) < ref[1], ref[0], 0.0)


def advect_level(l, c_ref, xh_ref, los_ref, his_ref, east, north, wet, cy_ref, adv_ref):
    east_co = coefs(east)
    north_co = coefs(north)
    for t in range(NT):
        ch = t * NL + l
        c = c_ref[t, l]
        cx = jnp.concatenate([c, aside(xh_ref[...], lax.rem(126 + W - 4 * ch, W))], 1)
        div = divergence(cx, east_co, rx)[:, :W]
        cy_ref[t, 0:R, :] = c
        cy_ref[t, R : R + 2, :] = his_ref[pl.ds(2 * ch, 2), :]
        cy_ref[t, R + HY - 2 : R + HY, :] = los_ref[pl.ds(2 * ch, 2), :]
        div = div + divergence(cy_ref[t], north_co, ry)[:R]
        adv_ref[t, l] = wet * (c - div)


def mix(adv_ref, dif_ref, wx_ref, mix_ref):
    above = None
    wet = wet_of(wx_ref, jnp.int32(0))[:, :W]
    for l in range(NL):
        if l + 1 < NL:
            below_wet = wet_of(wx_ref, jnp.int32(l + 1))[:, :W]
            below = dif_ref[l] * wet * below_wet
        for t in range(NT):
            c = adv_ref[t, l]
            out = c
            if l + 1 < NL:
                out = out + below * (adv_ref[t, l + 1] - c)
            if l:
                out = out - above * (c - adv_ref[t, l - 1])
            mix_ref[t, l] = out
        above, wet = below, below_wet


def split_absorb(ids_ref, mix_ref, parts):
    y = ids_ref[0] & 3
    for k, ref in enumerate(parts):
        j = (y + k) & 3
        ref[...] = mix_ref[1, pl.ds(2 * j, 2)]


def next_currents(u, v, ux, uy, vx, vy, east_open, north_open, coriolis):
    lap_u = (rx(ux, -1) + rx(ux, 1))[:, :W] + (ry(uy, -1) + ry(uy, 1))[:R] - 4.0 * u
    lap_v = (rx(vx, -1) + rx(vx, 1))[:, :W] + (ry(vy, -1) + ry(vy, 1))[:R] - 4.0 * v
    return (
        east_open * (u + coriolis * v + 0.2 * lap_u),
        north_open * (v - coriolis * u + 0.2 * lap_v),
    )


def coriolis_of(ids_ref):
    row = ids_ref[2] * R + lax.broadcasted_iota(jnp.int32, (R, W), 0)
    rows = (ids_ref[3] * R).astype(f32)
    return 0.1 + 0.1 * row.astype(f32) / rows


def with_y(ref, main, hi, lo):
    ref[0:R, :] = main
    ref[R : R + 1, :] = hi
    ref[R + HY - 1 : R + HY, :] = lo
    return ref[...]


def open_x(wx):
    return wx * rx(wx, -1)


def open_y(wy):
    return wy * ry(wy, -1)


def step_one(
    ids_ref, c_ref, g0, g1, g2, g3, even_ref, odd_ref, lo_ref, hi_ref, temp_ref, dif_ref, sea_ref,
    floor_ref, mix_ref, a0, a1, a2, a3, cur_ref, tadv_ref,
    g_ref, xh_ref, los_ref, his_ref, wx_ref, wy_ref, cy_ref, adv_ref, gx_ref, uy_ref,
):
    y = ids_ref[0] & 3
    z = ids_ref[0] >> 2
    for k, ref in enumerate((g0, g1, g2, g3)):
        for zz in range(2):
            g_ref[((z + zz) & 1) * 4 + ((y + 4 - k) & 3)] = ref[zz]
    xh = join_x(ids_ref, even_ref[...], odd_ref[...])
    xh_ref[...] = xh
    edges_y(ids_ref, lo_ref, hi_ref, los_ref, his_ref)
    wet_setup(xh, los_ref, his_ref, sea_ref, floor_ref, wx_ref, wy_ref)
    cols = jnp.concatenate([g_ref[l, 2 * R : 2 * R + 8, :] for l in range(NL)], 0)
    gx_ref[...] = jnp.concatenate([cols, jnp.zeros_like(cols)], 0).T[:R, :]
    coriolis = coriolis_of(ids_ref)

    def faces(l):
        u = g_ref[l, 0:R, :]
        v = g_ref[l, R : 2 * R, :]
        ux = jnp.concatenate([u, aside(gx_ref[...], lax.rem(W + 127 - 8 * l, W))], 1)
        edge = 2 * R + 4
        vy = with_y(
            uy_ref.at[1], v, g_ref[l, edge + 3 : edge + 4, :], g_ref[l, edge + 1 : edge + 2, :]
        )
        wx = wet_of(wx_ref, l)
        east_open = open_x(wx)
        north_open = open_y(wet_of(wy_ref, l))
        return u, v, ux, vy, wx, east_open, north_open

    def level(l, carry):
        u, v, ux, vy, wx, east_open, north_open = faces(l)
        vx = jnp.concatenate([v, aside(gx_ref[...], lax.rem(W + 125 - 8 * l, W))], 1)
        edge = 2 * R + 4
        uy = with_y(
            uy_ref.at[0], u, g_ref[l, edge + 2 : edge + 3, :], g_ref[l, edge : edge + 1, :]
        )
        new_u, new_v = next_currents(
            u, v, ux, uy, vx, vy, east_open[:, :W], north_open[:R], coriolis
        )
        cur_ref[0, l] = new_u
        cur_ref[1, l] = new_v
        advect_level(
            l, c_ref, xh_ref, los_ref, his_ref, east_open * ux, north_open * vy, wx[:, :W],
            cy_ref, adv_ref,
        )
        return carry

    lax.fori_loop(0, NL, level, 0)
    mix(adv_ref, dif_ref, wx_ref, mix_ref)
    split_absorb(ids_ref, mix_ref, (a0, a1, a2, a3))
    u, v, ux, vy, wx, east_open, north_open = faces(ids_ref[0])
    temp = temp_ref[0]
    tx = jnp.concatenate([temp, aside(xh_ref[...], 127 - 100)], 1)
    ty = with_y(uy_ref.at[0], temp, his_ref[50:51, :], los_ref[50:51, :])
    tadv_ref[...] = (
        temp - upwind(tx, east_open * ux, rx)[:, :W] - upwind(ty, north_open * vy, ry)[:R]
    )


def step_two(
    ids_ref, c_ref, cur_ref, even_ref, odd_ref, lo_ref, hi_ref, even1_ref, odd1_ref, lo1_ref,
    hi1_ref, temp_ref, dif_ref, sea_ref, floor_ref, mix_ref, a0, a1, a2, a3, out_ref, tadv_ref,
    xh_ref, los_ref, his_ref, wx_ref, wy_ref, cy_ref, adv_ref, uy_ref,
):
    xh1 = join_x(ids_ref, even1_ref[...], odd1_ref[...])
    edges_y(ids_ref, lo1_ref, hi1_ref, los_ref, his_ref)
    wet_setup(xh1, los_ref, his_ref, sea_ref, floor_ref, wx_ref, wy_ref)
    xh_ref[...] = join_x(ids_ref, even_ref[...], odd_ref[...], 104)
    edges_y(ids_ref, lo_ref, hi_ref, los_ref, his_ref)

    def faces(l):
        u = cur_ref[0, l]
        v = cur_ref[1, l]
        ux = jnp.concatenate([u, aside(xh_ref[...], 31 - l)], 1)
        vlow = los_ref[pl.ds(48 + l, 1), :]
        vy = with_y(uy_ref.at[1], v, vlow, vlow)
        wx = wet_of(wx_ref, l)
        return u, v, ux, vy, wx, open_x(wx), open_y(wet_of(wy_ref, l))

    def level(l, carry):
        u, v, ux, vy, wx, east_open, north_open = faces(l)
        advect_level(
            l, c_ref, xh_ref, los_ref, his_ref, east_open * ux, north_open * vy, wx[:, :W],
            cy_ref, adv_ref,
        )
        return carry

    lax.fori_loop(0, NL, level, 0)
    mix(adv_ref, dif_ref, wx_ref, mix_ref)
    split_absorb(ids_ref, mix_ref, (a0, a1, a2, a3))
    u, v, ux, vy, wx, east_open, north_open = faces(ids_ref[0])
    temp = temp_ref[...]
    tx = jnp.concatenate([temp, aside(xh_ref[...], 127 - 108)], 1)
    ty = with_y(uy_ref.at[0], temp, his_ref[58:59, :], los_ref[58:59, :])
    tadv_ref[...] = (
        temp - upwind(tx, east_open * ux, rx)[:, :W] - upwind(ty, north_open * vy, ry)[:R]
    )
    ux = jnp.concatenate([u, aside(xh_ref[...], 127 - 104)], 1)
    vx = jnp.concatenate([v, aside(xh_ref[...], 127 - 106)], 1)
    uy = with_y(uy_ref.at[0], u, his_ref[56:57, :], los_ref[56:57, :])
    vy = with_y(uy_ref.at[1], v, his_ref[57:58, :], los_ref[57:58, :])
    new_u, new_v = next_currents(
        u, v, ux, uy, vx, vy, east_open[:, :W], north_open[:R], coriolis_of(ids_ref)
    )
    out_ref[0] = new_u
    out_ref[1] = new_v


def biology(ids_ref, rate_ref, mix_ref, parts, solar_ref, sea_ref, floor_ref, c_ref, sum_ref, heat_ref):
    y = ids_ref[0] & 3
    for k, ref in enumerate(parts):
        sum_ref[pl.ds(2 * ((y + 4 - k) & 3), 2)] = ref[...]
    solar = solar_ref[...]
    sea = sea_ref[...].astype(f32)
    mu, mortal, recycle = rate_ref[0], rate_ref[1], rate_ref[2]

    def level(l, tau):
        a = 0.04 + 0.03 * sum_ref[l]
        light = solar * jnp.exp(-tau - 0.5 * a)
        heat_ref[l] = 0.5 * solar * (jnp.exp(-tau) - jnp.exp(-tau - a))
        wet = jnp.where(l < floor_ref[...], sea, 0.0)
        n, p, d = mix_ref[0, l], mix_ref[1, l], mix_ref[2, l]
        uptake = mu * (light / (light + 0.3)) * p * n / (jnp.abs(n) + 0.5)
        dead = mortal * p
        back = recycle * d
        c_ref[0, l] = wet * (n - uptake + back)
        c_ref[1, l] = wet * (p + uptake - dead)
        c_ref[2, l] = wet * (d + dead - back)
        return tau + a

    lax.fori_loop(0, NL, level, jnp.zeros((R, W), f32))
    own = ids_ref[0]
    wet = jnp.where(own < floor_ref[...], sea, 0.0)
    return heat_ref[own], wet


def biology_pack(
    ids_ref, rate_ref, mix_ref, t0, t1, t2, t3, solar_ref, sea_ref, floor_ref, tadv_ref, cur_ref,
    c_ref, temp_ref, px_ref, pyu_ref, pyd_ref, sum_ref, heat_ref,
):
    heat, wet = biology(
        ids_ref, rate_ref, mix_ref, (t0, t1, t2, t3), solar_ref, sea_ref, floor_ref, c_ref,
        sum_ref, heat_ref,
    )
    temp = wet * (tadv_ref[...] + heat)
    temp_ref[...] = temp
    px_ref[...] = jnp.zeros_like(px_ref)
    pyu_ref[...] = jnp.zeros_like(pyu_ref)
    pyd_ref[...] = jnp.zeros_like(pyd_ref)
    pack_tracers(c_ref, px_ref, pyu_ref, pyd_ref)
    acc = px_ref[...]
    at = lanes(acc.shape)
    for l in range(NL):
        acc = jnp.where(at == 96 + l, pltpu.roll(cur_ref[0, l], 97 + l, 1), acc)
        pyu_ref[48 + l : 49 + l, :] = cur_ref[1, l, R - 1 : R, :]
    own = ids_ref[0]
    for j, value in enumerate((cur_ref[0, own], cur_ref[1, own], temp)):
        acc = put_x(acc, value, 104 + 2 * j, 2)
        pack_rows(value, 56 + j, pyu_ref, pyd_ref)
    px_ref[...] = acc


def biology_last(
    ids_ref, rate_ref, mix_ref, t0, t1, t2, t3, solar_ref, sea_ref, floor_ref, tadv_ref,
    c_ref, temp_ref, sum_ref, heat_ref,
):
    heat, wet = biology(
        ids_ref, rate_ref, mix_ref, (t0, t1, t2, t3), solar_ref, sea_ref, floor_ref, c_ref,
        sum_ref, heat_ref,
    )
    temp_ref[0] = wet * (tadv_ref[...] + heat)


def swap_pairs(value, axis):
    n = lax.axis_size(axis)
    even = [(i, j) for a in range(0, n - 1, 2) for i, j in ((a, a + 1), (a + 1, a))]
    odd = [(i, j) for a in range(1, n - 1, 2) for i, j in ((a, a + 1), (a + 1, a))]
    return lax.ppermute(value, axis, even), lax.ppermute(value, axis, odd)


def ring_y(up, down):
    n = lax.axis_size("gy")
    ahead = [(i, (i + 1) % n) for i in range(n)]
    back = [(b, a) for a, b in ahead]
    return lax.ppermute(up, "gy", ahead), lax.ppermute(down, "gy", back)


def by_y(k):
    return [(z * 4 + y, z * 4 + (y + k) % 4) for z in range(2) for y in range(4)]


def over_z(value):
    return lax.ppermute(value, "tracer", [(i, i ^ 4) for i in range(8)])


def spread_y(value):
    return [value] + [lax.ppermute(value, "tracer", by_y(k)) for k in (1, 2, 3)]


def total(parts):
    got = [parts[0]] + [lax.ppermute(parts[k], "tracer", by_y(k)) for k in (1, 2, 3)]
    mine = got[0] + got[1] + (got[2] + got[3])
    return spread_y(mine + over_z(mine))


def per_device(c, flow, temp, dif, solar, rates, sea, floor):
    ids = jnp.stack(
        [
            lax.axis_index("tracer"),
            lax.axis_index("gx"),
            lax.axis_index("gy"),
            jnp.int32(lax.axis_size("gy")),
        ]
    )
    tile = (R, W)
    full = (NT, NL, R, W)
    part = (2, R, W)
    px, pyu, pyd = call(first_pack, "pack_one", [tile, tile, tile], 0)(c, flow, temp, sea, floor)
    even, odd = swap_pairs(px, "gx")
    lo, hi = ring_y(pyu, pyd)
    (own,) = call(extend_flow, "extend", [(2 * R + 8, W)], 1)(ids, flow, even, odd, lo, hi)
    gathered = spread_y(jnp.stack([own, over_z(own)]))
    edge = [tile, tile]
    wets = [(2, R, 2 * W), (2, R + HY, W)]
    mixed, a0, a1, a2, a3, cur, tadv = call(
        step_one, "step_one", [full, part, part, part, part, (2, NL, R, W), tile], 1,
        [(NL, 2 * R + 8, W), tile] + edge + wets + [(NT, R + HY, W), full, tile, (2, R + HY, W)],
    )(ids, c, *gathered, even, odd, lo, hi, temp, dif, sea, floor)
    sums = total((a0, a1, a2, a3))
    c, heated, px, pyu, pyd = call(
        biology_pack, "biology_one", [full, tile, tile, tile, tile], 2, [(NL, R, W), (NL, R, W)]
    )(ids, rates, mixed, *sums, solar, sea, floor, tadv, cur)
    even2, odd2 = swap_pairs(px, "gx")
    lo2, hi2 = ring_y(pyu, pyd)
    mixed, a0, a1, a2, a3, currents, tadv = call(
        step_two, "step_two", [full, part, part, part, part, (2, R, W), tile], 1,
        [tile] + edge + wets + [(NT, R + HY, W), full, (2, R + HY, W)],
    )(ids, c, cur, even2, odd2, lo2, hi2, even, odd, lo, hi, heated, dif, sea, floor)
    sums = total((a0, a1, a2, a3))
    c, last_temp = call(
        biology_last, "biology_two", [full, (1, R, W)], 2, [(NL, R, W), (NL, R, W)]
    )(ids, rates, mixed, *sums, solar, sea, floor, tadv)
    return c, currents.reshape(2, 1, R, W), last_temp


def solution(mesh):
    in_specs = (
        P("tracer", None, "gy", "gx"),
        P(None, "tracer", "gy", "gx"),
        P("tracer", "gy", "gx"),
        P(None, "gy", "gx"),
        P("gy", "gx"),
        P("tracer"),
        P("gy", "gx"),
        P("gy", "gx"),
    )
    out_specs = (
        P("tracer", None, "gy", "gx"),
        P(None, "tracer", "gy", "gx"),
        P("tracer", "gy", "gx"),
    )
    return jax.shard_map(
        per_device, mesh=mesh, in_specs=in_specs, out_specs=out_specs, check_vma=False
    )
```

time: 269 us -> 113 us (0.42)
  the two profiles are of different devices: /device:TPU:225 before, /device:TPU:2 now
where the time goes in v1:
time: 113 us; the launch traced here: 112 us
  starting transfers between devices  50.5 us (45%)
  waiting for transfers between devices  38.5 us (34%)
  Pallas kernels  17.5 us (15%)
  local copies, waits for them, and re-layouts  4.92 us (4%)
    ppermute x9, waiting for transfers between devices, spread_y(): return [value] + [lax.ppermute(value, 'tracer', by_y(k)) for k in (1, 2, 3)]  19.7 us
    pallas_call x6, Pallas kernels, run(): pl.pallas_call(body, name=name, out_shape=[jax.ShapeDtypeStruct(s, f32) f...  17.5 us
    ppermute x3, starting transfers between devices, over_z(): return lax.ppermute(value, 'tracer', [(i, i ^ 4) for i in range(8)])  17.1 us
    ppermute x9, starting transfers between devices, spread_y(): return [value] + [lax.ppermute(value, 'tracer', by_y(k)) for k in (1, 2, 3)]  11.8 us
    ppermute x4, starting transfers between devices, swap_pairs(): return (lax.ppermute(value, axis, even), lax.ppermute(value, axis, odd))  10.9 us
    ppermute x3, waiting for transfers between devices, over_z(): return lax.ppermute(value, 'tracer', [(i, i ^ 4) for i in range(8)])  8.42 us
    ppermute x6, starting transfers between devices, total(): lax.ppermute(parts[k], 'tracer', by_y(k))  7.29 us
    ppermute x6, waiting for transfers between devices, total(): lax.ppermute(parts[k], 'tracer', by_y(k))  7.02 us
  transfers between devices with their start and end apart: 26, of which 18 were waited for; matrix products, arithmetic and copies ran while one was open for 0% of the time, Pallas kernels for 0%

profile of v1, /device:TPU:2, one launch (start us, length us, event | category | flops | bytes accessed | tf_op | source)
XLA Modules:
  0.0 112.4 jit_solution(7617766235328920674)
XLA Ops:
  0.6 1.1 %copy-done = f32[3,8,64,128]{3,2,1,0:T(8,128)S(1)} copy-done((f32[3,8,64,128]{3,2,1,0:T(8,128)S(1)}, f32[3,8,64,128]{3,2,1,0:T(8,128)}, u32[]{:S(2)}) %copy-start) | copy-done | bytes 786456
  1.8 0.8 copy-done.3
  2.5 0.8 copy-done.5
  3.3 0.8 copy-done.7
  4.1 0.8 copy-done.9
  4.9 0.9 pack_one.1
  5.7 0.7 collective-permute-start.1
  6.4 5.2 %collective-permute-start = (f32[64,128]{1,0:T(8,128)S(1)}, f32[64,128]{1,0:T(8,128)S(1)}, u32[]{:S(2)}, u32[]{:S(2)}) collective-permute-start(f32[64,128]{1,0:T(8,128)S(1)} %get-tuple-element.27), channel_id=1, source_target_pairs={{0,64},{64,0},{128,192},{192,128},{1,65},{65,1},{129,193},{193,129... | collective-permute-start | bytes 98312 | tf_op jit(solution)/shard_map/ppermute | solution.py:407
  11.6 0.0 collective-permute-start.2
  11.6 1.7 %collective-permute-start.3 = (f32[64,128]{1,0:T(8,128)S(1)}, f32[64,128]{1,0:T(8,128)S(1)}, u32[]{:S(2)}, u32[]{:S(2)}) collective-permute-start(f32[64,128]{1,0:T(8,128)S(1)} %get-tuple-element.29), channel_id=1, source_target_pairs={{8,0},{16,8},{24,16},{32,24},{40,32},{48,40},{56,48},{0,56},{9,1},... | collective-permute-start | bytes 98312 | tf_op jit(solution)/shard_map/ppermute | solution.py:414
  13.3 0.1 pad_add_fusion.ids_ref
  13.4 1.5 %collective-permute-done.2.lo_ref.lo1_ref = f32[64,128]{1,0:T(8,128)S(1)} collective-permute-done((f32[64,128]{1,0:T(8,128)S(1)}, f32[64,128]{1,0:T(8,128)S(1)}, u32[]{:S(2)}, u32[]{:S(2)}) %collective-permute-start.2) | collective-permute-done | bytes 32800 | tf_op jit(solution)/shard_map/ppermute | solution.py:414
  14.9 0.0 collective-permute-done.3.hi_ref.hi1_ref
  14.9 0.0 collective-permute-done.even_ref.even1_ref
  14.9 0.6 extend.1
  15.5 5.5 %collective-permute-start.4 = (f32[136,128]{1,0:T(8,128)S(1)}, f32[136,128]{1,0:T(8,128)S(1)}, u32[]{:S(2)}, u32[]{:S(2)}) collective-permute-start(f32[136,128]{1,0:T(8,128)S(1)} %extend.1), channel_id=1, source_target_pairs={{0,4},{1,5},{2,6},{3,7},{4,0},{5,1},{6,2},{7,3},{8,12},{9,13},{10,... | collective-permute-start | bytes 208904 | tf_op jit(solution)/shard_map/ppermute | solution.py:422
  21.0 2.9 %collective-permute-done.4 = f32[136,128]{1,0:T(8,128)S(1)} collective-permute-done((f32[136,128]{1,0:T(8,128)S(1)}, f32[136,128]{1,0:T(8,128)S(1)}, u32[]{:S(2)}, u32[]{:S(2)}) %collective-permute-start.4) | collective-permute-done | bytes 69664 | tf_op jit(solution)/shard_map/ppermute | solution.py:422
  24.0 3.1 %collective-permute-start.7 = (f32[2,136,128]{2,1,0:T(8,128)S(1)}, f32[2,136,128]{2,1,0:T(8,128)S(1)}, u32[]{:S(2)}, u32[]{:S(2)}) collective-permute-start(f32[2,136,128]{2,1,0:T(8,128)S(1)} %pad_maximum_fusion.g0), channel_id=1, source_target_pairs={{0,3},{1,0},{2,1},{3,2},{4,7},{5,4},{6,5},{7,6},{8,11},{9,8},{10,9... | collective-permute-start | bytes 417800 | tf_op jit(solution)/shard_map/ppermute | solution.py:426
  27.1 0.6 collective-permute-start.6
  27.7 1.0 collective-permute-start.5
  28.7 4.9 %collective-permute-done.7.g3 = f32[2,136,128]{2,1,0:T(8,128)S(1)} collective-permute-done((f32[2,136,128]{2,1,0:T(8,128)S(1)}, f32[2,136,128]{2,1,0:T(8,128)S(1)}, u32[]{:S(2)}, u32[]{:S(2)}) %collective-permute-start.7) | collective-permute-done | bytes 139296 | tf_op jit(solution)/shard_map/ppermute | solution.py:426
  33.6 1.6 %collective-permute-done.6.g2 = f32[2,136,128]{2,1,0:T(8,128)S(1)} collective-permute-done((f32[2,136,128]{2,1,0:T(8,128)S(1)}, f32[2,136,128]{2,1,0:T(8,128)S(1)}, u32[]{:S(2)}, u32[]{:S(2)}) %collective-permute-start.6) | collective-permute-done | bytes 139296 | tf_op jit(solution)/shard_map/ppermute | solution.py:426
  35.2 2.1 %collective-permute-done.5.g1 = f32[2,136,128]{2,1,0:T(8,128)S(1)} collective-permute-done((f32[2,136,128]{2,1,0:T(8,128)S(1)}, f32[2,136,128]{2,1,0:T(8,128)S(1)}, u32[]{:S(2)}, u32[]{:S(2)}) %collective-permute-start.5) | collective-permute-done | bytes 139296 | tf_op jit(solution)/shard_map/ppermute | solution.py:426
  37.3 6.8 %step_one.1 = (f32[3,8,64,128]{3,2,1,0:T(8,128)S(1)}, f32[2,64,128]{2,1,0:T(8,128)S(1)}, f32[2,64,128]{2,1,0:T(8,128)S(1)}, f32[2,64,128]{2,1,0:T(8,128)S(1)}, f...) custom-call(s32[4]{0:T(128)S(1)} %pad_add_fusion.ids_ref, ...), custom_call_target="tpu_custom_call" | custom-call | tf_op jit(solution)/shard_map/step_one/pallas_call | solution.py:21
  44.2 0.1 collective-permute-start.8
  44.2 2.1 %collective-permute-start.9 = (f32[2,64,128]{2,1,0:T(8,128)S(1)}, f32[2,64,128]{2,1,0:T(8,128)S(1)}, u32[]{:S(2)}, u32[]{:S(2)}) collective-permute-start(f32[2,64,128]{2,1,0:T(8,128)S(1)} %get-tuple-element.33), channel_id=1, source_target_pairs={{0,2},{1,3},{2,0},{3,1},{4,6},{5,7},{6,4},{7,5},{8,10},{9,11},{10,... | collective-permute-start | bytes 196616 | tf_op jit(solution)/shard_map/ppermute | solution.py:430
  46.3 1.2 %collective-permute-start.10 = (f32[2,64,128]{2,1,0:T(8,128)S(1)}, f32[2,64,128]{2,1,0:T(8,128)S(1)}, u32[]{:S(2)}, u32[]{:S(2)}) collective-permute-start(f32[2,64,128]{2,1,0:T(8,128)S(1)} %get-tuple-element.34), channel_id=1, source_target_pairs={{0,3},{1,0},{2,1},{3,2},{4,7},{5,4},{6,5},{7,6},{8,11},{9,8},{10,9... | collective-permute-start | bytes 196616 | tf_op jit(solution)/shard_map/ppermute | solution.py:430
  47.5 3.4 %collective-permute-done.8 = f32[2,64,128]{2,1,0:T(8,128)S(1)} collective-permute-done((f32[2,64,128]{2,1,0:T(8,128)S(1)}, f32[2,64,128]{2,1,0:T(8,128)S(1)}, u32[]{:S(2)}, u32[]{:S(2)}) %collective-permute-start.8) | collective-permute-done | bytes 65568 | tf_op jit(solution)/shard_map/ppermute | solution.py:430
  50.9 0.0 collective-permute-done.9
  50.9 0.6 collective-permute-done.10
  51.5 0.0 copy-start.11
  51.5 5.6 %collective-permute-start.11 = (f32[2,64,128]{2,1,0:T(8,128)S(1)}, f32[2,64,128]{2,1,0:T(8,128)S(1)}, u32[]{:S(2)}, u32[]{:S(2)}) collective-permute-start(f32[2,64,128]{2,1,0:T(8,128)S(1)} %add_add_fusion.1), channel_id=1, source_target_pairs={{0,4},{1,5},{2,6},{3,7},{4,0},{5,1},{6,2},{7,3},{8,12},{9,13},{10,... | collective-permute-start | bytes 196616 | tf_op jit(solution)/shard_map/ppermute | solution.py:422
  57.0 2.8 %collective-permute-done.11 = f32[2,64,128]{2,1,0:T(8,128)S(1)} collective-permute-done((f32[2,64,128]{2,1,0:T(8,128)S(1)}, f32[2,64,128]{2,1,0:T(8,128)S(1)}, u32[]{:S(2)}, u32[]{:S(2)}) %collective-permute-start.11) | collective-permute-done | bytes 65568 | tf_op jit(solution)/shard_map/ppermute | solution.py:422
  59.8 2.5 %collective-permute-start.14 = (f32[2,64,128]{2,1,0:T(8,128)S(1)}, f32[2,64,128]{2,1,0:T(8,128)S(1)}, u32[]{:S(2)}, u32[]{:S(2)}) collective-permute-start(f32[2,64,128]{2,1,0:T(8,128)S(1)} %add.27.t0), channel_id=1, source_target_pairs={{0,3},{1,0},{2,1},{3,2},{4,7},{5,4},{6,5},{7,6},{8,11},{9,8},{10,9... | collective-permute-start | bytes 196616 | tf_op jit(solution)/shard_map/ppermute | solution.py:426
  62.3 0.8 collective-permute-start.13
  63.1 0.1 collective-permute-start.12
  63.3 1.6 %collective-permute-done.14.t3 = f32[2,64,128]{2,1,0:T(8,128)S(1)} collective-permute-done((f32[2,64,128]{2,1,0:T(8,128)S(1)}, f32[2,64,128]{2,1,0:T(8,128)S(1)}, u32[]{:S(2)}, u32[]{:S(2)}) %collective-permute-start.14) | collective-permute-done | bytes 65568 | tf_op jit(solution)/shard_map/ppermute | solution.py:426
  64.8 3.3 %collective-permute-done.13.t2 = f32[2,64,128]{2,1,0:T(8,128)S(1)} collective-permute-done((f32[2,64,128]{2,1,0:T(8,128)S(1)}, f32[2,64,128]{2,1,0:T(8,128)S(1)}, u32[]{:S(2)}, u32[]{:S(2)}) %collective-permute-start.13) | collective-permute-done | bytes 65568 | tf_op jit(solution)/shard_map/ppermute | solution.py:426
  68.1 0.7 collective-permute-done.12.t1
  68.8 0.7 copy-done.12
  69.4 1.9 %biology_one.1 = (f32[3,8,64,128]{3,2,1,0:T(8,128)S(1)}, f32[64,128]{1,0:T(8,128)S(1)}, f32[64,128]{1,0:T(8,128)S(1)}, f32[64,128]{1,0:T(8,128)S(1)}, f32[64,128]{1,0:T(8,128)S(1)}) custom-call(s32[4]{0:T(128)S(1)} %pad_add_fusion.ids_ref, f32[3]{0:T(128)S(1)} %copy-done.12, f32[3,8,64,128]{3,2,1,0:T(8,128)S(1)} %get-tuple-element.30.mix_ref, ...), custom_call_target="tpu_custom_call" | custom-call | tf_op jit(solution)/shard_map/biology_one/pallas_call | solution.py:21
  71.3 0.0 collective-permute-start.17
  71.3 1.7 %collective-permute-start.18 = (f32[64,128]{1,0:T(8,128)S(1)}, f32[64,128]{1,0:T(8,128)S(1)}, u32[]{:S(2)}, u32[]{:S(2)}) collective-permute-start(f32[64,128]{1,0:T(8,128)S(1)} %get-tuple-element.40), channel_id=1, source_target_pairs={{8,0},{16,8},{24,16},{32,24},{40,32},{48,40},{56,48},{0,56},{9,1},... | collective-permute-start | bytes 98312 | tf_op jit(solution)/shard_map/ppermute | solution.py:414
  73.1 0.7 collective-permute-start.16
  73.7 4.4 %collective-permute-start.15 = (f32[64,128]{1,0:T(8,128)S(1)}, f32[64,128]{1,0:T(8,128)S(1)}, u32[]{:S(2)}, u32[]{:S(2)}) collective-permute-start(f32[64,128]{1,0:T(8,128)S(1)} %get-tuple-element.38), channel_id=1, source_target_pairs={{0,64},{64,0},{128,192},{192,128},{1,65},{65,1},{129,193},{193,129... | collective-permute-start | bytes 98312 | tf_op jit(solution)/shard_map/ppermute | solution.py:407
  78.1 0.0 collective-permute-done.17.lo_ref
  78.2 0.0 collective-permute-done.18.hi_ref
  78.2 0.0 collective-permute-done.16.odd_ref
  78.2 1.9 %collective-permute-done.15.even_ref = f32[64,128]{1,0:T(8,128)S(1)} collective-permute-done((f32[64,128]{1,0:T(8,128)S(1)}, f32[64,128]{1,0:T(8,128)S(1)}, u32[]{:S(2)}, u32[]{:S(2)}) %collective-permute-start.15) | collective-permute-done | bytes 32800 | tf_op jit(solution)/shard_map/ppermute | solution.py:407
  80.0 5.5 %step_two.1 = (f32[3,8,64,128]{3,2,1,0:T(8,128)S(1)}, f32[2,64,128]{2,1,0:T(8,128)S(1)}, f32[2,64,128]{2,1,0:T(8,128)S(1)}, f32[2,64,128]{2,1,0:T(8,128)S(1)}, f...) custom-call(s32[4]{0:T(128)S(1)} %pad_add_fusion.ids_ref, ...), custom_call_target="tpu_custom_call" | custom-call | tf_op jit(solution)/shard_map/step_two/pallas_call | solution.py:21
  85.5 0.0 collective-permute-start.19
  85.5 2.0 %collective-permute-start.20 = (f32[2,64,128]{2,1,0:T(8,128)S(1)}, f32[2,64,128]{2,1,0:T(8,128)S(1)}, u32[]{:S(2)}, u32[]{:S(2)}) collective-permute-start(f32[2,64,128]{2,1,0:T(8,128)S(1)} %get-tuple-element.45), channel_id=1, source_target_pairs={{0,2},{1,3},{2,0},{3,1},{4,6},{5,7},{6,4},{7,5},{8,10},{9,11},{10,... | collective-permute-start | bytes 196616 | tf_op jit(solution)/shard_map/ppermute | solution.py:430
  87.5 1.9 %collective-permute-start.21 = (f32[2,64,128]{2,1,0:T(8,128)S(1)}, f32[2,64,128]{2,1,0:T(8,128)S(1)}, u32[]{:S(2)}, u32[]{:S(2)}) collective-permute-start(f32[2,64,128]{2,1,0:T(8,128)S(1)} %get-tuple-element.46), channel_id=1, source_target_pairs={{0,3},{1,0},{2,1},{3,2},{4,7},{5,4},{6,5},{7,6},{8,11},{9,8},{10,9... | collective-permute-start | bytes 196616 | tf_op jit(solution)/shard_map/ppermute | solution.py:430
  89.5 2.2 %collective-permute-done.19 = f32[2,64,128]{2,1,0:T(8,128)S(1)} collective-permute-done((f32[2,64,128]{2,1,0:T(8,128)S(1)}, f32[2,64,128]{2,1,0:T(8,128)S(1)}, u32[]{:S(2)}, u32[]{:S(2)}) %collective-permute-start.19) | collective-permute-done | bytes 65568 | tf_op jit(solution)/shard_map/ppermute | solution.py:430
  91.7 0.9 collective-permute-done.21
  92.6 6.0 %collective-permute-start.22 = (f32[2,64,128]{2,1,0:T(8,128)S(1)}, f32[2,64,128]{2,1,0:T(8,128)S(1)}, u32[]{:S(2)}, u32[]{:S(2)}) collective-permute-start(f32[2,64,128]{2,1,0:T(8,128)S(1)} %add_add_fusion), channel_id=1, source_target_pairs={{0,4},{1,5},{2,6},{3,7},{4,0},{5,1},{6,2},{7,3},{8,12},{9,13},{10,... | collective-permute-start | bytes 196616 | tf_op jit(solution)/shard_map/ppermute | solution.py:422
  98.6 2.7 %collective-permute-done.22 = f32[2,64,128]{2,1,0:T(8,128)S(1)} collective-permute-done((f32[2,64,128]{2,1,0:T(8,128)S(1)}, f32[2,64,128]{2,1,0:T(8,128)S(1)}, u32[]{:S(2)}, u32[]{:S(2)}) %collective-permute-start.22) | collective-permute-done | bytes 65568 | tf_op jit(solution)/shard_map/ppermute | solution.py:422
  101.3 2.8 %collective-permute-start.25 = (f32[2,64,128]{2,1,0:T(8,128)S(1)}, f32[2,64,128]{2,1,0:T(8,128)S(1)}, u32[]{:S(2)}, u32[]{:S(2)}) collective-permute-start(f32[2,64,128]{2,1,0:T(8,128)S(1)} %add.31.t0), channel_id=1, source_target_pairs={{0,3},{1,0},{2,1},{3,2},{4,7},{5,4},{6,5},{7,6},{8,11},{9,8},{10,9... | collective-permute-start | bytes 196616 | tf_op jit(solution)/shard_map/ppermute | solution.py:426
  104.0 0.6 collective-permute-start.24
  104.6 0.4 collective-permute-start.23
  105.0 1.6 %collective-permute-done.25.t3 = f32[2,64,128]{2,1,0:T(8,128)S(1)} collective-permute-done((f32[2,64,128]{2,1,0:T(8,128)S(1)}, f32[2,64,128]{2,1,0:T(8,128)S(1)}, u32[]{:S(2)}, u32[]{:S(2)}) %collective-permute-start.25) | collective-permute-done | bytes 65568 | tf_op jit(solution)/shard_map/ppermute | solution.py:426
  106.5 3.3 %collective-permute-done.24.t2 = f32[2,64,128]{2,1,0:T(8,128)S(1)} collective-permute-done((f32[2,64,128]{2,1,0:T(8,128)S(1)}, f32[2,64,128]{2,1,0:T(8,128)S(1)}, u32[]{:S(2)}, u32[]{:S(2)}) %collective-permute-start.24) | collective-permute-done | bytes 65568 | tf_op jit(solution)/shard_map/ppermute | solution.py:426
  109.8 0.7 collective-permute-done.23.t1
  110.5 1.9 %biology_two.1 = (f32[3,8,64,128]{3,2,1,0:T(8,128)}, f32[1,64,128]{2,1,0:T(8,128)}) custom-call(s32[4]{0:T(128)S(1)} %pad_add_fusion.ids_ref, f32[3]{0:T(128)S(1)} %copy-done.12, f32[3,8,64,128]{3,2,1,0:T(8,128)S(1)} %get-tuple-element.42.mix_ref, f32[2,64,128]{2,1,0:T(8,128)S(1)} %add.31.t0, f32[2,64,128]{2,1,0:T(8,128)S(1)} %collective-permute-done.23.t1, ...), custom_call_target="tpu_custom_call" | custom-call | tf_op jit(solution)/shard_map/biology_two/pallas_call | solution.py:21
  (26 shorter events, 0.1 us)
Async XLA Ops:
  0.6 1.1 %copy-start = (f32[3,8,64,128]{3,2,1,0:T(8,128)S(1)}, f32[3,8,64,128]{3,2,1,0:T(8,128)}, u32[]{:S(2)}) copy-start(f32[3,8,64,128]{3,2,1,0:T(8,128)} %c_ref.3) | copy-start | bytes 2359300
  1.8 0.8 copy-start.3
  2.5 0.8 copy-start.5
  3.3 0.8 copy-start.7
  4.1 0.8 copy-start.9
  4.9 10.1 %copy-start.8 = (f32[2,1,64,128]{3,2,1,0:T(8,128)S(1)}, f32[2,1,64,128]{3,2,1,0:T(8,128)}, u32[]{:S(2)}) copy-start(f32[2,1,64,128]{3,2,1,0:T(8,128)} %flow_ref.3) | copy-start | bytes 196612
  4.9 32.4 %copy-start.1 = (f32[3,8,64,128]{3,2,1,0:T(8,128)S(1)}, f32[3,8,64,128]{3,2,1,0:T(8,128)}, u32[]{:S(2)}) copy-start(f32[3,8,64,128]{3,2,1,0:T(8,128)} %c_ref.3) | copy-start | bytes 2359300
  5.7 9.2 %collective-permute-start.1 = (f32[64,128]{1,0:T(8,128)S(1)}, f32[64,128]{1,0:T(8,128)S(1)}, u32[]{:S(2)}, u32[]{:S(2)}) collective-permute-start(f32[64,128]{1,0:T(8,128)S(1)} %get-tuple-element.27), channel_id=1, source_target_pairs={{64,128},{128,64},{65,129},{129,65},{66,130},{130,66},{67,131},{13... | collective-permute-start | bytes 98312 | tf_op jit(solution)/shard_map/ppermute | solution.py:407
  6.4 8.5 %collective-permute-start = (f32[64,128]{1,0:T(8,128)S(1)}, f32[64,128]{1,0:T(8,128)S(1)}, u32[]{:S(2)}, u32[]{:S(2)}) collective-permute-start(f32[64,128]{1,0:T(8,128)S(1)} %get-tuple-element.27), channel_id=1, source_target_pairs={{0,64},{64,0},{128,192},{192,128},{1,65},{65,1},{129,193},{193,129... | collective-permute-start | bytes 98312 | tf_op jit(solution)/shard_map/ppermute | solution.py:407
  11.6 3.3 %collective-permute-start.2 = (f32[64,128]{1,0:T(8,128)S(1)}, f32[64,128]{1,0:T(8,128)S(1)}, u32[]{:S(2)}, u32[]{:S(2)}) collective-permute-start(f32[64,128]{1,0:T(8,128)S(1)} %get-tuple-element.28), channel_id=1, source_target_pairs={{0,8},{8,16},{16,24},{24,32},{32,40},{40,48},{48,56},{56,0},{1,9},... | collective-permute-start | bytes 98312 | tf_op jit(solution)/shard_map/ppermute | solution.py:414
  11.6 3.3 %collective-permute-start.3 = (f32[64,128]{1,0:T(8,128)S(1)}, f32[64,128]{1,0:T(8,128)S(1)}, u32[]{:S(2)}, u32[]{:S(2)}) collective-permute-start(f32[64,128]{1,0:T(8,128)S(1)} %get-tuple-element.29), channel_id=1, source_target_pairs={{8,0},{16,8},{24,16},{32,24},{40,32},{48,40},{56,48},{0,56},{9,1},... | collective-permute-start | bytes 98312 | tf_op jit(solution)/shard_map/ppermute | solution.py:414
  13.4 23.9 %copy-start.2 = (f32[8,64,128]{2,1,0:T(8,128)S(1)}, f32[8,64,128]{2,1,0:T(8,128)}, u32[]{:S(2)}) copy-start(f32[8,64,128]{2,1,0:T(8,128)} %dif_ref.3) | copy-start | bytes 786436
  15.5 8.4 %collective-permute-start.4 = (f32[136,128]{1,0:T(8,128)S(1)}, f32[136,128]{1,0:T(8,128)S(1)}, u32[]{:S(2)}, u32[]{:S(2)}) collective-permute-start(f32[136,128]{1,0:T(8,128)S(1)} %extend.1), channel_id=1, source_target_pairs={{0,4},{1,5},{2,6},{3,7},{4,0},{5,1},{6,2},{7,3},{8,12},{9,13},{10,... | collective-permute-start | bytes 208904 | tf_op jit(solution)/shard_map/ppermute | solution.py:422
  24.0 13.4 %copy-start.4 = (s32[64,128]{1,0:T(8,128)S(1)}, s32[64,128]{1,0:T(8,128)}, u32[]{:S(2)}) copy-start(s32[64,128]{1,0:T(8,128)} %sea_ref.9) | copy-start | bytes 98308
  24.0 13.4 %copy-start.6 = (s32[64,128]{1,0:T(8,128)S(1)}, s32[64,128]{1,0:T(8,128)}, u32[]{:S(2)}) copy-start(s32[64,128]{1,0:T(8,128)} %floor_ref.9) | copy-start | bytes 98308
  24.0 13.4 %copy-start.10 = (f32[1,64,128]{2,1,0:T(8,128)S(1)}, f32[1,64,128]{2,1,0:T(8,128)}, u32[]{:S(2)}) copy-start(f32[1,64,128]{2,1,0:T(8,128)} %temp_ref.3) | copy-start | bytes 98308
  24.0 9.6 %collective-permute-start.7 = (f32[2,136,128]{2,1,0:T(8,128)S(1)}, f32[2,136,128]{2,1,0:T(8,128)S(1)}, u32[]{:S(2)}, u32[]{:S(2)}) collective-permute-start(f32[2,136,128]{2,1,0:T(8,128)S(1)} %pad_maximum_fusion.g0), channel_id=1, source_target_pairs={{0,3},{1,0},{2,1},{3,2},{4,7},{5,4},{6,5},{7,6},{8,11},{9,8},{10,9... | collective-permute-start | bytes 417800 | tf_op jit(solution)/shard_map/ppermute | solution.py:426
  27.1 8.1 %collective-permute-start.6 = (f32[2,136,128]{2,1,0:T(8,128)S(1)}, f32[2,136,128]{2,1,0:T(8,128)S(1)}, u32[]{:S(2)}, u32[]{:S(2)}) collective-permute-start(f32[2,136,128]{2,1,0:T(8,128)S(1)} %pad_maximum_fusion.g0), channel_id=1, source_target_pairs={{0,2},{1,3},{2,0},{3,1},{4,6},{5,7},{6,4},{7,5},{8,10},{9,11},{10,... | collective-permute-start | bytes 417800 | tf_op jit(solution)/shard_map/ppermute | solution.py:426
  27.7 9.6 %collective-permute-start.5 = (f32[2,136,128]{2,1,0:T(8,128)S(1)}, f32[2,136,128]{2,1,0:T(8,128)S(1)}, u32[]{:S(2)}, u32[]{:S(2)}) collective-permute-start(f32[2,136,128]{2,1,0:T(8,128)S(1)} %pad_maximum_fusion.g0), channel_id=1, source_target_pairs={{0,1},{1,2},{2,3},{3,0},{4,5},{5,6},{6,7},{7,4},{8,9},{9,10},{10,1... | collective-permute-start | bytes 417800 | tf_op jit(solution)/shard_map/ppermute | solution.py:426
  44.2 6.7 %collective-permute-start.8 = (f32[2,64,128]{2,1,0:T(8,128)S(1)}, f32[2,64,128]{2,1,0:T(8,128)S(1)}, u32[]{:S(2)}, u32[]{:S(2)}) collective-permute-start(f32[2,64,128]{2,1,0:T(8,128)S(1)} %get-tuple-element.32), channel_id=1, source_target_pairs={{0,1},{1,2},{2,3},{3,0},{4,5},{5,6},{6,7},{7,4},{8,9},{9,10},{10,1... | collective-permute-start | bytes 196616 | tf_op jit(solution)/shard_map/ppermute | solution.py:430
  44.2 6.6 %collective-permute-start.9 = (f32[2,64,128]{2,1,0:T(8,128)S(1)}, f32[2,64,128]{2,1,0:T(8,128)S(1)}, u32[]{:S(2)}, u32[]{:S(2)}) collective-permute-start(f32[2,64,128]{2,1,0:T(8,128)S(1)} %get-tuple-element.33), channel_id=1, source_target_pairs={{0,2},{1,3},{2,0},{3,1},{4,6},{5,7},{6,4},{7,5},{8,10},{9,11},{10,... | collective-permute-start | bytes 196616 | tf_op jit(solution)/shard_map/ppermute | solution.py:430
  46.3 5.1 %collective-permute-start.10 = (f32[2,64,128]{2,1,0:T(8,128)S(1)}, f32[2,64,128]{2,1,0:T(8,128)S(1)}, u32[]{:S(2)}, u32[]{:S(2)}) collective-permute-start(f32[2,64,128]{2,1,0:T(8,128)S(1)} %get-tuple-element.34), channel_id=1, source_target_pairs={{0,3},{1,0},{2,1},{3,2},{4,7},{5,4},{6,5},{7,6},{8,11},{9,8},{10,9... | collective-permute-start | bytes 196616 | tf_op jit(solution)/shard_map/ppermute | solution.py:430
  51.5 17.3 %copy-start.11 = (f32[64,128]{1,0:T(8,128)S(1)}, f32[64,128]{1,0:T(8,128)}, u32[]{:S(2)}) copy-start(f32[64,128]{1,0:T(8,128)} %solar_ref.3) | copy-start | bytes 98308
  51.5 8.4 %collective-permute-start.11 = (f32[2,64,128]{2,1,0:T(8,128)S(1)}, f32[2,64,128]{2,1,0:T(8,128)S(1)}, u32[]{:S(2)}, u32[]{:S(2)}) collective-permute-start(f32[2,64,128]{2,1,0:T(8,128)S(1)} %add_add_fusion.1), channel_id=1, source_target_pairs={{0,4},{1,5},{2,6},{3,7},{4,0},{5,1},{6,2},{7,3},{8,12},{9,13},{10,... | collective-permute-start | bytes 196616 | tf_op jit(solution)/shard_map/ppermute | solution.py:422
  59.8 5.0 %collective-permute-start.14 = (f32[2,64,128]{2,1,0:T(8,128)S(1)}, f32[2,64,128]{2,1,0:T(8,128)S(1)}, u32[]{:S(2)}, u32[]{:S(2)}) collective-permute-start(f32[2,64,128]{2,1,0:T(8,128)S(1)} %add.27.t0), channel_id=1, source_target_pairs={{0,3},{1,0},{2,1},{3,2},{4,7},{5,4},{6,5},{7,6},{8,11},{9,8},{10,9... | collective-permute-start | bytes 196616 | tf_op jit(solution)/shard_map/ppermute | solution.py:426
  62.3 5.8 %collective-permute-start.13 = (f32[2,64,128]{2,1,0:T(8,128)S(1)}, f32[2,64,128]{2,1,0:T(8,128)S(1)}, u32[]{:S(2)}, u32[]{:S(2)}) collective-permute-start(f32[2,64,128]{2,1,0:T(8,128)S(1)} %add.27.t0), channel_id=1, source_target_pairs={{0,2},{1,3},{2,0},{3,1},{4,6},{5,7},{6,4},{7,5},{8,10},{9,11},{10,... | collective-permute-start | bytes 196616 | tf_op jit(solution)/shard_map/ppermute | solution.py:426
  63.1 5.6 %collective-permute-start.12 = (f32[2,64,128]{2,1,0:T(8,128)S(1)}, f32[2,64,128]{2,1,0:T(8,128)S(1)}, u32[]{:S(2)}, u32[]{:S(2)}) collective-permute-start(f32[2,64,128]{2,1,0:T(8,128)S(1)} %add.27.t0), channel_id=1, source_target_pairs={{0,1},{1,2},{2,3},{3,0},{4,5},{5,6},{6,7},{7,4},{8,9},{9,10},{10,1... | collective-permute-start | bytes 196616 | tf_op jit(solution)/shard_map/ppermute | solution.py:426
  68.8 0.7 copy-start.12
  71.3 6.8 %collective-permute-start.17 = (f32[64,128]{1,0:T(8,128)S(1)}, f32[64,128]{1,0:T(8,128)S(1)}, u32[]{:S(2)}, u32[]{:S(2)}) collective-permute-start(f32[64,128]{1,0:T(8,128)S(1)} %get-tuple-element.39), channel_id=1, source_target_pairs={{0,8},{8,16},{16,24},{24,32},{32,40},{40,48},{48,56},{56,0},{1,9},... | collective-permute-start | bytes 98312 | tf_op jit(solution)/shard_map/ppermute | solution.py:414
  71.3 6.8 %collective-permute-start.18 = (f32[64,128]{1,0:T(8,128)S(1)}, f32[64,128]{1,0:T(8,128)S(1)}, u32[]{:S(2)}, u32[]{:S(2)}) collective-permute-start(f32[64,128]{1,0:T(8,128)S(1)} %get-tuple-element.40), channel_id=1, source_target_pairs={{8,0},{16,8},{24,16},{32,24},{40,32},{48,40},{56,48},{0,56},{9,1},... | collective-permute-start | bytes 98312 | tf_op jit(solution)/shard_map/ppermute | solution.py:414
  73.1 5.1 %collective-permute-start.16 = (f32[64,128]{1,0:T(8,128)S(1)}, f32[64,128]{1,0:T(8,128)S(1)}, u32[]{:S(2)}, u32[]{:S(2)}) collective-permute-start(f32[64,128]{1,0:T(8,128)S(1)} %get-tuple-element.38), channel_id=1, source_target_pairs={{64,128},{128,64},{65,129},{129,65},{66,130},{130,66},{67,131},{13... | collective-permute-start | bytes 98312 | tf_op jit(solution)/shard_map/ppermute | solution.py:407
  73.7 6.3 %collective-permute-start.15 = (f32[64,128]{1,0:T(8,128)S(1)}, f32[64,128]{1,0:T(8,128)S(1)}, u32[]{:S(2)}, u32[]{:S(2)}) collective-permute-start(f32[64,128]{1,0:T(8,128)S(1)} %get-tuple-element.38), channel_id=1, source_target_pairs={{0,64},{64,0},{128,192},{192,128},{1,65},{65,1},{129,193},{193,129... | collective-permute-start | bytes 98312 | tf_op jit(solution)/shard_map/ppermute | solution.py:407
  85.5 6.2 %collective-permute-start.19 = (f32[2,64,128]{2,1,0:T(8,128)S(1)}, f32[2,64,128]{2,1,0:T(8,128)S(1)}, u32[]{:S(2)}, u32[]{:S(2)}) collective-permute-start(f32[2,64,128]{2,1,0:T(8,128)S(1)} %get-tuple-element.44), channel_id=1, source_target_pairs={{0,1},{1,2},{2,3},{3,0},{4,5},{5,6},{6,7},{7,4},{8,9},{9,10},{10,1... | collective-permute-start | bytes 196616 | tf_op jit(solution)/shard_map/ppermute | solution.py:430
  85.5 6.2 %collective-permute-start.20 = (f32[2,64,128]{2,1,0:T(8,128)S(1)}, f32[2,64,128]{2,1,0:T(8,128)S(1)}, u32[]{:S(2)}, u32[]{:S(2)}) collective-permute-start(f32[2,64,128]{2,1,0:T(8,128)S(1)} %get-tuple-element.45), channel_id=1, source_target_pairs={{0,2},{1,3},{2,0},{3,1},{4,6},{5,7},{6,4},{7,5},{8,10},{9,11},{10,... | collective-permute-start | bytes 196616 | tf_op jit(solution)/shard_map/ppermute | solution.py:430
  87.5 5.0 %collective-permute-start.21 = (f32[2,64,128]{2,1,0:T(8,128)S(1)}, f32[2,64,128]{2,1,0:T(8,128)S(1)}, u32[]{:S(2)}, u32[]{:S(2)}) collective-permute-start(f32[2,64,128]{2,1,0:T(8,128)S(1)} %get-tuple-element.46), channel_id=1, source_target_pairs={{0,3},{1,0},{2,1},{3,2},{4,7},{5,4},{6,5},{7,6},{8,11},{9,8},{10,9... | collective-permute-start | bytes 196616 | tf_op jit(solution)/shard_map/ppermute | solution.py:430
  92.6 8.7 %collective-permute-start.22 = (f32[2,64,128]{2,1,0:T(8,128)S(1)}, f32[2,64,128]{2,1,0:T(8,128)S(1)}, u32[]{:S(2)}, u32[]{:S(2)}) collective-permute-start(f32[2,64,128]{2,1,0:T(8,128)S(1)} %add_add_fusion), channel_id=1, source_target_pairs={{0,4},{1,5},{2,6},{3,7},{4,0},{5,1},{6,2},{7,3},{8,12},{9,13},{10,... | collective-permute-start | bytes 196616 | tf_op jit(solution)/shard_map/ppermute | solution.py:422
  101.3 5.3 %collective-permute-start.25 = (f32[2,64,128]{2,1,0:T(8,128)S(1)}, f32[2,64,128]{2,1,0:T(8,128)S(1)}, u32[]{:S(2)}, u32[]{:S(2)}) collective-permute-start(f32[2,64,128]{2,1,0:T(8,128)S(1)} %add.31.t0), channel_id=1, source_target_pairs={{0,3},{1,0},{2,1},{3,2},{4,7},{5,4},{6,5},{7,6},{8,11},{9,8},{10,9... | collective-permute-start | bytes 196616 | tf_op jit(solution)/shard_map/ppermute | solution.py:426
  104.0 5.8 %collective-permute-start.24 = (f32[2,64,128]{2,1,0:T(8,128)S(1)}, f32[2,64,128]{2,1,0:T(8,128)S(1)}, u32[]{:S(2)}, u32[]{:S(2)}) collective-permute-start(f32[2,64,128]{2,1,0:T(8,128)S(1)} %add.31.t0), channel_id=1, source_target_pairs={{0,2},{1,3},{2,0},{3,1},{4,6},{5,7},{6,4},{7,5},{8,10},{9,11},{10,... | collective-permute-start | bytes 196616 | tf_op jit(solution)/shard_map/ppermute | solution.py:426
  104.6 5.9 %collective-permute-start.23 = (f32[2,64,128]{2,1,0:T(8,128)S(1)}, f32[2,64,128]{2,1,0:T(8,128)S(1)}, u32[]{:S(2)}, u32[]{:S(2)}) collective-permute-start(f32[2,64,128]{2,1,0:T(8,128)S(1)} %add.31.t0), channel_id=1, source_target_pairs={{0,1},{1,2},{2,3},{3,0},{4,5},{5,6},{6,7},{7,4},{8,9},{9,10},{10,1... | collective-permute-start | bytes 196616 | tf_op jit(solution)/shard_map/ppermute | solution.py:426

commit v2 on v1

v2 whole, which is shorter than its diff:
```python
import jax
import jax.numpy as jnp
from jax import lax
from jax.experimental import pallas as pl
from jax.experimental.pallas import tpu as pltpu
from jax.sharding import PartitionSpec as P

NL = 8
R = 64
W = 128
NT = 3
NCH = NT * NL
HY = 16
UNROLL = 4
f32 = jnp.float32
VM = pl.BlockSpec(memory_space=pltpu.VMEM)
AN = pl.BlockSpec(memory_space=pl.ANY)
HB = pl.BlockSpec(memory_space=pltpu.HBM)
SM = pl.BlockSpec(memory_space=pltpu.SMEM)


def call(body, name, outs, n_scalar, scratch=(), n_any=0, sems=0):
    def run(*args):
        return pl.pallas_call(
            body,
            name=name,
            out_shape=[jax.ShapeDtypeStruct(s, f32) for s in outs],
            in_specs=[SM] * n_scalar + [VM] * (len(args) - n_scalar - n_any) + [HB if sems else AN] * n_any,
            out_specs=[VM] * len(outs),
            scratch_shapes=[s if hasattr(s, "dtype") else pltpu.VMEM(s, f32) for s in scratch]
            + ([pltpu.SemaphoreType.DMA((sems,))] if sems else []),
            compiler_params=pltpu.CompilerParams(vmem_limit_bytes=40 * 2**20),
        )(*args)

    return run


def lanes(shape):
    return lax.broadcasted_iota(jnp.int32, shape, 1)


def rx(v, k):
    return pltpu.roll(v, k % v.shape[1], 1)


def ry(v, k):
    return pltpu.roll(v, k % v.shape[0], 0)


def aside(v, shift):
    return pltpu.roll(v, shift, 1)


def minmod(a, b):
    return jnp.maximum(jnp.minimum(a, b), 0.0) + jnp.minimum(jnp.maximum(a, b), 0.0)


def coefs(vel):
    up = jnp.maximum(vel, 0.0)
    um = jnp.minimum(vel, 0.0)
    return up, um, 0.5 * up * (1.0 - up), 0.5 * um * (1.0 + um)


def divergence(c, co, roll):
    up, um, a, b = co
    ahead = roll(c, -1)
    d = ahead - c
    s = minmod(d, roll(d, 1))
    flux = up * c + a * s + um * ahead - b * roll(s, -1)
    return flux - roll(flux, 1)


def upwind(c, vel, roll):
    flux = jnp.maximum(vel, 0.0) * c + jnp.minimum(vel, 0.0) * roll(c, -1)
    return flux - roll(flux, 1)


def put_x(acc, value, lane, width):
    at = lanes(acc.shape)
    half = width // 2
    return jnp.where((at >= lane) & (at < lane + width), pltpu.roll(value, lane + half, 1), acc)


def pack_tracers(c_refs, px_ref, pyu_ref, pyd_ref):
    def level(l, carry):
        for t in range(NT):
            ch = t * NL + l
            c_ref = c_refs[t]
            px_ref[...] = put_x(px_ref[...], c_ref[l], 4 * ch, 4)
            pyu_ref[pl.ds(2 * ch, 2), :] = c_ref[l, R - 2 : R, :]
            pyd_ref[pl.ds(2 * ch, 2), :] = c_ref[l, 0:2, :]
        return carry

    lax.fori_loop(0, NL, level, 0, unroll=2)


def pack_rows(value, row, pyu_ref, pyd_ref):
    pyu_ref[row : row + 1, :] = value[R - 1 : R, :]
    pyd_ref[row : row + 1, :] = value[0:1, :]


def first_pack(
    c_hbm, flow_hbm, temp_hbm, sea_hbm, floor_hbm, px_ref, pyu_ref, pyd_ref,
    c_ref, flow_ref, temp_ref, sea_ref, floor_ref, sems,
):
    pairs = (
        (c_hbm, c_ref), (flow_hbm, flow_ref), (temp_hbm, temp_ref), (sea_hbm, sea_ref),
        (floor_hbm, floor_ref),
    )
    copies = [pltpu.make_async_copy(a, b, sems.at[k]) for k, (a, b) in enumerate(pairs)]
    for copy in copies:
        copy.start()
    px_ref[...] = jnp.zeros_like(px_ref)
    pyu_ref[...] = jnp.zeros_like(pyu_ref)
    pyd_ref[...] = jnp.zeros_like(pyd_ref)
    for copy in copies[1:]:
        copy.wait()
    singles = (
        (0, flow_ref[0, 0]),
        (1, flow_ref[1, 0]),
        (4, temp_ref[0]),
        (5, sea_ref[...].astype(f32)),
        (6, floor_ref[...].astype(f32)),
    )
    acc = px_ref[...]
    for j, value in singles:
        acc = put_x(acc, value, 96 + 2 * j, 2)
        pack_rows(value, 48 + j, pyu_ref, pyd_ref)
    px_ref[...] = acc
    copies[0].wait()
    pack_tracers([c_ref.at[t] for t in range(NT)], px_ref, pyu_ref, pyd_ref)


def pack_other(other_ref, px_in, pyu_in, pyd_in, px_ref, pyu_ref, pyd_ref):
    pyu_ref[...] = pyu_in[...]
    pyd_ref[...] = pyd_in[...]
    acc = px_in[...]
    for j in range(2):
        value = other_ref[j, 0]
        acc = put_x(acc, value, 100 + 2 * j, 2)
        pack_rows(value, 50 + j, pyu_ref, pyd_ref)
    px_ref[...] = acc


def join_x(ids_ref, left, right, left_end=96):
    at = lanes(left.shape)
    half = jnp.where(at < 96, (at >> 1) & 1, jnp.where(at < left_end, 0, at & 1))
    gx = ids_ref[1]
    left = jnp.where(gx == 0, 0.0, left)
    right = jnp.where(gx == ids_ref[4] - 1, 0.0, right)
    return jnp.where(half == 0, left, right)


def edges_y(ids_ref, lo_ref, hi_ref, los_ref, his_ref):
    gy = ids_ref[2]
    los_ref[...] = jnp.where(gy == 0, 0.0, lo_ref[...])
    his_ref[...] = jnp.where(gy == ids_ref[3] - 1, 0.0, hi_ref[...])


def extend_flow(
    ids_ref, flow_ref, other_ref, left_ref, right_ref, lo_ref, hi_ref, e_ref, xh_ref, los_ref,
    his_ref,
):
    joined = join_x(ids_ref, left_ref[...], right_ref[...])
    xh_ref[...] = joined
    edges_y(ids_ref, lo_ref, hi_ref, los_ref, his_ref)
    turned = jnp.concatenate([joined, jnp.zeros_like(joined)], 0).T
    for k, ref in enumerate((flow_ref, other_ref)):
        e_ref[k, 0:R, :] = ref[0, 0]
        e_ref[k, R : 2 * R, :] = ref[1, 0]
        e_ref[k, 2 * R : 2 * R + 4, :] = turned[96 + 4 * k : 100 + 4 * k, :]
        e_ref[k, 2 * R + 4 : 2 * R + 6, :] = los_ref[48 + 2 * k : 50 + 2 * k, :]
        e_ref[k, 2 * R + 6 : 2 * R + 8, :] = his_ref[48 + 2 * k : 50 + 2 * k, :]


def wet_setup(xh_ref, los_ref, his_ref, sea_ref, floor_ref, wx_ref, wy_ref):
    for k, ref in enumerate((sea_ref, floor_ref)):
        main = ref[...].astype(f32)
        wx_ref[k, :, :W] = main
        wx_ref[k, :, W:] = aside(xh_ref[...], (127 - (96 + 2 * (5 + k))) % W)
        wy_ref[k, :R, :] = main
        wy_ref[k, R : R + HY, :] = jnp.zeros((HY, W), f32)
        wy_ref[k, R : R + 1, :] = his_ref[53 + k : 54 + k, :]
        wy_ref[k, R + HY - 1 : R + HY, :] = los_ref[53 + k : 54 + k, :]


def wet_of(ref, l):
    return jnp.where(l.astype(f32) < ref[1], ref[0], 0.0)


def advect_level(t, l, c, xh_ref, los_ref, his_ref, east, north, wet, cy_all):
    cy_ref = cy_all.at[l]
    ch = t * NL + l
    cx = jnp.concatenate([c, aside(xh_ref[...], lax.rem(126 + W - 4 * ch, W))], 1)
    div = divergence(cx, coefs(east), rx)[:, :W]
    cy_ref[0:R, :] = c
    cy_ref[R : R + 2, :] = his_ref[pl.ds(2 * ch, 2), :]
    cy_ref[R + HY - 2 : R + HY, :] = los_ref[pl.ds(2 * ch, 2), :]
    div = div + divergence(cy_ref[...], coefs(north), ry)[:R]
    return wet * (c - div)


def mix(adv_ref, dif_ref, wx_ref, mix_ref):
    above = None
    wet = wet_of(wx_ref, jnp.int32(0))[:, :W]
    for l in range(NL):
        if l + 1 < NL:
            below_wet = wet_of(wx_ref, jnp.int32(l + 1))[:, :W]
            below = dif_ref[l] * wet * below_wet
        c = adv_ref[l]
        out = c
        if l + 1 < NL:
            out = out + below * (adv_ref[l + 1] - c)
        if l:
            out = out - above * (c - adv_ref[l - 1])
        mix_ref[l] = out
        above, wet = below, below_wet


def split_absorb(ids_ref, mix_ref, parts):
    y = ids_ref[0] & 3
    for k, ref in enumerate(parts):
        j = (y + k) & 3
        ref[...] = mix_ref[pl.ds(2 * j, 2)]


def next_currents(u, v, ux, uy, vx, vy, east_open, north_open, coriolis):
    lap_u = (rx(ux, -1) + rx(ux, 1))[:, :W] + (ry(uy, -1) + ry(uy, 1))[:R] - 4.0 * u
    lap_v = (rx(vx, -1) + rx(vx, 1))[:, :W] + (ry(vy, -1) + ry(vy, 1))[:R] - 4.0 * v
    return (
        east_open * (u + coriolis * v + 0.2 * lap_u),
        north_open * (v - coriolis * u + 0.2 * lap_v),
    )


def coriolis_of(ids_ref):
    row = ids_ref[2] * R + lax.broadcasted_iota(jnp.int32, (R, W), 0)
    rows = (ids_ref[3] * R).astype(f32)
    return 0.1 + 0.1 * row.astype(f32) / rows


def with_y(ref, main, hi, lo):
    ref[0:R, :] = main
    ref[R : R + 1, :] = hi
    ref[R + HY - 1 : R + HY, :] = lo
    return ref[...]


def open_x(wx):
    return wx * rx(wx, -1)


def open_y(wy):
    return wy * ry(wy, -1)


EDGE = 2 * R + 4


def plankton_one(
    ids_ref, c_ref, g0, g1, g2, g3, xh_ref, los_ref, his_ref, dif_ref, sea_ref, floor_ref, mix_ref,
    a0, a1, a2, a3, g_ref, gx_ref, east_ref, north_ref, wx_ref, wy_ref, cy_ref, adv_ref, vy_ref,
):
    y = ids_ref[0] & 3
    z = ids_ref[0] >> 2
    for k, ref in enumerate((g0, g1, g2, g3)):
        for zz in range(2):
            g_ref[((z + zz) & 1) * 4 + ((y + 4 - k) & 3)] = ref[zz]
    wet_setup(xh_ref, los_ref, his_ref, sea_ref, floor_ref, wx_ref, wy_ref)
    cols = jnp.concatenate([g_ref[l, 2 * R : 2 * R + 8, :] for l in range(NL)], 0)
    gx_ref[...] = jnp.concatenate([cols, jnp.zeros_like(cols)], 0).T[:R, :]

    def level(l, carry):
        u = g_ref[l, 0:R, :]
        v = g_ref[l, R : 2 * R, :]
        ux = jnp.concatenate([u, aside(gx_ref[...], lax.rem(W + 127 - 8 * l, W))], 1)
        vy = with_y(vy_ref.at[l], v, g_ref[l, EDGE + 3 : EDGE + 4, :], g_ref[l, EDGE + 1 : EDGE + 2, :])
        wx = wet_of(wx_ref, l)
        east = open_x(wx) * ux
        north = open_y(wet_of(wy_ref, l)) * vy
        east_ref[l] = east
        north_ref[l] = north
        adv_ref[l] = advect_level(
            1, l, c_ref[1, l], xh_ref, los_ref, his_ref, east, north, wx[:, :W], cy_ref
        )
        return carry

    lax.fori_loop(0, NL, level, 0, unroll=UNROLL)
    mix(adv_ref, dif_ref, wx_ref, mix_ref)
    split_absorb(ids_ref, mix_ref, (a0, a1, a2, a3))


def plankton_two(
    ids_ref, c_ref, cur_ref, left_ref, right_ref, lo_ref, hi_ref, dif_ref, wx_ref, wy_ref, mix_ref,
    a0, a1, a2, a3, xh_ref, los_ref, his_ref, east_ref, north_ref, cy_ref, adv_ref, vy_ref,
):
    xh_ref[...] = join_x(ids_ref, left_ref[...], right_ref[...], 104)
    edges_y(ids_ref, lo_ref, hi_ref, los_ref, his_ref)

    def level(l, carry):
        ux = jnp.concatenate([cur_ref[0, l], aside(xh_ref[...], 31 - l)], 1)
        vlow = los_ref[pl.ds(48 + l, 1), :]
        vy = with_y(vy_ref.at[l], cur_ref[1, l], vlow, vlow)
        wx = wet_of(wx_ref, l)
        east = open_x(wx) * ux
        north = open_y(wet_of(wy_ref, l)) * vy
        east_ref[l] = east
        north_ref[l] = north
        adv_ref[l] = advect_level(
            1, l, c_ref[l], xh_ref, los_ref, his_ref, east, north, wx[:, :W], cy_ref
        )
        return carry

    lax.fori_loop(0, NL, level, 0, unroll=UNROLL)
    mix(adv_ref, dif_ref, wx_ref, mix_ref)
    split_absorb(ids_ref, mix_ref, (a0, a1, a2, a3))


def other_tracer(t):
    def body(
        c_ref, xh_ref, los_ref, his_ref, east_ref, north_ref, dif_ref, wx_ref, mix_ref, cy_ref,
        adv_ref,
    ):
        c_ref = c_ref.at[t] if len(c_ref.shape) == 4 else c_ref

        def level(l, carry):
            adv_ref[l] = advect_level(
                t, l, c_ref[l], xh_ref, los_ref, his_ref, east_ref[l], north_ref[l],
                wet_of(wx_ref, l)[:, :W], cy_ref,
            )
            return carry

        lax.fori_loop(0, NL, level, 0, unroll=UNROLL)
        mix(adv_ref, dif_ref, wx_ref, mix_ref)

    return body


def rest_one(
    ids_ref, rate_ref, g_ref, gx_ref, east_ref, north_ref, wx_ref, wy_ref, temp_ref, xh_ref, los_ref, his_ref,
    solar_ref, cur_ref, tadv_ref, sun_ref, pace_ref, ty_ref,
):
    sun_ref[...] = solar_ref[...]
    for t in range(NT):
        pace_ref[t] = jnp.full((8, W), rate_ref[t], f32)
    coriolis = coriolis_of(ids_ref)

    def level(l, carry):
        u = g_ref[l, 0:R, :]
        v = g_ref[l, R : 2 * R, :]
        ux = jnp.concatenate([u, aside(gx_ref[...], lax.rem(W + 127 - 8 * l, W))], 1)
        vx = jnp.concatenate([v, aside(gx_ref[...], lax.rem(W + 125 - 8 * l, W))], 1)
        uy = with_y(
            ty_ref.at[l, 0], u, g_ref[l, EDGE + 2 : EDGE + 3, :], g_ref[l, EDGE : EDGE + 1, :]
        )
        vy = with_y(
            ty_ref.at[l, 1], v, g_ref[l, EDGE + 3 : EDGE + 4, :], g_ref[l, EDGE + 1 : EDGE + 2, :]
        )
        new_u, new_v = next_currents(
            u, v, ux, uy, vx, vy, open_x(wet_of(wx_ref, l))[:, :W], open_y(wet_of(wy_ref, l))[:R],
            coriolis,
        )
        cur_ref[0, l] = new_u
        cur_ref[1, l] = new_v
        return carry

    lax.fori_loop(0, NL, level, 0, unroll=UNROLL)
    own = ids_ref[0]
    temp = temp_ref[0]
    tx = jnp.concatenate([temp, aside(xh_ref[...], 127 - 104)], 1)
    ty = with_y(ty_ref.at[0, 0], temp, his_ref[52:53, :], los_ref[52:53, :])
    tadv_ref[...] = (
        temp - upwind(tx, east_ref[own], rx)[:, :W] - upwind(ty, north_ref[own], ry)[:R]
    )


def rest_two(
    ids_ref, cur_ref, east_ref, north_ref, wx_ref, wy_ref, temp_ref, xh_ref, los_ref, his_ref,
    out_ref, tadv_ref, ty_ref,
):
    own = ids_ref[0]
    temp = temp_ref[...]
    tx = jnp.concatenate([temp, aside(xh_ref[...], 127 - 108)], 1)
    ty = with_y(ty_ref.at[0, 0], temp, his_ref[58:59, :], los_ref[58:59, :])
    tadv_ref[...] = (
        temp - upwind(tx, east_ref[own], rx)[:, :W] - upwind(ty, north_ref[own], ry)[:R]
    )
    u = cur_ref[0, own]
    v = cur_ref[1, own]
    ux = jnp.concatenate([u, aside(xh_ref[...], 127 - 104)], 1)
    vx = jnp.concatenate([v, aside(xh_ref[...], 127 - 106)], 1)
    uy = with_y(ty_ref.at[1, 0], u, his_ref[56:57, :], los_ref[56:57, :])
    vy = with_y(ty_ref.at[1, 1], v, his_ref[57:58, :], los_ref[57:58, :])
    new_u, new_v = next_currents(
        u, v, ux, uy, vx, vy, open_x(wet_of(wx_ref, own))[:, :W], open_y(wet_of(wy_ref, own))[:R],
        coriolis_of(ids_ref),
    )
    out_ref[0, 0] = new_u
    out_ref[1, 0] = new_v


def biology(
    ids_ref, rate_ref, mixes, parts, solar_ref, wx_ref, tadv_ref, outs, sum_ref, tau_ref
):
    y = ids_ref[0] & 3
    for k, ref in enumerate(parts):
        sum_ref[pl.ds(2 * ((y + 4 - k) & 3), 2)] = ref[...]
    solar = solar_ref[...]
    sea = wx_ref[0, :, :W]
    depth = wx_ref[1, :, :W]
    mu, mortal, recycle = (rate_ref[t, 0:1, :] for t in range(NT))

    def level(l, tau):
        a = 0.04 + 0.03 * sum_ref[l]
        light = solar * jnp.exp(-tau - 0.5 * a)
        tau_ref[l] = tau
        wet = jnp.where(l.astype(f32) < depth, sea, 0.0)
        n, p, d = mixes[0][l], mixes[1][l], mixes[2][l]
        uptake = mu * (light / (light + 0.3)) * p * n / (jnp.abs(n) + 0.5)
        dead = mortal * p
        back = recycle * d
        outs[0][l] = wet * (n - uptake + back)
        outs[1][l] = wet * (p + uptake - dead)
        outs[2][l] = wet * (d + dead - back)
        return tau + a

    lax.fori_loop(0, NL, level, jnp.zeros((R, W), f32), unroll=2)
    own = ids_ref[0]
    tau = tau_ref[own]
    a = 0.04 + 0.03 * sum_ref[own]
    heat = 0.5 * solar * (jnp.exp(-tau) - jnp.exp(-tau - a))
    wet = jnp.where(own.astype(f32) < depth, sea, 0.0)
    return wet * (tadv_ref[...] + heat)


def biology_pack(
    ids_ref, rate_ref, n_ref, p_ref, d_ref, t0, t1, t2, t3, solar_ref, wx_ref, tadv_ref,
    cur_ref, n_out, p_out, d_out, temp_ref, px_ref, pyu_ref, pyd_ref, sum_ref, tau_ref,
):
    outs = (n_out, p_out, d_out)
    temp = biology(
        ids_ref, rate_ref, (n_ref, p_ref, d_ref), (t0, t1, t2, t3), solar_ref, wx_ref, tadv_ref,
        outs, sum_ref, tau_ref,
    )
    temp_ref[...] = temp
    px_ref[...] = jnp.zeros_like(px_ref)
    pyu_ref[...] = jnp.zeros_like(pyu_ref)
    pyd_ref[...] = jnp.zeros_like(pyd_ref)
    pack_tracers(outs, px_ref, pyu_ref, pyd_ref)
    acc = px_ref[...]
    at = lanes(acc.shape)
    for l in range(NL):
        acc = jnp.where(at == 96 + l, pltpu.roll(cur_ref[0, l], 97 + l, 1), acc)
        pyu_ref[48 + l : 49 + l, :] = cur_ref[1, l, R - 1 : R, :]
    own = ids_ref[0]
    for j, value in enumerate((cur_ref[0, own], cur_ref[1, own], temp)):
        acc = put_x(acc, value, 104 + 2 * j, 2)
        pack_rows(value, 56 + j, pyu_ref, pyd_ref)
    px_ref[...] = acc


def biology_last(
    ids_ref, rate_ref, n_ref, p_ref, d_ref, t0, t1, t2, t3, solar_ref, wx_ref, tadv_ref,
    c_ref, temp_ref, sum_ref, tau_ref,
):
    temp_ref[0] = biology(
        ids_ref, rate_ref, (n_ref, p_ref, d_ref), (t0, t1, t2, t3), solar_ref, wx_ref, tadv_ref,
        [c_ref.at[t] for t in range(NT)], sum_ref, tau_ref,
    )


def ring_x(value):
    n, m = lax.axis_size("gx"), lax.axis_size("tracer")
    ahead = [
        (g * m + t, (g + 1) * m + t if g + 1 < n else t ^ (m // 2))
        for g in range(n)
        for t in range(m)
    ]
    back = [(b, a) for a, b in ahead]
    axes = ("gx", "tracer")
    return lax.ppermute(value, axes, ahead), lax.ppermute(value, axes, back)


def ring_y(up, down):
    n = lax.axis_size("gy")
    ahead = [(i, (i + 1) % n) for i in range(n)]
    back = [(b, a) for a, b in ahead]
    return lax.ppermute(up, "gy", ahead), lax.ppermute(down, "gy", back)


def by_y(k):
    return [(z * 4 + y, z * 4 + (y + k) % 4) for z in range(2) for y in range(4)]


def over_z(value):
    return lax.ppermute(value, "tracer", [(i, i ^ 4) for i in range(8)])


def spread_y(value):
    return [value] + [lax.ppermute(value, "tracer", by_y(k)) for k in (1, 2, 3)]


def add_parts(*refs):
    ins, out = refs[:-2], refs[-1]
    acc = ins[0][...] + ins[1][...]
    if len(ins) > 2:
        acc = acc + (ins[2][...] + ins[3][...])
    out[...] = acc


def total(parts, during_y, during_z):
    got = [parts[0]] + [lax.ppermute(parts[k], "tracer", by_y(k)) for k in (1, 2, 3)]
    part = parts[0].shape
    (mine,) = call(add_parts, "add_y", [part], 0, n_any=1)(*got, during_y)
    away = over_z(mine)
    (full,) = call(add_parts, "add_z", [part], 0, n_any=1)(mine, away, during_z)
    return spread_y(full)


def per_device(c, flow, temp, dif, solar, rates, sea, floor):
    ids = jnp.stack(
        [
            lax.axis_index("tracer"),
            lax.axis_index("gx"),
            lax.axis_index("gy"),
            jnp.int32(lax.axis_size("gy")),
            jnp.int32(lax.axis_size("gx")),
        ]
    )
    tile = (R, W)
    col = (NL, R, W)
    part = (2, R, W)
    wide = (NL, R, 2 * W)
    tall = (NL, R + HY, W)
    wets = [(2, R, 2 * W), (2, R + HY, W)]
    two = (NL, 2, R + HY, W)
    other = over_z(flow)
    px, pyu, pyd = call(
        first_pack, "pack_one", [tile, tile, tile], 0,
        [(NT, NL, R, W), (2, 1, R, W), (1, R, W), pltpu.VMEM(tile, jnp.int32),
         pltpu.VMEM(tile, jnp.int32)],
        n_any=5, sems=5,
    )(c, flow, temp, sea, floor)
    px, pyu, pyd = call(pack_other, "pack_two", [tile, tile, tile], 0)(other, px, pyu, pyd)
    left, right = ring_x(px)
    lo, hi = ring_y(pyu, pyd)
    ext, xh, los, his = call(extend_flow, "extend", [(2, 2 * R + 8, W), tile, tile, tile], 1)(
        ids, flow, other, left, right, lo, hi
    )
    gathered = spread_y(ext)
    plank, a0, a1, a2, a3, g, gcol, east, north, wx, wy = call(
        plankton_one, "plankton_one",
        [col, part, part, part, part, (NL, 2 * R + 8, W), tile, wide, tall] + wets, 1,
        [tall, col, tall],
    )(ids, c, *gathered, xh, los, his, dif, sea, floor)
    nutri, detri = (
        call(other_tracer(t), "other_one", [col], 0, [tall, col])(
            c, xh, los, his, east, north, dif, wx
        )[0]
        for t in (0, 2)
    )
    cur, tadv, sun, pace = call(
        rest_one, "rest_one", [(2, NL, R, W), tile, tile, (NT, 8, W)], 2, [two]
    )(
        ids, rates, g, gcol, east, north, wx, wy, temp, xh, los, his, solar
    )
    sums = total((a0, a1, a2, a3), nutri, detri)
    n, p, d, heated, px, pyu, pyd = call(
        biology_pack, "biology_one", [col, col, col, tile, tile, tile, tile], 1, [col, col]
    )(ids, pace, nutri, plank, detri, *sums, sun, wx, tadv, cur)
    left, right = ring_x(px)
    lo, hi = ring_y(pyu, pyd)
    plank, a0, a1, a2, a3, xh, los, his, east, north = call(
        plankton_two, "plankton_two",
        [col, part, part, part, part, tile, tile, tile, wide, tall], 1,
        [tall, col, tall],
    )(ids, p, cur, left, right, lo, hi, dif, wx, wy)
    nutri, detri = (
        call(other_tracer(t), "other_two", [col], 0, [tall, col])(
            q, xh, los, his, east, north, dif, wx
        )[0]
        for t, q in ((0, n), (2, d))
    )
    currents, tadv = call(rest_two, "rest_two", [(2, 1, R, W), tile], 1, [two])(
        ids, cur, east, north, wx, wy, heated, xh, los, his
    )
    sums = total((a0, a1, a2, a3), nutri, detri)
    c, last_temp = call(
        biology_last, "biology_two", [(NT, NL, R, W), (1, R, W)], 1, [col, col]
    )(ids, pace, nutri, plank, detri, *sums, sun, wx, tadv)
    return c, currents, last_temp


def solution(mesh):
    in_specs = (
        P("tracer", None, "gy", "gx"),
        P(None, "tracer", "gy", "gx"),
        P("tracer", "gy", "gx"),
        P(None, "gy", "gx"),
        P("gy", "gx"),
        P("tracer"),
        P("gy", "gx"),
        P("gy", "gx"),
    )
    out_specs = (
        P("tracer", None, "gy", "gx"),
        P(None, "tracer", "gy", "gx"),
        P("tracer", "gy", "gx"),
    )
    return jax.shard_map(
        per_device, mesh=mesh, in_specs=in_specs, out_specs=out_specs, check_vma=False
    )
```

time: 113 us -> 99.8 us (0.88)
  starting transfers between devices: 50.5 us -> 39.8 us
  waiting for transfers between devices: 38.5 us -> 34.8 us
    ppermute x4, starting transfers between devices: 10.9 us -> 4.05 us  [ring_x(): return (lax.ppermute(value, axes, ahead), lax.ppermute(value, axes, back))]
    ppermute x4, waiting for transfers between devices: 1.89 us -> 8.55 us  [ring_x(): return (lax.ppermute(value, axes, ahead), lax.ppermute(value, axes, back))]
    ppermute x9, waiting for transfers between devices: 19.7 us -> 13.6 us  [spread_y(): return [value] + [lax.ppermute(value, 'tracer', by_y(k)) for k in (1, 2, 3)]]
    ppermute x3, starting transfers between devices: 17.1 us -> 13 us  [over_z(): return lax.ppermute(value, 'tracer', [(i, i ^ 4) for i in range(8)])]
    ppermute x6, waiting for transfers between devices: 7.02 us -> 4.39 us  [total(): lax.ppermute(parts[k], 'tracer', by_y(k))]
    ppermute x4, waiting for transfers between devices: 1.52 us -> 0.01 us  [ring_y(): return (lax.ppermute(up, 'gy', ahead), lax.ppermute(down, 'gy', back))]
    pallas_call x6 -> x17, Pallas kernels: 17.5 us -> 17.8 us  [run(): pl.pallas_call(body, name=name, out_shape=[jax.ShapeDtypeStruct(s, f32) f...]
  transfers between devices with their start and end apart: 26 -> 26, of which waited for: 18 -> 18; matrix products, arithmetic and copies ran while one was open for 0% -> 0% of each run, Pallas kernels for 0% -> 9%
where the time goes in v2:
time: 99.8 us; the launch traced here: 98.3 us
  starting transfers between devices  39.8 us (40%)
  waiting for transfers between devices  34.8 us (35%)
  Pallas kernels  17.8 us (18%)
  local copies, waits for them, and re-layouts  5 us (5%)
    pallas_call x17, Pallas kernels, run(): pl.pallas_call(body, name=name, out_shape=[jax.ShapeDtypeStruct(s, f32) f...  17.8 us
    ppermute x9, waiting for transfers between devices, spread_y(): return [value] + [lax.ppermute(value, 'tracer', by_y(k)) for k in (1, 2, 3)]  13.6 us
    ppermute x3, starting transfers between devices, over_z(): return lax.ppermute(value, 'tracer', [(i, i ^ 4) for i in range(8)])  13 us
    ppermute x9, starting transfers between devices, spread_y(): return [value] + [lax.ppermute(value, 'tracer', by_y(k)) for k in (1, 2, 3)]  11.9 us
    ppermute x4, waiting for transfers between devices, ring_x(): return (lax.ppermute(value, axes, ahead), lax.ppermute(value, axes, back))  8.55 us
    ppermute x3, waiting for transfers between devices, over_z(): return lax.ppermute(value, 'tracer', [(i, i ^ 4) for i in range(8)])  8.3 us
    ppermute x6, starting transfers between devices, total(): lax.ppermute(parts[k], 'tracer', by_y(k))  7.36 us
    unnamed x26, local copies, waits for them, and re-layouts  4.92 us
  transfers between devices with their start and end apart: 26, of which 18 were waited for; matrix products, arithmetic and copies ran while one was open for 0% of the time, Pallas kernels for 9%

profile of v2, /device:TPU:2, one launch (start us, length us, event | category | flops | bytes accessed | tf_op | source)
XLA Modules:
  0.0 98.3 jit_solution(4406666547892607955)
XLA Ops:
  0.6 7.3 %collective-permute-start = (f32[2,1,64,128]{3,2,1,0:T(8,128)}, f32[2,1,64,128]{3,2,1,0:T(8,128)S(1)}, u32[]{:S(2)}, u32[]{:S(2)}) collective-permute-start(f32[2,1,64,128]{3,2,1,0:T(8,128)} %flow_ref.1), channel_id=1, source_target_pairs={{0,4},{1,5},{2,6},{3,7},{4,0},{5,1},{6,2},{7,3},{8,12},{9,13},{10,... | collective-permute-start | bytes 196616 | tf_op jit(solution)/shard_map/ppermute | solution.py:496
  7.9 1.1 %copy-done = f32[3,8,64,128]{3,2,1,0:T(8,128)S(1)} copy-done((f32[3,8,64,128]{3,2,1,0:T(8,128)S(1)}, f32[3,8,64,128]{3,2,1,0:T(8,128)}, u32[]{:S(2)}) %copy-start) | copy-done | bytes 786456
  9.0 0.8 copy-done.3
  9.9 0.8 copy-done.5
  10.6 0.8 copy-done.7
  11.4 0.8 copy-done.9
  12.2 0.9 pack_one.1
  13.1 0.1 pack_two.1
  13.2 0.0 collective-permute-start.3
  13.2 1.7 %collective-permute-start.4 = (f32[64,128]{1,0:T(8,128)S(1)}, f32[64,128]{1,0:T(8,128)S(1)}, u32[]{:S(2)}, u32[]{:S(2)}) collective-permute-start(f32[64,128]{1,0:T(8,128)S(1)} %get-tuple-element.54), channel_id=1, source_target_pairs={{8,0},{16,8},{24,16},{32,24},{40,32},{48,40},{56,48},{0,56},{9,1},... | collective-permute-start | bytes 98312 | tf_op jit(solution)/shard_map/ppermute | solution.py:488
  14.9 1.9 %collective-permute-start.2 = (f32[64,128]{1,0:T(8,128)S(1)}, f32[64,128]{1,0:T(8,128)S(1)}, u32[]{:S(2)}, u32[]{:S(2)}) collective-permute-start(f32[64,128]{1,0:T(8,128)S(1)} %get-tuple-element.52), channel_id=1, source_target_pairs={{64,0},{65,1},{66,2},{67,3},{68,4},{69,5},{70,6},{71,7},{128,64},{... | collective-permute-start | bytes 98312 | tf_op jit(solution)/shard_map/ppermute | solution.py:481
  16.8 0.1 collective-permute-start.1
  17.0 0.1 stack.15.ids_ref
  17.1 1.8 %collective-permute-done.2.right_ref = f32[64,128]{1,0:T(8,128)S(1)} collective-permute-done((f32[64,128]{1,0:T(8,128)S(1)}, f32[64,128]{1,0:T(8,128)S(1)}, u32[]{:S(2)}, u32[]{:S(2)}) %collective-permute-start.2) | collective-permute-done | bytes 32800 | tf_op jit(solution)/shard_map/ppermute | solution.py:481
  18.9 3.1 %collective-permute-done.1.left_ref = f32[64,128]{1,0:T(8,128)S(1)} collective-permute-done((f32[64,128]{1,0:T(8,128)S(1)}, f32[64,128]{1,0:T(8,128)S(1)}, u32[]{:S(2)}, u32[]{:S(2)}) %collective-permute-start.1) | collective-permute-done | bytes 32800 | tf_op jit(solution)/shard_map/ppermute | solution.py:481
  22.0 0.6 extend.1
  22.5 3.1 %collective-permute-start.7 = (f32[2,136,128]{2,1,0:T(8,128)S(1)}, f32[2,136,128]{2,1,0:T(8,128)S(1)}, u32[]{:S(2)}, u32[]{:S(2)}) collective-permute-start(f32[2,136,128]{2,1,0:T(8,128)S(1)} %get-tuple-element.55.g0), channel_id=1, source_target_pairs={{0,3},{1,0},{2,1},{3,2},{4,7},{5,4},{6,5},{7,6},{8,11},{9,8},{10,9... | collective-permute-start | bytes 417800 | tf_op jit(solution)/shard_map/ppermute | solution.py:500
  25.6 0.6 collective-permute-start.6
  26.3 1.0 collective-permute-start.5
  27.2 3.0 %collective-permute-done.7.g3 = f32[2,136,128]{2,1,0:T(8,128)S(1)} collective-permute-done((f32[2,136,128]{2,1,0:T(8,128)S(1)}, f32[2,136,128]{2,1,0:T(8,128)S(1)}, u32[]{:S(2)}, u32[]{:S(2)}) %collective-permute-start.7) | collective-permute-done | bytes 139296 | tf_op jit(solution)/shard_map/ppermute | solution.py:500
  30.2 2.2 %collective-permute-done.6.g2 = f32[2,136,128]{2,1,0:T(8,128)S(1)} collective-permute-done((f32[2,136,128]{2,1,0:T(8,128)S(1)}, f32[2,136,128]{2,1,0:T(8,128)S(1)}, u32[]{:S(2)}, u32[]{:S(2)}) %collective-permute-start.6) | collective-permute-done | bytes 139296 | tf_op jit(solution)/shard_map/ppermute | solution.py:500
  32.5 1.4 %collective-permute-done.5.g1 = f32[2,136,128]{2,1,0:T(8,128)S(1)} collective-permute-done((f32[2,136,128]{2,1,0:T(8,128)S(1)}, f32[2,136,128]{2,1,0:T(8,128)S(1)}, u32[]{:S(2)}, u32[]{:S(2)}) %collective-permute-start.5) | collective-permute-done | bytes 139296 | tf_op jit(solution)/shard_map/ppermute | solution.py:500
  33.9 2.4 %plankton_one.1 = (f32[8,64,128]{2,1,0:T(8,128)S(1)}, f32[2,64,128]{2,1,0:T(8,128)S(1)}, f32[2,64,128]{2,1,0:T(8,128)S(1)}, f32[2,64,128]{2,1,0:T(8,128)S(1)}, f...) custom-call(s32[5]{0:T(128)S(1)} %stack.15.ids_ref, ...), custom_call_target="tpu_custom_call" | custom-call | tf_op jit(solution)/shard_map/plankton_one/pallas_call | solution.py:24
  36.3 0.1 collective-permute-start.8
  36.4 2.0 %collective-permute-start.9 = (f32[2,64,128]{2,1,0:T(8,128)S(1)}, f32[2,64,128]{2,1,0:T(8,128)S(1)}, u32[]{:S(2)}, u32[]{:S(2)}) collective-permute-start(f32[2,64,128]{2,1,0:T(8,128)S(1)} %get-tuple-element.69), channel_id=1, source_target_pairs={{0,2},{1,3},{2,0},{3,1},{4,6},{5,7},{6,4},{7,5},{8,10},{9,11},{10,... | collective-permute-start | bytes 196616 | tf_op jit(solution)/shard_map/ppermute | solution.py:512
  38.4 1.2 %collective-permute-start.10 = (f32[2,64,128]{2,1,0:T(8,128)S(1)}, f32[2,64,128]{2,1,0:T(8,128)S(1)}, u32[]{:S(2)}, u32[]{:S(2)}) collective-permute-start(f32[2,64,128]{2,1,0:T(8,128)S(1)} %get-tuple-element.70), channel_id=1, source_target_pairs={{0,3},{1,0},{2,1},{3,2},{4,7},{5,4},{6,5},{7,6},{8,11},{9,8},{10,9... | collective-permute-start | bytes 196616 | tf_op jit(solution)/shard_map/ppermute | solution.py:512
  39.6 1.2 %other_one.2.refs_4_.n_ref = f32[8,64,128]{2,1,0:T(8,128)S(1)} custom-call(f32[3,8,64,128]{3,2,1,0:T(8,128)S(1)} %copy-done.1, f32[64,128]{1,0:T(8,128)S(1)} %get-tuple-element.56.xh_ref, f32[64,128]{1,0:T(8,128)S(1)} %get-tuple-element.57.los_ref, f32[64,128]{1,0:T(8,128)S(1)} %get-tuple-element.58.his_ref, f32[8,64,256]{2,1,0:T(8,128)S(1)} %get-tuple-element.61.east_ref, ...), custom_call_target="tpu_custom_call" | custom-call | tf_op jit(solution)/shard_map/other_one/pallas_call | solution.py:24
  40.9 1.7 %collective-permute-done.8.refs_1_ = f32[2,64,128]{2,1,0:T(8,128)S(1)} collective-permute-done((f32[2,64,128]{2,1,0:T(8,128)S(1)}, f32[2,64,128]{2,1,0:T(8,128)S(1)}, u32[]{:S(2)}, u32[]{:S(2)}) %collective-permute-start.8) | collective-permute-done | bytes 65568 | tf_op jit(solution)/shard_map/ppermute | solution.py:512
  42.6 0.9 collective-permute-done.10.refs_3_
  43.4 2.8 %collective-permute-start.11 = (f32[2,64,128]{2,1,0:T(8,128)S(1)}, f32[2,64,128]{2,1,0:T(8,128)S(1)}, u32[]{:S(2)}, u32[]{:S(2)}) collective-permute-start(f32[2,64,128]{2,1,0:T(8,128)S(1)} %add_y.2.refs_0_), channel_id=1, source_target_pairs={{0,4},{1,5},{2,6},{3,7},{4,0},{5,1},{6,2},{7,3},{8,12},{9,13},{10,... | collective-permute-start | bytes 196616 | tf_op jit(solution)/shard_map/ppermute | solution.py:496
  46.2 1.2 %other_one.3.refs_2_.d_ref = f32[8,64,128]{2,1,0:T(8,128)S(1)} custom-call(f32[3,8,64,128]{3,2,1,0:T(8,128)S(1)} %copy-done.1, f32[64,128]{1,0:T(8,128)S(1)} %get-tuple-element.56.xh_ref, f32[64,128]{1,0:T(8,128)S(1)} %get-tuple-element.57.los_ref, f32[64,128]{1,0:T(8,128)S(1)} %get-tuple-element.58.his_ref, f32[8,64,256]{2,1,0:T(8,128)S(1)} %get-tuple-element.61.east_ref, ...), custom_call_target="tpu_custom_call" | custom-call | tf_op jit(solution)/shard_map/other_one/pallas_call | solution.py:24
  47.5 0.0 copy-start.11
  47.5 4.2 %collective-permute-done.11.refs_1_ = f32[2,64,128]{2,1,0:T(8,128)S(1)} collective-permute-done((f32[2,64,128]{2,1,0:T(8,128)S(1)}, f32[2,64,128]{2,1,0:T(8,128)S(1)}, u32[]{:S(2)}, u32[]{:S(2)}) %collective-permute-start.11) | collective-permute-done | bytes 65568 | tf_op jit(solution)/shard_map/ppermute | solution.py:496
  51.7 2.5 %collective-permute-start.14 = (f32[2,64,128]{2,1,0:T(8,128)S(1)}, f32[2,64,128]{2,1,0:T(8,128)S(1)}, u32[]{:S(2)}, u32[]{:S(2)}) collective-permute-start(f32[2,64,128]{2,1,0:T(8,128)S(1)} %add_z.2.t0), channel_id=1, source_target_pairs={{0,3},{1,0},{2,1},{3,2},{4,7},{5,4},{6,5},{7,6},{8,11},{9,8},{10,9... | collective-permute-start | bytes 196616 | tf_op jit(solution)/shard_map/ppermute | solution.py:500
  54.2 1.0 %collective-permute-start.13 = (f32[2,64,128]{2,1,0:T(8,128)S(1)}, f32[2,64,128]{2,1,0:T(8,128)S(1)}, u32[]{:S(2)}, u32[]{:S(2)}) collective-permute-start(f32[2,64,128]{2,1,0:T(8,128)S(1)} %add_z.2.t0), channel_id=1, source_target_pairs={{0,2},{1,3},{2,0},{3,1},{4,6},{5,7},{6,4},{7,5},{8,10},{9,11},{10,... | collective-permute-start | bytes 196616 | tf_op jit(solution)/shard_map/ppermute | solution.py:500
  55.2 0.6 copy-done.12
  55.8 2.0 %rest_one.1 = (f32[2,8,64,128]{3,2,1,0:T(8,128)S(1)}, f32[64,128]{1,0:T(8,128)S(1)}, f32[64,128]{1,0:T(8,128)S(1)}, f32[3,8,128]{2,1,0:T(8,128)S(1)}) custom-call(s32[5]{0:T(128)S(1)} %stack.15.ids_ref, f32[3]{0:T(128)S(1)} %copy-done.12, f32[8,136,128]{2,1,0:T(8,128)S(1)} %get-tuple-element.59.g_ref, f32[64,128]{1,0:T(8,128)S(1)} %get-tuple-element.60.gx_ref, ...), custom_call_target="tpu_custom_call" | custom-call | tf_op jit(solution)/shard_map/rest_one/pallas_call | solution.py:24
  57.8 2.1 %collective-permute-done.13.t2 = f32[2,64,128]{2,1,0:T(8,128)S(1)} collective-permute-done((f32[2,64,128]{2,1,0:T(8,128)S(1)}, f32[2,64,128]{2,1,0:T(8,128)S(1)}, u32[]{:S(2)}, u32[]{:S(2)}) %collective-permute-start.13) | collective-permute-done | bytes 65568 | tf_op jit(solution)/shard_map/ppermute | solution.py:500
  60.0 0.7 collective-permute-done.12.t1
  60.7 1.5 %biology_one.1 = (f32[8,64,128]{2,1,0:T(8,128)S(1)}, f32[8,64,128]{2,1,0:T(8,128)S(1)}, f32[8,64,128]{2,1,0:T(8,128)S(1)}, f32[64,128]{1,0:T(8,128)S(1)}, f32[64...) custom-call(s32[5]{0:T(128)S(1)} %stack.15.ids_ref, f32[3,8,128]{2,1,0:T(8,128)S(1)} %get-tuple-element.65.rate_ref, ...), custom_call_target="tpu_custom_call" | custom-call | tf_op jit(solution)/shard_map/biology_one/pallas_call | solution.py:24
  62.2 0.0 collective-permute-start.17
  62.2 1.7 %collective-permute-start.18 = (f32[64,128]{1,0:T(8,128)S(1)}, f32[64,128]{1,0:T(8,128)S(1)}, u32[]{:S(2)}, u32[]{:S(2)}) collective-permute-start(f32[64,128]{1,0:T(8,128)S(1)} %get-tuple-element.78), channel_id=1, source_target_pairs={{8,0},{16,8},{24,16},{32,24},{40,32},{48,40},{56,48},{0,56},{9,1},... | collective-permute-start | bytes 98312 | tf_op jit(solution)/shard_map/ppermute | solution.py:488
  63.9 0.6 collective-permute-start.16
  64.5 1.5 %collective-permute-start.15 = (f32[64,128]{1,0:T(8,128)S(1)}, f32[64,128]{1,0:T(8,128)S(1)}, u32[]{:S(2)}, u32[]{:S(2)}) collective-permute-start(f32[64,128]{1,0:T(8,128)S(1)} %get-tuple-element.76), channel_id=1, source_target_pairs={{0,64},{1,65},{2,66},{3,67},{4,68},{5,69},{6,70},{7,71},{64,128},{... | collective-permute-start | bytes 98312 | tf_op jit(solution)/shard_map/ppermute | solution.py:481
  66.0 1.9 %collective-permute-done.16.right_ref = f32[64,128]{1,0:T(8,128)S(1)} collective-permute-done((f32[64,128]{1,0:T(8,128)S(1)}, f32[64,128]{1,0:T(8,128)S(1)}, u32[]{:S(2)}, u32[]{:S(2)}) %collective-permute-start.16) | collective-permute-done | bytes 32800 | tf_op jit(solution)/shard_map/ppermute | solution.py:481
  67.9 1.8 %collective-permute-done.15.left_ref = f32[64,128]{1,0:T(8,128)S(1)} collective-permute-done((f32[64,128]{1,0:T(8,128)S(1)}, f32[64,128]{1,0:T(8,128)S(1)}, u32[]{:S(2)}, u32[]{:S(2)}) %collective-permute-start.15) | collective-permute-done | bytes 32800 | tf_op jit(solution)/shard_map/ppermute | solution.py:481
  69.6 2.2 %plankton_two.1 = (f32[8,64,128]{2,1,0:T(8,128)S(1)}, f32[2,64,128]{2,1,0:T(8,128)S(1)}, f32[2,64,128]{2,1,0:T(8,128)S(1)}, f32[2,64,128]{2,1,0:T(8,128)S(1)}, f...) custom-call(s32[5]{0:T(128)S(1)} %stack.15.ids_ref, ...), custom_call_target="tpu_custom_call" | custom-call | tf_op jit(solution)/shard_map/plankton_two/pallas_call | solution.py:24
  71.9 0.1 collective-permute-start.19
  72.0 2.0 %collective-permute-start.20 = (f32[2,64,128]{2,1,0:T(8,128)S(1)}, f32[2,64,128]{2,1,0:T(8,128)S(1)}, u32[]{:S(2)}, u32[]{:S(2)}) collective-permute-start(f32[2,64,128]{2,1,0:T(8,128)S(1)} %get-tuple-element.88), channel_id=1, source_target_pairs={{0,2},{1,3},{2,0},{3,1},{4,6},{5,7},{6,4},{7,5},{8,10},{9,11},{10,... | collective-permute-start | bytes 196616 | tf_op jit(solution)/shard_map/ppermute | solution.py:512
  74.0 1.9 %collective-permute-start.21 = (f32[2,64,128]{2,1,0:T(8,128)S(1)}, f32[2,64,128]{2,1,0:T(8,128)S(1)}, u32[]{:S(2)}, u32[]{:S(2)}) collective-permute-start(f32[2,64,128]{2,1,0:T(8,128)S(1)} %get-tuple-element.89), channel_id=1, source_target_pairs={{0,3},{1,0},{2,1},{3,2},{4,7},{5,4},{6,5},{7,6},{8,11},{9,8},{10,9... | collective-permute-start | bytes 196616 | tf_op jit(solution)/shard_map/ppermute | solution.py:512
  75.9 1.2 %other_two.2.refs_4_.n_ref = f32[8,64,128]{2,1,0:T(8,128)S(1)} custom-call(f32[8,64,128]{2,1,0:T(8,128)S(1)} %get-tuple-element.74.c_ref, f32[64,128]{1,0:T(8,128)S(1)} %get-tuple-element.79.xh_ref, f32[64,128]{1,0:T(8,128)S(1)} %get-tuple-element.80.los_ref, f32[64,128]{1,0:T(8,128)S(1)} %get-tuple-element.81.his_ref, ...), custom_call_target="tpu_custom_call" | custom-call | tf_op jit(solution)/shard_map/other_two/pallas_call | solution.py:24
  77.2 1.0 %collective-permute-done.19.refs_1_ = f32[2,64,128]{2,1,0:T(8,128)S(1)} collective-permute-done((f32[2,64,128]{2,1,0:T(8,128)S(1)}, f32[2,64,128]{2,1,0:T(8,128)S(1)}, u32[]{:S(2)}, u32[]{:S(2)}) %collective-permute-start.19) | collective-permute-done | bytes 65568 | tf_op jit(solution)/shard_map/ppermute | solution.py:512
  78.2 0.9 collective-permute-done.21.refs_3_
  79.0 2.9 %collective-permute-start.22 = (f32[2,64,128]{2,1,0:T(8,128)S(1)}, f32[2,64,128]{2,1,0:T(8,128)S(1)}, u32[]{:S(2)}, u32[]{:S(2)}) collective-permute-start(f32[2,64,128]{2,1,0:T(8,128)S(1)} %add_y.3.refs_0_), channel_id=1, source_target_pairs={{0,4},{1,5},{2,6},{3,7},{4,0},{5,1},{6,2},{7,3},{8,12},{9,13},{10,... | collective-permute-start | bytes 196616 | tf_op jit(solution)/shard_map/ppermute | solution.py:496
  82.0 1.2 %other_two.3.refs_2_.d_ref = f32[8,64,128]{2,1,0:T(8,128)S(1)} custom-call(f32[8,64,128]{2,1,0:T(8,128)S(1)} %get-tuple-element.85.c_ref, f32[64,128]{1,0:T(8,128)S(1)} %get-tuple-element.79.xh_ref, f32[64,128]{1,0:T(8,128)S(1)} %get-tuple-element.80.los_ref, f32[64,128]{1,0:T(8,128)S(1)} %get-tuple-element.81.his_ref, ...), custom_call_target="tpu_custom_call" | custom-call | tf_op jit(solution)/shard_map/other_two/pallas_call | solution.py:24
  83.2 4.1 %collective-permute-done.22.refs_1_ = f32[2,64,128]{2,1,0:T(8,128)S(1)} collective-permute-done((f32[2,64,128]{2,1,0:T(8,128)S(1)}, f32[2,64,128]{2,1,0:T(8,128)S(1)}, u32[]{:S(2)}, u32[]{:S(2)}) %collective-permute-start.22) | collective-permute-done | bytes 65568 | tf_op jit(solution)/shard_map/ppermute | solution.py:496
  87.3 2.8 %collective-permute-start.25 = (f32[2,64,128]{2,1,0:T(8,128)S(1)}, f32[2,64,128]{2,1,0:T(8,128)S(1)}, u32[]{:S(2)}, u32[]{:S(2)}) collective-permute-start(f32[2,64,128]{2,1,0:T(8,128)S(1)} %add_z.3.t0), channel_id=1, source_target_pairs={{0,3},{1,0},{2,1},{3,2},{4,7},{5,4},{6,5},{7,6},{8,11},{9,8},{10,9... | collective-permute-start | bytes 196616 | tf_op jit(solution)/shard_map/ppermute | solution.py:500
  90.1 0.7 collective-permute-start.24
  90.8 0.2 collective-permute-start.23
  91.0 1.4 %rest_two.1 = (f32[2,1,64,128]{3,2,1,0:T(8,128)}, f32[64,128]{1,0:T(8,128)S(1)}) custom-call(s32[5]{0:T(128)S(1)} %stack.15.ids_ref, f32[2,8,64,128]{3,2,1,0:T(8,128)S(1)} %get-tuple-element.73.cur_ref, f32[8,64,256]{2,1,0:T(8,128)S(1)} %get-tuple-element.82.east_ref, f32[8,80,128]{2,1,0:T(8,128)S(1)} %get-tuple-element.83.north_ref, ...), custom_call_target="tpu_custom_call" | custom-call | tf_op jit(solution)/shard_map/rest_two/pallas_call | solution.py:24
  92.4 0.2 collective-permute-done.25.t3
  92.6 3.3 %collective-permute-done.24.t2 = f32[2,64,128]{2,1,0:T(8,128)S(1)} collective-permute-done((f32[2,64,128]{2,1,0:T(8,128)S(1)}, f32[2,64,128]{2,1,0:T(8,128)S(1)}, u32[]{:S(2)}, u32[]{:S(2)}) %collective-permute-start.24) | collective-permute-done | bytes 65568 | tf_op jit(solution)/shard_map/ppermute | solution.py:500
  95.9 0.7 collective-permute-done.23.t1
  96.5 1.8 %biology_two.1 = (f32[3,8,64,128]{3,2,1,0:T(8,128)}, f32[1,64,128]{2,1,0:T(8,128)}) custom-call(s32[5]{0:T(128)S(1)} %stack.15.ids_ref, f32[3,8,128]{2,1,0:T(8,128)S(1)} %get-tuple-element.65.rate_ref, f32[8,64,128]{2,1,0:T(8,128)S(1)} %other_two.2.refs_4_.n_ref, f32[8,64,128]{2,1,0:T(8,128)S(1)} %get-tuple-element.84.p_ref, ...), custom_call_target="tpu_custom_call" | custom-call | tf_op jit(solution)/shard_map/biology_two/pallas_call | solution.py:24
  (32 shorter events, 0.1 us)
Async XLA Ops:
  0.6 12.5 %collective-permute-start = (f32[2,1,64,128]{3,2,1,0:T(8,128)}, f32[2,1,64,128]{3,2,1,0:T(8,128)S(1)}, u32[]{:S(2)}, u32[]{:S(2)}) collective-permute-start(f32[2,1,64,128]{3,2,1,0:T(8,128)} %flow_ref.1), channel_id=1, source_target_pairs={{0,4},{1,5},{2,6},{3,7},{4,0},{5,1},{6,2},{7,3},{8,12},{9,13},{10,... | collective-permute-start | bytes 196616 | tf_op jit(solution)/shard_map/ppermute | solution.py:496
  7.9 1.1 %copy-start = (f32[3,8,64,128]{3,2,1,0:T(8,128)S(1)}, f32[3,8,64,128]{3,2,1,0:T(8,128)}, u32[]{:S(2)}) copy-start(f32[3,8,64,128]{3,2,1,0:T(8,128)} %c_ref.5) | copy-start | bytes 2359300
  9.0 0.8 copy-start.3
  9.9 0.8 copy-start.5
  10.6 0.8 copy-start.7
  11.4 0.8 copy-start.9
  12.2 9.8 %copy-start.4 = (f32[2,1,64,128]{3,2,1,0:T(8,128)S(1)}, f32[2,1,64,128]{3,2,1,0:T(8,128)}, u32[]{:S(2)}) copy-start(f32[2,1,64,128]{3,2,1,0:T(8,128)} %flow_ref.1) | copy-start | bytes 196612
  12.2 21.7 %copy-start.1 = (f32[3,8,64,128]{3,2,1,0:T(8,128)S(1)}, f32[3,8,64,128]{3,2,1,0:T(8,128)}, u32[]{:S(2)}) copy-start(f32[3,8,64,128]{3,2,1,0:T(8,128)} %c_ref.5) | copy-start | bytes 2359300
  13.1 20.8 %copy-start.2 = (f32[8,64,128]{2,1,0:T(8,128)S(1)}, f32[8,64,128]{2,1,0:T(8,128)}, u32[]{:S(2)}) copy-start(f32[8,64,128]{2,1,0:T(8,128)} %dif_ref.11) | copy-start | bytes 786436
  13.2 3.9 %collective-permute-start.3 = (f32[64,128]{1,0:T(8,128)S(1)}, f32[64,128]{1,0:T(8,128)S(1)}, u32[]{:S(2)}, u32[]{:S(2)}) collective-permute-start(f32[64,128]{1,0:T(8,128)S(1)} %get-tuple-element.53), channel_id=1, source_target_pairs={{0,8},{8,16},{16,24},{24,32},{32,40},{40,48},{48,56},{56,0},{1,9},... | collective-permute-start | bytes 98312 | tf_op jit(solution)/shard_map/ppermute | solution.py:488
  13.2 3.9 %collective-permute-start.4 = (f32[64,128]{1,0:T(8,128)S(1)}, f32[64,128]{1,0:T(8,128)S(1)}, u32[]{:S(2)}, u32[]{:S(2)}) collective-permute-start(f32[64,128]{1,0:T(8,128)S(1)} %get-tuple-element.54), channel_id=1, source_target_pairs={{8,0},{16,8},{24,16},{32,24},{40,32},{48,40},{56,48},{0,56},{9,1},... | collective-permute-start | bytes 98312 | tf_op jit(solution)/shard_map/ppermute | solution.py:488
  14.9 3.9 %collective-permute-start.2 = (f32[64,128]{1,0:T(8,128)S(1)}, f32[64,128]{1,0:T(8,128)S(1)}, u32[]{:S(2)}, u32[]{:S(2)}) collective-permute-start(f32[64,128]{1,0:T(8,128)S(1)} %get-tuple-element.52), channel_id=1, source_target_pairs={{64,0},{65,1},{66,2},{67,3},{68,4},{69,5},{70,6},{71,7},{128,64},{... | collective-permute-start | bytes 98312 | tf_op jit(solution)/shard_map/ppermute | solution.py:481
  16.8 5.1 %collective-permute-start.1 = (f32[64,128]{1,0:T(8,128)S(1)}, f32[64,128]{1,0:T(8,128)S(1)}, u32[]{:S(2)}, u32[]{:S(2)}) collective-permute-start(f32[64,128]{1,0:T(8,128)S(1)} %get-tuple-element.52), channel_id=1, source_target_pairs={{0,64},{1,65},{2,66},{3,67},{4,68},{5,69},{6,70},{7,71},{64,128},{... | collective-permute-start | bytes 98312 | tf_op jit(solution)/shard_map/ppermute | solution.py:481
  17.1 16.8 %copy-start.8 = (s32[64,128]{1,0:T(8,128)S(1)}, s32[64,128]{1,0:T(8,128)}, u32[]{:S(2)}) copy-start(s32[64,128]{1,0:T(8,128)} %sea_ref.1) | copy-start | bytes 98308
  17.1 16.8 %copy-start.10 = (s32[64,128]{1,0:T(8,128)S(1)}, s32[64,128]{1,0:T(8,128)}, u32[]{:S(2)}) copy-start(s32[64,128]{1,0:T(8,128)} %floor_ref.1) | copy-start | bytes 98308
  22.5 7.7 %collective-permute-start.7 = (f32[2,136,128]{2,1,0:T(8,128)S(1)}, f32[2,136,128]{2,1,0:T(8,128)S(1)}, u32[]{:S(2)}, u32[]{:S(2)}) collective-permute-start(f32[2,136,128]{2,1,0:T(8,128)S(1)} %get-tuple-element.55.g0), channel_id=1, source_target_pairs={{0,3},{1,0},{2,1},{3,2},{4,7},{5,4},{6,5},{7,6},{8,11},{9,8},{10,9... | collective-permute-start | bytes 417800 | tf_op jit(solution)/shard_map/ppermute | solution.py:500
  25.6 6.8 %collective-permute-start.6 = (f32[2,136,128]{2,1,0:T(8,128)S(1)}, f32[2,136,128]{2,1,0:T(8,128)S(1)}, u32[]{:S(2)}, u32[]{:S(2)}) collective-permute-start(f32[2,136,128]{2,1,0:T(8,128)S(1)} %get-tuple-element.55.g0), channel_id=1, source_target_pairs={{0,2},{1,3},{2,0},{3,1},{4,6},{5,7},{6,4},{7,5},{8,10},{9,11},{10,... | collective-permute-start | bytes 417800 | tf_op jit(solution)/shard_map/ppermute | solution.py:500
  26.3 7.6 %collective-permute-start.5 = (f32[2,136,128]{2,1,0:T(8,128)S(1)}, f32[2,136,128]{2,1,0:T(8,128)S(1)}, u32[]{:S(2)}, u32[]{:S(2)}) collective-permute-start(f32[2,136,128]{2,1,0:T(8,128)S(1)} %get-tuple-element.55.g0), channel_id=1, source_target_pairs={{0,1},{1,2},{2,3},{3,0},{4,5},{5,6},{6,7},{7,4},{8,9},{9,10},{10,1... | collective-permute-start | bytes 417800 | tf_op jit(solution)/shard_map/ppermute | solution.py:500
  36.3 6.3 %collective-permute-start.8 = (f32[2,64,128]{2,1,0:T(8,128)S(1)}, f32[2,64,128]{2,1,0:T(8,128)S(1)}, u32[]{:S(2)}, u32[]{:S(2)}) collective-permute-start(f32[2,64,128]{2,1,0:T(8,128)S(1)} %get-tuple-element.68), channel_id=1, source_target_pairs={{0,1},{1,2},{2,3},{3,0},{4,5},{5,6},{6,7},{7,4},{8,9},{9,10},{10,1... | collective-permute-start | bytes 196616 | tf_op jit(solution)/shard_map/ppermute | solution.py:512
  36.4 6.2 %collective-permute-start.9 = (f32[2,64,128]{2,1,0:T(8,128)S(1)}, f32[2,64,128]{2,1,0:T(8,128)S(1)}, u32[]{:S(2)}, u32[]{:S(2)}) collective-permute-start(f32[2,64,128]{2,1,0:T(8,128)S(1)} %get-tuple-element.69), channel_id=1, source_target_pairs={{0,2},{1,3},{2,0},{3,1},{4,6},{5,7},{6,4},{7,5},{8,10},{9,11},{10,... | collective-permute-start | bytes 196616 | tf_op jit(solution)/shard_map/ppermute | solution.py:512
  38.4 5.0 %collective-permute-start.10 = (f32[2,64,128]{2,1,0:T(8,128)S(1)}, f32[2,64,128]{2,1,0:T(8,128)S(1)}, u32[]{:S(2)}, u32[]{:S(2)}) collective-permute-start(f32[2,64,128]{2,1,0:T(8,128)S(1)} %get-tuple-element.70), channel_id=1, source_target_pairs={{0,3},{1,0},{2,1},{3,2},{4,7},{5,4},{6,5},{7,6},{8,11},{9,8},{10,9... | collective-permute-start | bytes 196616 | tf_op jit(solution)/shard_map/ppermute | solution.py:512
  43.4 8.3 %collective-permute-start.11 = (f32[2,64,128]{2,1,0:T(8,128)S(1)}, f32[2,64,128]{2,1,0:T(8,128)S(1)}, u32[]{:S(2)}, u32[]{:S(2)}) collective-permute-start(f32[2,64,128]{2,1,0:T(8,128)S(1)} %add_y.2.refs_0_), channel_id=1, source_target_pairs={{0,4},{1,5},{2,6},{3,7},{4,0},{5,1},{6,2},{7,3},{8,12},{9,13},{10,... | collective-permute-start | bytes 196616 | tf_op jit(solution)/shard_map/ppermute | solution.py:496
  47.5 7.7 %copy-start.6 = (f32[1,64,128]{2,1,0:T(8,128)S(1)}, f32[1,64,128]{2,1,0:T(8,128)}, u32[]{:S(2)}) copy-start(f32[1,64,128]{2,1,0:T(8,128)} %temp_ref.1) | copy-start | bytes 98308
  47.5 7.7 %copy-start.11 = (f32[64,128]{1,0:T(8,128)S(1)}, f32[64,128]{1,0:T(8,128)}, u32[]{:S(2)}) copy-start(f32[64,128]{1,0:T(8,128)} %solar_ref.1) | copy-start | bytes 98308
  51.7 6.1 %collective-permute-start.14 = (f32[2,64,128]{2,1,0:T(8,128)S(1)}, f32[2,64,128]{2,1,0:T(8,128)S(1)}, u32[]{:S(2)}, u32[]{:S(2)}) collective-permute-start(f32[2,64,128]{2,1,0:T(8,128)S(1)} %add_z.2.t0), channel_id=1, source_target_pairs={{0,3},{1,0},{2,1},{3,2},{4,7},{5,4},{6,5},{7,6},{8,11},{9,8},{10,9... | collective-permute-start | bytes 196616 | tf_op jit(solution)/shard_map/ppermute | solution.py:500
  54.2 5.8 %collective-permute-start.13 = (f32[2,64,128]{2,1,0:T(8,128)S(1)}, f32[2,64,128]{2,1,0:T(8,128)S(1)}, u32[]{:S(2)}, u32[]{:S(2)}) collective-permute-start(f32[2,64,128]{2,1,0:T(8,128)S(1)} %add_z.2.t0), channel_id=1, source_target_pairs={{0,2},{1,3},{2,0},{3,1},{4,6},{5,7},{6,4},{7,5},{8,10},{9,11},{10,... | collective-permute-start | bytes 196616 | tf_op jit(solution)/shard_map/ppermute | solution.py:500
  55.2 5.5 %collective-permute-start.12 = (f32[2,64,128]{2,1,0:T(8,128)S(1)}, f32[2,64,128]{2,1,0:T(8,128)S(1)}, u32[]{:S(2)}, u32[]{:S(2)}) collective-permute-start(f32[2,64,128]{2,1,0:T(8,128)S(1)} %add_z.2.t0), channel_id=1, source_target_pairs={{0,1},{1,2},{2,3},{3,0},{4,5},{5,6},{6,7},{7,4},{8,9},{9,10},{10,1... | collective-permute-start | bytes 196616 | tf_op jit(solution)/shard_map/ppermute | solution.py:500
  55.2 0.7 copy-start.12
  62.2 3.8 %collective-permute-start.17 = (f32[64,128]{1,0:T(8,128)S(1)}, f32[64,128]{1,0:T(8,128)S(1)}, u32[]{:S(2)}, u32[]{:S(2)}) collective-permute-start(f32[64,128]{1,0:T(8,128)S(1)} %get-tuple-element.77), channel_id=1, source_target_pairs={{0,8},{8,16},{16,24},{24,32},{32,40},{40,48},{48,56},{56,0},{1,9},... | collective-permute-start | bytes 98312 | tf_op jit(solution)/shard_map/ppermute | solution.py:488
  62.2 3.8 %collective-permute-start.18 = (f32[64,128]{1,0:T(8,128)S(1)}, f32[64,128]{1,0:T(8,128)S(1)}, u32[]{:S(2)}, u32[]{:S(2)}) collective-permute-start(f32[64,128]{1,0:T(8,128)S(1)} %get-tuple-element.78), channel_id=1, source_target_pairs={{8,0},{16,8},{24,16},{32,24},{40,32},{48,40},{56,48},{0,56},{9,1},... | collective-permute-start | bytes 98312 | tf_op jit(solution)/shard_map/ppermute | solution.py:488
  63.9 3.9 %collective-permute-start.16 = (f32[64,128]{1,0:T(8,128)S(1)}, f32[64,128]{1,0:T(8,128)S(1)}, u32[]{:S(2)}, u32[]{:S(2)}) collective-permute-start(f32[64,128]{1,0:T(8,128)S(1)} %get-tuple-element.76), channel_id=1, source_target_pairs={{64,0},{65,1},{66,2},{67,3},{68,4},{69,5},{70,6},{71,7},{128,64},{... | collective-permute-start | bytes 98312 | tf_op jit(solution)/shard_map/ppermute | solution.py:481
  64.5 5.1 %collective-permute-start.15 = (f32[64,128]{1,0:T(8,128)S(1)}, f32[64,128]{1,0:T(8,128)S(1)}, u32[]{:S(2)}, u32[]{:S(2)}) collective-permute-start(f32[64,128]{1,0:T(8,128)S(1)} %get-tuple-element.76), channel_id=1, source_target_pairs={{0,64},{1,65},{2,66},{3,67},{4,68},{5,69},{6,70},{7,71},{64,128},{... | collective-permute-start | bytes 98312 | tf_op jit(solution)/shard_map/ppermute | solution.py:481
  71.9 6.3 %collective-permute-start.19 = (f32[2,64,128]{2,1,0:T(8,128)S(1)}, f32[2,64,128]{2,1,0:T(8,128)S(1)}, u32[]{:S(2)}, u32[]{:S(2)}) collective-permute-start(f32[2,64,128]{2,1,0:T(8,128)S(1)} %get-tuple-element.87), channel_id=1, source_target_pairs={{0,1},{1,2},{2,3},{3,0},{4,5},{5,6},{6,7},{7,4},{8,9},{9,10},{10,1... | collective-permute-start | bytes 196616 | tf_op jit(solution)/shard_map/ppermute | solution.py:512
  72.0 6.2 %collective-permute-start.20 = (f32[2,64,128]{2,1,0:T(8,128)S(1)}, f32[2,64,128]{2,1,0:T(8,128)S(1)}, u32[]{:S(2)}, u32[]{:S(2)}) collective-permute-start(f32[2,64,128]{2,1,0:T(8,128)S(1)} %get-tuple-element.88), channel_id=1, source_target_pairs={{0,2},{1,3},{2,0},{3,1},{4,6},{5,7},{6,4},{7,5},{8,10},{9,11},{10,... | collective-permute-start | bytes 196616 | tf_op jit(solution)/shard_map/ppermute | solution.py:512
  74.0 5.0 %collective-permute-start.21 = (f32[2,64,128]{2,1,0:T(8,128)S(1)}, f32[2,64,128]{2,1,0:T(8,128)S(1)}, u32[]{:S(2)}, u32[]{:S(2)}) collective-permute-start(f32[2,64,128]{2,1,0:T(8,128)S(1)} %get-tuple-element.89), channel_id=1, source_target_pairs={{0,3},{1,0},{2,1},{3,2},{4,7},{5,4},{6,5},{7,6},{8,11},{9,8},{10,9... | collective-permute-start | bytes 196616 | tf_op jit(solution)/shard_map/ppermute | solution.py:512
  79.0 8.3 %collective-permute-start.22 = (f32[2,64,128]{2,1,0:T(8,128)S(1)}, f32[2,64,128]{2,1,0:T(8,128)S(1)}, u32[]{:S(2)}, u32[]{:S(2)}) collective-permute-start(f32[2,64,128]{2,1,0:T(8,128)S(1)} %add_y.3.refs_0_), channel_id=1, source_target_pairs={{0,4},{1,5},{2,6},{3,7},{4,0},{5,1},{6,2},{7,3},{8,12},{9,13},{10,... | collective-permute-start | bytes 196616 | tf_op jit(solution)/shard_map/ppermute | solution.py:496
  87.3 5.3 %collective-permute-start.25 = (f32[2,64,128]{2,1,0:T(8,128)S(1)}, f32[2,64,128]{2,1,0:T(8,128)S(1)}, u32[]{:S(2)}, u32[]{:S(2)}) collective-permute-start(f32[2,64,128]{2,1,0:T(8,128)S(1)} %add_z.3.t0), channel_id=1, source_target_pairs={{0,3},{1,0},{2,1},{3,2},{4,7},{5,4},{6,5},{7,6},{8,11},{9,8},{10,9... | collective-permute-start | bytes 196616 | tf_op jit(solution)/shard_map/ppermute | solution.py:500
  90.1 5.8 %collective-permute-start.24 = (f32[2,64,128]{2,1,0:T(8,128)S(1)}, f32[2,64,128]{2,1,0:T(8,128)S(1)}, u32[]{:S(2)}, u32[]{:S(2)}) collective-permute-start(f32[2,64,128]{2,1,0:T(8,128)S(1)} %add_z.3.t0), channel_id=1, source_target_pairs={{0,2},{1,3},{2,0},{3,1},{4,6},{5,7},{6,4},{7,5},{8,10},{9,11},{10,... | collective-permute-start | bytes 196616 | tf_op jit(solution)/shard_map/ppermute | solution.py:500
  90.8 5.8 %collective-permute-start.23 = (f32[2,64,128]{2,1,0:T(8,128)S(1)}, f32[2,64,128]{2,1,0:T(8,128)S(1)}, u32[]{:S(2)}, u32[]{:S(2)}) collective-permute-start(f32[2,64,128]{2,1,0:T(8,128)S(1)} %add_z.3.t0), channel_id=1, source_target_pairs={{0,1},{1,2},{2,3},{3,0},{4,5},{5,6},{6,7},{7,4},{8,9},{9,10},{10,1... | collective-permute-start | bytes 196616 | tf_op jit(solution)/shard_map/ppermute | solution.py:500

commit v3 on v2

v3 whole, which is shorter than its diff:
```python
import jax
import jax.numpy as jnp
from jax import lax
from jax.experimental import pallas as pl
from jax.experimental.pallas import tpu as pltpu
from jax.sharding import PartitionSpec as P

NL = 8
R = 64
W = 128
NT = 3
NCH = NT * NL
HY = 8
UNROLL = 4
f32 = jnp.float32
VM = pl.BlockSpec(memory_space=pltpu.VMEM)
AN = pl.BlockSpec(memory_space=pl.ANY)
SM = pl.BlockSpec(memory_space=pltpu.SMEM)


def call(body, name, outs, n_scalar, scratch=(), n_any=0, cost=None):
    def run(*args):
        return pl.pallas_call(
            body,
            name=name,
            out_shape=[jax.ShapeDtypeStruct(s, f32) for s in outs],
            in_specs=[SM] * n_scalar + [VM] * (len(args) - n_scalar - n_any) + [AN] * n_any,
            out_specs=[VM] * len(outs),
            scratch_shapes=[pltpu.VMEM(s, f32) for s in scratch],
            cost_estimate=cost,
            compiler_params=pltpu.CompilerParams(vmem_limit_bytes=40 * 2**20),
        )(*args)

    return run


def lanes(shape):
    return lax.broadcasted_iota(jnp.int32, shape, 1)


def rx(v, k):
    return pltpu.roll(v, k % v.shape[1], 1)


def ry(v, k):
    return pltpu.roll(v, k % v.shape[0], 0)


def aside(v, shift):
    return pltpu.roll(v, shift, 1)


def minmod(a, b):
    return jnp.maximum(jnp.minimum(a, b), 0.0) + jnp.minimum(jnp.maximum(a, b), 0.0)


def coefs(vel):
    up = jnp.maximum(vel, 0.0)
    um = jnp.minimum(vel, 0.0)
    return up, um, 0.5 * up * (1.0 - up), 0.5 * um * (1.0 + um)


def divergence(c, co, roll):
    up, um, a, b = co
    ahead = roll(c, -1)
    d = ahead - c
    s = minmod(d, roll(d, 1))
    flux = up * c + a * s + um * ahead - b * roll(s, -1)
    return flux - roll(flux, 1)


def upwind(c, vel, roll):
    flux = jnp.maximum(vel, 0.0) * c + jnp.minimum(vel, 0.0) * roll(c, -1)
    return flux - roll(flux, 1)


M = 4
ER = R + HY
EW = 2 * W
TILES = 3
NROW = 176
CORNER = 160
FLOW, TEMP, SEA, FLOOR, SUN, DIF = 24, 28, 29, 30, 31, 32
GROWS = 32
COVER = 16 * 2**20
PART = 2 * R + 16


def put_x(px_ref, value, i):
    tile, lane = i >> 4, (i & 15) * 8
    acc = px_ref[tile]
    at = lanes(acc.shape)
    moved = pltpu.roll(value, lane + M, 1)
    px_ref[tile] = jnp.where((at >= lane) & (at < lane + 8), moved, acc)


def put_y(value_ref, index, i, pyu_ref, pyd_ref):
    pyu_ref[pl.ds(4 * i, M), :] = value_ref[index + (slice(R - M, R),)]
    pyd_ref[pl.ds(4 * i, M), :] = value_ref[index + (slice(0, M),)]


def flow_pack(flow_ref, px_ref, pyu_ref, pyd_ref):
    px_ref[...] = jnp.zeros_like(px_ref)
    pyu_ref[...] = jnp.zeros_like(pyu_ref)
    pyd_ref[...] = jnp.zeros_like(pyd_ref)
    for q in range(2):
        put_x(px_ref, flow_ref[q, 0], FLOW + q)
        put_y(flow_ref, (q, 0), FLOW + q, pyu_ref, pyd_ref)


def first_pack(
    c_ref, temp_ref, sea_ref, floor_ref, sun_ref, dif_ref, px_in, pyu_in, pyd_in,
    px_ref, pyu_ref, pyd_ref, mask_ref,
):
    px_ref[...] = px_in[...]
    pyu_ref[...] = pyu_in[...]
    pyd_ref[...] = pyd_in[...]
    mask_ref[0] = sea_ref[...].astype(f32)
    mask_ref[1] = floor_ref[...].astype(f32)
    mask_ref[2] = sun_ref[...]
    mask_ref[3] = temp_ref[0]
    for t in range(NT):
        for l in range(NL):
            put_x(px_ref, c_ref[t, l], t * NL + l)
            put_y(c_ref, (t, l), t * NL + l, pyu_ref, pyd_ref)
    for l in range(NL):
        put_x(px_ref, dif_ref[l], DIF + l)
        put_y(dif_ref, (l,), DIF + l, pyu_ref, pyd_ref)
    for j, i in enumerate((SEA, FLOOR, SUN, TEMP)):
        put_x(px_ref, mask_ref[j], i)
        put_y(mask_ref, (j,), i, pyu_ref, pyd_ref)


def pack_other(flow_ref, other_ref, px_in, px_ref, pair_ref):
    px_ref[...] = px_in[...]
    for q in range(2):
        put_x(px_ref, other_ref[q, 0], FLOW + 2 + q)
        pair_ref[0, q * R : (q + 1) * R, :] = flow_ref[q, 0]
        pair_ref[1, q * R : (q + 1) * R, :] = other_ref[q, 0]


def pack_y(ids_ref, left_ref, right_ref, other_ref, pyu_in, pyd_in, hx_ref, pyu_ref, pyd_ref):
    at = lanes((R, W))
    gx = ids_ref[1]
    for k in range(TILES):
        left = jnp.where(gx == 0, 0.0, left_ref[k])
        right = jnp.where(gx == ids_ref[4] - 1, 0.0, right_ref[k])
        hx_ref[k] = jnp.where(((at >> 2) & 1) == 0, left, right)
    pyu_ref[...] = pyu_in[...]
    pyd_ref[...] = pyd_in[...]
    for j in range(2):
        put_y(other_ref, (j, 0), FLOW + 2 + j, pyu_ref, pyd_ref)
    for k in range(TILES):
        pyu_ref[CORNER + 4 * k : CORNER + 4 * k + M, :] = hx_ref[k, R - M : R, :]
        pyd_ref[CORNER + 4 * k : CORNER + 4 * k + M, :] = hx_ref[k, 0:M, :]


def extend_flow(
    ids_ref, side_ref, lo_ref, hi_ref, e_ref, hx_ref, los_ref, his_ref
):
    gy = ids_ref[2]
    los_ref[...] = jnp.where(gy == 0, 0.0, lo_ref[...])
    his_ref[...] = jnp.where(gy == ids_ref[3] - 1, 0.0, hi_ref[...])
    for k in range(TILES):
        hx_ref[k, 0:R] = side_ref[k]
        hx_ref[k, R:ER] = jnp.zeros((HY, W), f32)
        hx_ref[k, R : R + M] = his_ref[CORNER + 4 * k : CORNER + 4 * k + M, :]
        hx_ref[k, ER - M : ER] = los_ref[CORNER + 4 * k : CORNER + 4 * k + M, :]
    block = hx_ref[FLOW >> 4]
    turned = jnp.concatenate([block, jnp.zeros((W - ER, W), f32)], 0).T
    for k in range(2):
        for q in range(2):
            i = FLOW + 2 * k + q
            at = 8 * q
            e_ref[k, at : at + M, :] = his_ref[4 * i : 4 * i + M, :]
            e_ref[k, at + M : at + 2 * M, :] = los_ref[4 * i : 4 * i + M, :]
        first = (FLOW & 15) * 8 + 16 * k
        e_ref[k, 16:GROWS, :] = turned[first : first + 16, :]


def place(ref, main, side, hi, lo):
    ref[0:R, 0:W] = main
    ref[:, W:] = side
    ref[R : R + M, 0:W] = hi
    ref[ER - M : ER, 0:W] = lo
    return ref[...]


def channel(ref, main, i, hx_ref, los_ref, his_ref):
    side = pltpu.roll(hx_ref[i >> 4], (W + W - M - (i & 15) * 8) & (W - 1), 1)
    return place(ref, main, side, his_ref[pl.ds(4 * i, M), :], los_ref[pl.ds(4 * i, M), :])


def wet_of(wx_ref, l):
    return jnp.where(l < wx_ref[1], wx_ref[0], 0.0)


def open_x(wet):
    return wet * rx(wet, -1)


def open_y(wet):
    return wet * ry(wet, -1)


def laplace(v):
    return rx(v, -1) + rx(v, 1) + ry(v, -1) + ry(v, 1) - 4.0 * v


def next_currents(u, v, wet, coriolis):
    return (
        open_x(wet) * (u + coriolis * v + 0.2 * laplace(u)),
        open_y(wet) * (v - coriolis * u + 0.2 * laplace(v)),
    )


def coriolis_of(ids_ref):
    at = lax.broadcasted_iota(jnp.int32, (ER, EW), 0)
    row = ids_ref[2] * R + jnp.where(at < R + M, at, at - ER)
    rows = (ids_ref[3] * R).astype(f32)
    return 0.1 + 0.1 * row.astype(f32) / rows


def mix(adv_ref, kv_ref, mix_ref, rows, cols):
    for l in range(NL):
        c = adv_ref[l]
        out = c
        if l + 1 < NL:
            out = out + kv_ref[l, :rows, :cols] * (adv_ref[l + 1] - c)
        if l:
            out = out - kv_ref[l - 1, :rows, :cols] * (c - adv_ref[l - 1])
        mix_ref[l] = out


def wide_step(t, l, c, wet, east, north, hx_ref, los_ref, his_ref, slot_ref):
    c = channel(slot_ref, c, t * NL + l, hx_ref, los_ref, his_ref)
    return wet * (c - divergence(c, coefs(east), rx) - divergence(c, coefs(north), ry))


def plankton_one(
    ids_ref, c_ref, mask_ref, dif_ref, g0, g1, g2, g3, e0, e1, e2, e3, hx_ref, los_ref, his_ref,
    mix_ref, a0, a1, a2, a3, u_ref, v_ref, east_ref, north_ref, wx_ref, kv_ref,
    g_ref, e_ref, gx_ref, slot_ref, adv_ref, cols_ref,
):
    y = ids_ref[0] & 3
    z = ids_ref[0] >> 2
    for k, (ref, edge) in enumerate(((g0, e0), (g1, e1), (g2, e2), (g3, e3))):
        for zz in range(2):
            level = ((z + zz) & 1) * 4 + ((y + 4 - k) & 3)
            g_ref[level] = ref[zz]
            e_ref[level] = edge[zz]
    halos = (hx_ref, los_ref, his_ref)
    for k in range(2):
        channel(wx_ref.at[k], mask_ref[k], SEA + k, *halos)
    gx_ref[...] = jnp.concatenate([e_ref[l, 16:GROWS, :] for l in range(NL)], 0).T[:ER]

    for l in range(NL):
        u = place(
            u_ref.at[l], g_ref[l, 0:R, :], pltpu.roll(gx_ref[...], (W - M - 16 * l) % W, 1),
            e_ref[l, 0:M, :], e_ref[l, M : 2 * M, :],
        )
        v = place(
            v_ref.at[l], g_ref[l, R : 2 * R, :], pltpu.roll(gx_ref[...], (W - M - 8 - 16 * l) % W, 1),
            e_ref[l, 2 * M : 3 * M, :], e_ref[l, 3 * M : 4 * M, :],
        )
        wet = wet_of(wx_ref, float(l))
        east = open_x(wet) * u
        north = open_y(wet) * v
        east_ref[l] = east
        north_ref[l] = north
        adv_ref[l] = wide_step(1, l, c_ref[1, l], wet, east, north, *halos, slot_ref.at[0, l])
        if l + 1 < NL:
            dif = channel(slot_ref.at[1, l], dif_ref[l], DIF + l, *halos)
            kv_ref[l] = dif * wet * wet_of(wx_ref, float(l + 1))
    mix(adv_ref, kv_ref, mix_ref, ER, EW)
    acc = jnp.zeros((R, W), f32)
    at = lanes(acc.shape)
    for l in range(NL):
        moved = pltpu.roll(mix_ref[l, 0:R, W:], 4 * l + 2, 1)
        acc = jnp.where((at >= 4 * l) & (at < 4 * l + 4), moved, acc)
    cols_ref[...] = jnp.concatenate([acc, acc], 0).T
    for k, ref in enumerate((a0, a1, a2, a3)):
        j = (y + k) & 3
        for q in range(2):
            l = 2 * j + q
            ref[q * R : (q + 1) * R, :] = mix_ref[l, 0:R, 0:W]
            ref[2 * R + 4 * q : 2 * R + 4 * q + 2, :] = mix_ref[l, R : R + 2, 0:W]
            ref[2 * R + 4 * q + 2 : 2 * R + 4 * q + 4, :] = mix_ref[l, ER - 2 : ER, 0:W]
        ref[2 * R + 8 : PART, :] = cols_ref[pl.ds(pl.multiple_of(8 * j, 8), 8), :]


def other_one(t):
    def body(
        c_ref, hx_ref, los_ref, his_ref, east_ref, north_ref, kv_ref, wx_ref, mix_ref, slot_ref,
        adv_ref,
    ):
        for l in range(NL):
            adv_ref[l] = wide_step(
                t, l, c_ref[t, l], wet_of(wx_ref, float(l)), east_ref[l], north_ref[l], hx_ref,
                los_ref, his_ref, slot_ref.at[l],
            )
        mix(adv_ref, kv_ref, mix_ref, ER, EW)

    return body


def rest_one(
    ids_ref, rate_ref, mask_ref, u_ref, v_ref, east_ref, north_ref, wx_ref, hx_ref, los_ref, his_ref,
    cur_ref, tadv_ref, sun_ref, pace_ref, slot_ref,
):
    for t in range(NT):
        pace_ref[t] = jnp.full((8, W), rate_ref[t], f32)
    channel(sun_ref, mask_ref[2], SUN, hx_ref, los_ref, his_ref)
    coriolis = coriolis_of(ids_ref)

    def level(l, carry):
        new_u, new_v = next_currents(
            u_ref[l], v_ref[l], wet_of(wx_ref, l.astype(f32)), coriolis
        )
        cur_ref[0, l] = new_u
        cur_ref[1, l] = new_v
        return carry

    lax.fori_loop(0, NL, level, 0, unroll=UNROLL)
    own = ids_ref[0]
    temp = channel(slot_ref, mask_ref[3], TEMP, hx_ref, los_ref, his_ref)
    tadv_ref[...] = temp - upwind(temp, east_ref[own], rx) - upwind(temp, north_ref[own], ry)


def inner_step(c_ref, l, wx_ref, east, north):
    c = c_ref[l, 0:R, 0:W]
    div = divergence(c_ref[l, 0:R, :], coefs(east), rx)[:, :W]
    div = div + divergence(c_ref[l, :, 0:W], coefs(north), ry)[:R]
    return jnp.where(float(l) < wx_ref[1, 0:R, 0:W], wx_ref[0, 0:R, 0:W], 0.0) * (c - div)


def plankton_two(
    ids_ref, c_ref, cur_ref, kv_ref, wx_ref, mix_ref, parts, east_ref, north_ref, adv_ref
):
    for l in range(NL):
        wet = wet_of(wx_ref, float(l))
        east = open_x(wet[:R]) * cur_ref[0, l, 0:R, :]
        north = open_y(wet[:, :W]) * cur_ref[1, l, :, 0:W]
        east_ref[l] = east
        north_ref[l] = north
        adv_ref[l] = inner_step(c_ref, l, wx_ref, east, north)
    mix(adv_ref, kv_ref, mix_ref, R, W)
    y = ids_ref[0] & 3
    for k, ref in enumerate(parts):
        ref[...] = mix_ref[pl.ds(2 * ((y + k) & 3), 2)]


def other_two(c_ref, east_ref, north_ref, kv_ref, wx_ref, mix_ref, adv_ref):
    for l in range(NL):
        adv_ref[l] = inner_step(c_ref, l, wx_ref, east_ref[l], north_ref[l])
    mix(adv_ref, kv_ref, mix_ref, R, W)


def rest_two(ids_ref, cur_ref, east_ref, north_ref, wx_ref, temp_ref, out_ref, tadv_ref):
    own = ids_ref[0]
    temp = temp_ref[0:R, 0:W]
    tadv_ref[...] = (
        temp
        - upwind(temp_ref[0:R, :], east_ref[own], rx)[:, :W]
        - upwind(temp_ref[:, 0:W], north_ref[own], ry)[:R]
    )
    new_u, new_v = next_currents(
        cur_ref[0, own], cur_ref[1, own], wet_of(wx_ref, own.astype(f32)), coriolis_of(ids_ref)
    )
    out_ref[0, 0] = new_u[:R, :W]
    out_ref[1, 0] = new_v[:R, :W]


def biology(ids_ref, rate_ref, mixes, absorb, solar, wx, tadv_ref, outs, tau_ref, a_ref):
    sea, depth = wx
    mu, mortal, recycle = (rate_ref[t, 0:1, 0:1] for t in range(NT))
    tau = jnp.zeros(solar.shape, f32)
    for l in range(NL):
        a = 0.04 + 0.03 * absorb(l)
        light = solar * jnp.exp(-tau - 0.5 * a)
        tau_ref[l] = tau
        a_ref[l] = a
        wet = jnp.where(float(l) < depth, sea, 0.0)
        n, p, d = mixes[0][l], mixes[1][l], mixes[2][l]
        uptake = mu * (light / (light + 0.3)) * p * n / (jnp.abs(n) + 0.5)
        dead = mortal * p
        back = recycle * d
        outs[0][l] = wet * (n - uptake + back)
        outs[1][l] = wet * (p + uptake - dead)
        outs[2][l] = wet * (d + dead - back)
        tau = tau + a
    own = ids_ref[0]
    tau, a = tau_ref[own], a_ref[own]
    heat = 0.5 * solar * (jnp.exp(-tau) - jnp.exp(-tau - a))
    wet = jnp.where(own.astype(f32) < depth, sea, 0.0)
    return wet * (tadv_ref[...] + heat)


def biology_one(
    ids_ref, rate_ref, n_ref, p_ref, d_ref, t0, t1, t2, t3, sun_ref, wx_ref, tadv_ref, cur_ref,
    kv_ref, n_out, p_out, d_out, temp_ref, mix_ref, a0, a1, a2, a3, east_ref, north_ref,
    sum_ref, cols_ref, turn_ref, slot_ref, tau_ref, a_ref, adv_ref,
):
    y = ids_ref[0] & 3
    for k, ref in enumerate((t0, t1, t2, t3)):
        j = (y + 4 - k) & 3
        sum_ref[j] = ref[...]
        cols_ref[pl.ds(pl.multiple_of(8 * j, 8), 8), :] = ref[2 * R + 8 : PART, :]
    turned = jnp.concatenate([cols_ref[...], jnp.zeros((W - 4 * NL, W), f32)], 0).T
    turn_ref[...] = turned[:ER]

    def absorb(l):
        j, q = l // 2, l % 2
        slot = slot_ref.at[l]
        slot[0:R, 0:W] = sum_ref[j, q * R : (q + 1) * R, :]
        slot[:, W:] = pltpu.roll(turn_ref[...], (W - 2 - 4 * l) % W, 1)
        at = 2 * R + 4 * q
        slot[R : R + 2, 0:W] = sum_ref[j, at : at + 2, :]
        slot[ER - 2 : ER, 0:W] = sum_ref[j, at + 2 : at + 4, :]
        return slot[...]

    temp_ref[...] = biology(
        ids_ref, rate_ref, (n_ref, p_ref, d_ref), absorb, sun_ref[...], (wx_ref[0], wx_ref[1]),
        tadv_ref, (n_out, p_out, d_out), tau_ref, a_ref,
    )
    plankton_two(
        ids_ref, p_out, cur_ref, kv_ref, wx_ref, mix_ref, (a0, a1, a2, a3), east_ref, north_ref,
        adv_ref,
    )


def biology_two(
    ids_ref, rate_ref, n_ref, p_ref, d_ref, t0, t1, t2, t3, sun_ref, wx_ref, tadv_ref,
    c_ref, temp_ref, sum_ref, tau_ref, a_ref,
):
    y = ids_ref[0] & 3
    for k, ref in enumerate((t0, t1, t2, t3)):
        sum_ref[pl.ds(2 * ((y + 4 - k) & 3), 2)] = ref[...]
    wx = (wx_ref[0, 0:R, 0:W], wx_ref[1, 0:R, 0:W])
    temp_ref[0] = biology(
        ids_ref, rate_ref, (n_ref, p_ref, d_ref), lambda l: sum_ref[l], sun_ref[0:R, 0:W], wx,
        tadv_ref, [c_ref.at[t] for t in range(NT)], tau_ref, a_ref,
    )


def ring_x(value):
    n, m = lax.axis_size("gx"), lax.axis_size("tracer")
    ahead = [
        (g * m + t, (g + 1) * m + t if g + 1 < n else t ^ (m // 2))
        for g in range(n)
        for t in range(m)
    ]
    back = [(b, a) for a, b in ahead]
    axes = ("gx", "tracer")
    return lax.ppermute(value, axes, ahead), lax.ppermute(value, axes, back)


def ring_y(up, down):
    n = lax.axis_size("gy")
    ahead = [(i, (i + 1) % n) for i in range(n)]
    back = [(b, a) for a, b in ahead]
    return lax.ppermute(up, "gy", ahead), lax.ppermute(down, "gy", back)


def by_y(k):
    return [(z * 4 + y, z * 4 + (y + k) % 4) for z in range(2) for y in range(4)]


def over_z(value):
    return lax.ppermute(value, "tracer", [(i, i ^ 4) for i in range(8)])


def spread_y(value):
    return [value] + [lax.ppermute(value, "tracer", by_y(k)) for k in (1, 2, 3)]


def add_parts(*refs):
    ins, out = refs[:-2], refs[-1]
    acc = ins[0][...] + ins[1][...]
    if len(ins) > 2:
        acc = acc + (ins[2][...] + ins[3][...])
    out[...] = acc


def total(parts, during_y, during_z):
    got = [parts[0]] + [lax.ppermute(parts[k], "tracer", by_y(k)) for k in (1, 2, 3)]
    part = parts[0].shape
    (mine,) = call(add_parts, "add_y", [part], 0, n_any=1)(*got, during_y)
    away = over_z(mine)
    (full,) = call(add_parts, "add_z", [part], 0, n_any=1)(mine, away, during_z)
    return spread_y(full)


def per_device(c, flow, temp, dif, solar, rates, sea, floor):
    ids = jnp.stack(
        [
            lax.axis_index("tracer"),
            lax.axis_index("gx"),
            lax.axis_index("gy"),
            jnp.int32(lax.axis_size("gy")),
            jnp.int32(lax.axis_size("gx")),
        ]
    )
    tile = (R, W)
    col = (NL, R, W)
    ext = (ER, EW)
    deep = (NL, ER, EW)
    other = over_z(flow)
    rows = (NROW, W)
    sides = (TILES, R, W)
    packs = call(
        flow_pack, "pack_flow", [sides, rows, rows], 0,
        cost=pl.CostEstimate(flops=0, transcendentals=0, bytes_accessed=COVER),
    )(flow)
    px, pyu, pyd, masks = call(first_pack, "pack_one", [sides, rows, rows, (4, R, W)], 0)(
        c, temp, sea, floor, solar, dif, *packs
    )
    px, pair = call(pack_other, "pack_two", [sides, (2, 2 * R, W)], 0)(flow, other, px)
    left, right = ring_x(px)
    gathered = spread_y(pair)
    side, pyu, pyd = call(pack_y, "pack_y", [sides, rows, rows], 1)(
        ids, left, right, other, pyu, pyd
    )
    lo, hi = ring_y(pyu, pyd)
    own, hx, los, his = call(
        extend_flow, "extend", [(2, GROWS, W), (TILES, ER, W), rows, rows], 1
    )(ids, side, lo, hi)
    margins = spread_y(own)
    part = (PART, W)
    plank, a0, a1, a2, a3, u, v, east, north, wx, kv = call(
        plankton_one, "plankton_one",
        [deep, part, part, part, part, deep, deep, deep, deep, (2, ER, EW), deep], 1,
        [(NL, 2 * R, W), (NL, GROWS, W), (ER, W), (2, NL, ER, EW), deep, (W, W)],
    )(ids, c, masks, dif, *gathered, *margins, hx, los, his)
    nutri, detri = (
        call(other_one(t), "other_one", [deep], 0, [deep, deep])(
            c, hx, los, his, east, north, kv, wx
        )[0]
        for t in (0, 2)
    )
    cur, tadv, sun, pace = call(
        rest_one, "rest_one", [(2, NL, ER, EW), ext, ext, (NT, 8, W)], 2, [ext]
    )(ids, rates, masks, u, v, east, north, wx, hx, los, his)
    sums = total((a0, a1, a2, a3), nutri, detri)
    half = (2, R, W)
    n, p, d, heated, plank, a0, a1, a2, a3, east, north = call(
        biology_one, "biology_one",
        [deep, deep, deep, ext, col, half, half, half, half, (NL, R, EW), (NL, ER, W)], 1,
        [(4, PART, W), (4 * NL, W), (ER, W), deep, deep, deep, col],
    )(ids, pace, nutri, plank, detri, *sums, sun, wx, tadv, cur, kv)
    nutri, detri = (
        call(other_two, "other_two", [col], 0, [col])(q, east, north, kv, wx)[0] for q in (n, d)
    )
    currents, tadv = call(rest_two, "rest_two", [(2, 1, R, W), tile], 1)(
        ids, cur, east, north, wx, heated
    )
    sums = total((a0, a1, a2, a3), nutri, detri)
    c, last_temp = call(
        biology_two, "biology_two", [(NT, NL, R, W), (1, R, W)], 1, [col, col, col]
    )(ids, pace, nutri, plank, detri, *sums, sun, wx, tadv)
    return c, currents, last_temp


def solution(mesh):
    in_specs = (
        P("tracer", None, "gy", "gx"),
        P(None, "tracer", "gy", "gx"),
        P("tracer", "gy", "gx"),
        P(None, "gy", "gx"),
        P("gy", "gx"),
        P("tracer"),
        P("gy", "gx"),
        P("gy", "gx"),
    )
    out_specs = (
        P("tracer", None, "gy", "gx"),
        P(None, "tracer", "gy", "gx"),
        P("tracer", "gy", "gx"),
    )
    return jax.shard_map(
        per_device, mesh=mesh, in_specs=in_specs, out_specs=out_specs, check_vma=False
    )
```

time: 99.8 us -> 97.3 us (0.975); the launches traced: 98.3 us -> 96.9 us
  waiting for transfers between devices: 34.8 us -> 25.5 us
  starting transfers between devices: 39.8 us -> 43.9 us
  Pallas kernels: 17.8 us -> 20.6 us
  local copies, waits for them, and re-layouts: 5 us -> 6.08 us
    ppermute x4 -> x2, waiting for transfers between devices: 8.55 us -> 0.01 us  [ring_x(): return (lax.ppermute(value, axes, ahead), lax.ppermute(value, axes, back))]
    ppermute x9 -> x12, starting transfers between devices: 11.9 us -> 17.7 us  [spread_y(): return [value] + [lax.ppermute(value, 'tracer', by_y(k)) for k in (1, 2, 3)]]
    pallas_call x17 -> x18, Pallas kernels: 17.8 us -> 20.6 us  [run(): pl.pallas_call(body, name=name, out_shape=[jax.ShapeDtypeStruct(s, f32) f...]
    ppermute x4 -> x2, waiting for transfers between devices: 0.01 us -> 2.21 us  [ring_y(): return (lax.ppermute(up, 'gy', ahead), lax.ppermute(down, 'gy', back))]
    ppermute x4 -> x2, starting transfers between devices: 4.05 us -> 2.1 us  [ring_x(): return (lax.ppermute(value, axes, ahead), lax.ppermute(value, axes, back))]
    ppermute x4 -> x2, starting transfers between devices: 3.5 us -> 1.75 us  [ring_y(): return (lax.ppermute(up, 'gy', ahead), lax.ppermute(down, 'gy', back))]
    ppermute x3, starting transfers between devices: 13 us -> 14.3 us  [over_z(): return lax.ppermute(value, 'tracer', [(i, i ^ 4) for i in range(8)])]
    ppermute x3, waiting for transfers between devices: 8.3 us -> 7.17 us  [over_z(): return lax.ppermute(value, 'tracer', [(i, i ^ 4) for i in range(8)])]
  transfers between devices with their start and end apart: 26 -> 25, of which waited for: 18 -> 14; matrix products, arithmetic and copies ran while one was open for 0% -> 0% of each run, Pallas kernels for 9% -> 12%
where the time goes in v3:
time: 97.3 us; the launch traced here: 96.9 us
  starting transfers between devices  43.9 us (45%)
  waiting for transfers between devices  25.5 us (26%)
  Pallas kernels  20.6 us (21%)
  local copies, waits for them, and re-layouts  6.08 us (6%)
    pallas_call x18, Pallas kernels, run(): pl.pallas_call(body, name=name, out_shape=[jax.ShapeDtypeStruct(s, f32) f...  20.6 us
    ppermute x12, starting transfers between devices, spread_y(): return [value] + [lax.ppermute(value, 'tracer', by_y(k)) for k in (1, 2, 3)]  17.7 us
    ppermute x3, starting transfers between devices, over_z(): return lax.ppermute(value, 'tracer', [(i, i ^ 4) for i in range(8)])  14.3 us
    ppermute x12, waiting for transfers between devices, spread_y(): return [value] + [lax.ppermute(value, 'tracer', by_y(k)) for k in (1, 2, 3)]  12.7 us
    ppermute x6, starting transfers between devices, total(): lax.ppermute(parts[k], 'tracer', by_y(k))  8.02 us
    ppermute x3, waiting for transfers between devices, over_z(): return lax.ppermute(value, 'tracer', [(i, i ^ 4) for i in range(8)])  7.17 us
    unnamed x22, local copies, waits for them, and re-layouts  6 us
    ppermute x6, waiting for transfers between devices, total(): lax.ppermute(parts[k], 'tracer', by_y(k))  3.4 us
  transfers between devices with their start and end apart: 25, of which 14 were waited for; matrix products, arithmetic and copies ran while one was open for 0% of the time, Pallas kernels for 12%

profile of v3, /device:TPU:2, one launch (start us, length us, event | category | flops | bytes accessed | tf_op | source)
XLA Modules:
  0.0 96.9 jit_solution(10055902695108786440)
XLA Ops:
  0.6 7.3 %collective-permute-start = (f32[2,1,64,128]{3,2,1,0:T(8,128)}, f32[2,1,64,128]{3,2,1,0:T(8,128)S(1)}, u32[]{:S(2)}, u32[]{:S(2)}) collective-permute-start(f32[2,1,64,128]{3,2,1,0:T(8,128)} %flow_ref.3), channel_id=1, source_target_pairs={{0,4},{1,5},{2,6},{3,7},{4,0},{5,1},{6,2},{7,3},{8,12},{9,13},{10,... | collective-permute-start | bytes 196616 | tf_op jit(solution)/shard_map/ppermute | solution.py:470
  7.9 0.9 copy-done.4
  8.8 0.1 pack_flow.1
  8.9 0.0 copy-start
  8.9 1.1 %copy-done = f32[3,8,64,128]{3,2,1,0:T(8,128)S(1)} copy-done((f32[3,8,64,128]{3,2,1,0:T(8,128)S(1)}, f32[3,8,64,128]{3,2,1,0:T(8,128)}, u32[]{:S(2)}) %copy-start) | copy-done | bytes 786456
  10.0 0.9 copy-done.2
  11.0 0.8 copy-done.6
  11.7 0.8 copy-done.7
  12.5 0.8 copy-done.8
  13.2 0.8 copy-done.9
  14.0 0.4 pack_one.1
  14.4 0.0 collective-permute-done.other_ref
  14.4 0.1 pack_two.1
  14.5 0.6 collective-permute-start.5
  15.2 1.5 %collective-permute-start.4 = (f32[3,64,128]{2,1,0:T(8,128)S(1)}, f32[3,64,128]{2,1,0:T(8,128)S(1)}, u32[]{:S(2)}, u32[]{:S(2)}) collective-permute-start(f32[3,64,128]{2,1,0:T(8,128)S(1)} %get-tuple-element.54), channel_id=1, source_target_pairs={{0,64},{1,65},{2,66},{3,67},{4,68},{5,69},{6,70},{7,71},{64,128},{... | collective-permute-start | bytes 294920 | tf_op jit(solution)/shard_map/ppermute | solution.py:455
  16.6 3.0 %collective-permute-start.3 = (f32[2,128,128]{2,1,0:T(8,128)S(1)}, f32[2,128,128]{2,1,0:T(8,128)S(1)}, u32[]{:S(2)}, u32[]{:S(2)}) collective-permute-start(f32[2,128,128]{2,1,0:T(8,128)S(1)} %get-tuple-element.53.g0), channel_id=1, source_target_pairs={{0,3},{1,0},{2,1},{3,2},{4,7},{5,4},{6,5},{7,6},{8,11},{9,8},{10,9... | collective-permute-start | bytes 393224 | tf_op jit(solution)/shard_map/ppermute | solution.py:474
  19.6 0.6 collective-permute-start.2
  20.3 1.0 %collective-permute-start.1 = (f32[2,128,128]{2,1,0:T(8,128)S(1)}, f32[2,128,128]{2,1,0:T(8,128)S(1)}, u32[]{:S(2)}, u32[]{:S(2)}) collective-permute-start(f32[2,128,128]{2,1,0:T(8,128)S(1)} %get-tuple-element.53.g0), channel_id=1, source_target_pairs={{0,1},{1,2},{2,3},{3,0},{4,5},{5,6},{6,7},{7,4},{8,9},{9,10},{10,1... | collective-permute-start | bytes 393224 | tf_op jit(solution)/shard_map/ppermute | solution.py:474
  21.2 0.1 stack.15.ids_ref
  21.3 0.6 pack_y.1
  21.9 0.0 collective-permute-start.6
  21.9 1.7 %collective-permute-start.7 = (f32[176,128]{1,0:T(8,128)S(1)}, f32[176,128]{1,0:T(8,128)S(1)}, u32[]{:S(2)}, u32[]{:S(2)}) collective-permute-start(f32[176,128]{1,0:T(8,128)S(1)} %get-tuple-element.59), channel_id=1, source_target_pairs={{8,0},{16,8},{24,16},{32,24},{40,32},{48,40},{56,48},{0,56},{9,1},... | collective-permute-start | bytes 270344 | tf_op jit(solution)/shard_map/ppermute | solution.py:462
  23.7 2.2 %collective-permute-done.6.lo_ref = f32[176,128]{1,0:T(8,128)S(1)} collective-permute-done((f32[176,128]{1,0:T(8,128)S(1)}, f32[176,128]{1,0:T(8,128)S(1)}, u32[]{:S(2)}, u32[]{:S(2)}) %collective-permute-start.6) | collective-permute-done | bytes 90144 | tf_op jit(solution)/shard_map/ppermute | solution.py:462
  25.9 0.0 collective-permute-done.7.hi_ref
  25.9 0.6 extend.1
  26.5 2.8 %collective-permute-start.10 = (f32[2,32,128]{2,1,0:T(8,128)S(1)}, f32[2,32,128]{2,1,0:T(8,128)S(1)}, u32[]{:S(2)}, u32[]{:S(2)}) collective-permute-start(f32[2,32,128]{2,1,0:T(8,128)S(1)} %get-tuple-element.60.e0), channel_id=1, source_target_pairs={{0,3},{1,0},{2,1},{3,2},{4,7},{5,4},{6,5},{7,6},{8,11},{9,8},{10,9... | collective-permute-start | bytes 98312 | tf_op jit(solution)/shard_map/ppermute | solution.py:474
  29.3 1.3 %collective-permute-start.9 = (f32[2,32,128]{2,1,0:T(8,128)S(1)}, f32[2,32,128]{2,1,0:T(8,128)S(1)}, u32[]{:S(2)}, u32[]{:S(2)}) collective-permute-start(f32[2,32,128]{2,1,0:T(8,128)S(1)} %get-tuple-element.60.e0), channel_id=1, source_target_pairs={{0,2},{1,3},{2,0},{3,1},{4,6},{5,7},{6,4},{7,5},{8,10},{9,11},{10,... | collective-permute-start | bytes 98312 | tf_op jit(solution)/shard_map/ppermute | solution.py:474
  30.5 0.0 collective-permute-done.3.g3
  30.5 0.3 collective-permute-start.8
  30.9 3.8 %collective-permute-done.9.e2 = f32[2,32,128]{2,1,0:T(8,128)S(1)} collective-permute-done((f32[2,32,128]{2,1,0:T(8,128)S(1)}, f32[2,32,128]{2,1,0:T(8,128)S(1)}, u32[]{:S(2)}, u32[]{:S(2)}) %collective-permute-start.9) | collective-permute-done | bytes 32800 | tf_op jit(solution)/shard_map/ppermute | solution.py:474
  34.7 1.3 %collective-permute-done.8.e1 = f32[2,32,128]{2,1,0:T(8,128)S(1)} collective-permute-done((f32[2,32,128]{2,1,0:T(8,128)S(1)}, f32[2,32,128]{2,1,0:T(8,128)S(1)}, u32[]{:S(2)}, u32[]{:S(2)}) %collective-permute-start.8) | collective-permute-done | bytes 32800 | tf_op jit(solution)/shard_map/ppermute | solution.py:474
  36.0 3.8 %plankton_one.1 = (f32[8,72,256]{2,1,0:T(8,128)S(1)}, f32[144,128]{1,0:T(8,128)S(1)}, f32[144,128]{1,0:T(8,128)S(1)}, f32[144,128]{1,0:T(8,128)S(1)}, f32[144,12...) custom-call(s32[5]{0:T(128)S(1)} %stack.15.ids_ref, ...), custom_call_target="tpu_custom_call" | custom-call | tf_op jit(solution)/shard_map/plankton_one/pallas_call | solution.py:23
  39.8 0.1 collective-permute-start.11
  39.9 1.4 %collective-permute-start.12 = (f32[144,128]{1,0:T(8,128)S(1)}, f32[144,128]{1,0:T(8,128)S(1)}, u32[]{:S(2)}, u32[]{:S(2)}) collective-permute-start(f32[144,128]{1,0:T(8,128)S(1)} %get-tuple-element.74), channel_id=1, source_target_pairs={{0,2},{1,3},{2,0},{3,1},{4,6},{5,7},{6,4},{7,5},{8,10},{9,11},{10,... | collective-permute-start | bytes 221192 | tf_op jit(solution)/shard_map/ppermute | solution.py:486
  41.3 2.4 %collective-permute-start.13 = (f32[144,128]{1,0:T(8,128)S(1)}, f32[144,128]{1,0:T(8,128)S(1)}, u32[]{:S(2)}, u32[]{:S(2)}) collective-permute-start(f32[144,128]{1,0:T(8,128)S(1)} %get-tuple-element.75), channel_id=1, source_target_pairs={{0,3},{1,0},{2,1},{3,2},{4,7},{5,4},{6,5},{7,6},{8,11},{9,8},{10,9... | collective-permute-start | bytes 221192 | tf_op jit(solution)/shard_map/ppermute | solution.py:486
  43.7 1.8 %other_one.2.refs_4_.n_ref = f32[8,72,256]{2,1,0:T(8,128)S(1)} custom-call(f32[3,8,64,128]{3,2,1,0:T(8,128)S(1)} %copy-done.1, f32[3,72,128]{2,1,0:T(8,128)S(1)} %get-tuple-element.61.hx_ref, f32[176,128]{1,0:T(8,128)S(1)} %get-tuple-element.62.los_ref, f32[176,128]{1,0:T(8,128)S(1)} %get-tuple-element.63.his_ref, ...), custom_call_target="tpu_custom_call" | custom-call | tf_op jit(solution)/shard_map/other_one/pallas_call | solution.py:23
  45.5 1.4 %collective-permute-done.11.refs_1_ = f32[144,128]{1,0:T(8,128)S(1)} collective-permute-done((f32[144,128]{1,0:T(8,128)S(1)}, f32[144,128]{1,0:T(8,128)S(1)}, u32[]{:S(2)}, u32[]{:S(2)}) %collective-permute-start.11) | collective-permute-done | bytes 73760 | tf_op jit(solution)/shard_map/ppermute | solution.py:486
  47.0 0.6 collective-permute-done.13.refs_3_
  47.6 0.0 copy-start.10
  47.6 3.8 %collective-permute-start.14 = (f32[144,128]{1,0:T(8,128)S(1)}, f32[144,128]{1,0:T(8,128)S(1)}, u32[]{:S(2)}, u32[]{:S(2)}) collective-permute-start(f32[144,128]{1,0:T(8,128)S(1)} %add_y.2.refs_0_), channel_id=1, source_target_pairs={{0,4},{1,5},{2,6},{3,7},{4,0},{5,1},{6,2},{7,3},{8,12},{9,13},{10,... | collective-permute-start | bytes 221192 | tf_op jit(solution)/shard_map/ppermute | solution.py:470
  51.4 1.8 %other_one.3.refs_2_.d_ref = f32[8,72,256]{2,1,0:T(8,128)S(1)} custom-call(f32[3,8,64,128]{3,2,1,0:T(8,128)S(1)} %copy-done.1, f32[3,72,128]{2,1,0:T(8,128)S(1)} %get-tuple-element.61.hx_ref, f32[176,128]{1,0:T(8,128)S(1)} %get-tuple-element.62.los_ref, f32[176,128]{1,0:T(8,128)S(1)} %get-tuple-element.63.his_ref, ...), custom_call_target="tpu_custom_call" | custom-call | tf_op jit(solution)/shard_map/other_one/pallas_call | solution.py:23
  53.2 2.7 %collective-permute-done.14.refs_1_ = f32[144,128]{1,0:T(8,128)S(1)} collective-permute-done((f32[144,128]{1,0:T(8,128)S(1)}, f32[144,128]{1,0:T(8,128)S(1)}, u32[]{:S(2)}, u32[]{:S(2)}) %collective-permute-start.14) | collective-permute-done | bytes 73760 | tf_op jit(solution)/shard_map/ppermute | solution.py:470
  55.9 4.0 %collective-permute-start.17 = (f32[144,128]{1,0:T(8,128)S(1)}, f32[144,128]{1,0:T(8,128)S(1)}, u32[]{:S(2)}, u32[]{:S(2)}) collective-permute-start(f32[144,128]{1,0:T(8,128)S(1)} %add_z.2.t0), channel_id=1, source_target_pairs={{0,3},{1,0},{2,1},{3,2},{4,7},{5,4},{6,5},{7,6},{8,11},{9,8},{10,9... | collective-permute-start | bytes 221192 | tf_op jit(solution)/shard_map/ppermute | solution.py:474
  60.0 1.0 collective-permute-start.15
  60.9 1.9 %rest_one.1 = (f32[2,8,72,256]{3,2,1,0:T(8,128)S(1)}, f32[72,256]{1,0:T(8,128)S(1)}, f32[72,256]{1,0:T(8,128)S(1)}, f32[3,8,128]{2,1,0:T(8,128)S(1)}) custom-call(s32[5]{0:T(128)S(1)} %stack.15.ids_ref, f32[3]{0:T(128)S(1)} %copy-done.10, f32[4,64,128]{2,1,0:T(8,128)S(1)} %get-tuple-element.51.mask_ref, f32[8,72,256]{2,1,0:T(8,128)S(1)} %get-tuple-element.64.u_ref, ...), custom_call_target="tpu_custom_call" | custom-call | tf_op jit(solution)/shard_map/rest_one/pallas_call | solution.py:23
  62.9 3.1 %collective-permute-done.16.t2 = f32[144,128]{1,0:T(8,128)S(1)} collective-permute-done((f32[144,128]{1,0:T(8,128)S(1)}, f32[144,128]{1,0:T(8,128)S(1)}, u32[]{:S(2)}, u32[]{:S(2)}) %collective-permute-start.16) | collective-permute-done | bytes 73760 | tf_op jit(solution)/shard_map/ppermute | solution.py:474
  65.9 0.4 collective-permute-done.15.t1
  66.3 3.3 %biology_one.1 = (f32[8,72,256]{2,1,0:T(8,128)S(1)}, f32[8,72,256]{2,1,0:T(8,128)}, f32[8,72,256]{2,1,0:T(8,128)S(1)}, f32[72,256]{1,0:T(8,128)S(1)}, f32[8,64,1...) custom-call(s32[5]{0:T(128)S(1)} %stack.15.ids_ref, ...), custom_call_target="tpu_custom_call" | custom-call | tf_op jit(solution)/shard_map/biology_one/pallas_call | solution.py:23
  69.6 2.3 %collective-permute-start.19 = (f32[2,64,128]{2,1,0:T(8,128)S(1)}, f32[2,64,128]{2,1,0:T(8,128)S(1)}, u32[]{:S(2)}, u32[]{:S(2)}) collective-permute-start(f32[2,64,128]{2,1,0:T(8,128)S(1)} %get-tuple-element.86), channel_id=1, source_target_pairs={{0,2},{1,3},{2,0},{3,1},{4,6},{5,7},{6,4},{7,5},{8,10},{9,11},{10,... | collective-permute-start | bytes 196616 | tf_op jit(solution)/shard_map/ppermute | solution.py:486
  71.9 1.8 %collective-permute-start.20 = (f32[2,64,128]{2,1,0:T(8,128)S(1)}, f32[2,64,128]{2,1,0:T(8,128)S(1)}, u32[]{:S(2)}, u32[]{:S(2)}) collective-permute-start(f32[2,64,128]{2,1,0:T(8,128)S(1)} %get-tuple-element.87), channel_id=1, source_target_pairs={{0,3},{1,0},{2,1},{3,2},{4,7},{5,4},{6,5},{7,6},{8,11},{9,8},{10,9... | collective-permute-start | bytes 196616 | tf_op jit(solution)/shard_map/ppermute | solution.py:486
  73.8 1.5 %other_two.2.refs_4_.n_ref = f32[8,64,128]{2,1,0:T(8,128)S(1)} custom-call(f32[8,72,256]{2,1,0:T(8,128)S(1)} %get-tuple-element.79.c_ref, f32[8,64,256]{2,1,0:T(8,128)S(1)} %get-tuple-element.80.east_ref, f32[8,72,128]{2,1,0:T(8,128)S(1)} %get-tuple-element.81.north_ref, f32[8,72,256]{2,1,0:T(8,128)S(1)} %get-tuple-element.70.kv_ref, ...), custom_call_target="tpu_custom_call" | custom-call | tf_op jit(solution)/shard_map/other_two/pallas_call | solution.py:23
  75.3 0.5 collective-permute-done.18.refs_1_
  75.8 0.9 collective-permute-done.20.refs_3_
  76.7 3.2 %collective-permute-start.21 = (f32[2,64,128]{2,1,0:T(8,128)S(1)}, f32[2,64,128]{2,1,0:T(8,128)S(1)}, u32[]{:S(2)}, u32[]{:S(2)}) collective-permute-start(f32[2,64,128]{2,1,0:T(8,128)S(1)} %add_y.3.refs_0_), channel_id=1, source_target_pairs={{0,4},{1,5},{2,6},{3,7},{4,0},{5,1},{6,2},{7,3},{8,12},{9,13},{10,... | collective-permute-start | bytes 196616 | tf_op jit(solution)/shard_map/ppermute | solution.py:470
  79.9 1.5 %other_two.3.refs_2_.d_ref = f32[8,64,128]{2,1,0:T(8,128)S(1)} custom-call(f32[8,72,256]{2,1,0:T(8,128)S(1)} %get-tuple-element.83.c_ref, f32[8,64,256]{2,1,0:T(8,128)S(1)} %get-tuple-element.80.east_ref, f32[8,72,128]{2,1,0:T(8,128)S(1)} %get-tuple-element.81.north_ref, f32[8,72,256]{2,1,0:T(8,128)S(1)} %get-tuple-element.70.kv_ref, ...), custom_call_target="tpu_custom_call" | custom-call | tf_op jit(solution)/shard_map/other_two/pallas_call | solution.py:23
  81.4 4.5 %collective-permute-done.21.refs_1_ = f32[2,64,128]{2,1,0:T(8,128)S(1)} collective-permute-done((f32[2,64,128]{2,1,0:T(8,128)S(1)}, f32[2,64,128]{2,1,0:T(8,128)S(1)}, u32[]{:S(2)}, u32[]{:S(2)}) %collective-permute-start.21) | collective-permute-done | bytes 65568 | tf_op jit(solution)/shard_map/ppermute | solution.py:470
  85.9 2.8 %collective-permute-start.24 = (f32[2,64,128]{2,1,0:T(8,128)S(1)}, f32[2,64,128]{2,1,0:T(8,128)S(1)}, u32[]{:S(2)}, u32[]{:S(2)}) collective-permute-start(f32[2,64,128]{2,1,0:T(8,128)S(1)} %add_z.3.t0), channel_id=1, source_target_pairs={{0,3},{1,0},{2,1},{3,2},{4,7},{5,4},{6,5},{7,6},{8,11},{9,8},{10,9... | collective-permute-start | bytes 196616 | tf_op jit(solution)/shard_map/ppermute | solution.py:474
  88.6 0.7 collective-permute-start.23
  89.3 0.2 collective-permute-start.22
  89.6 1.4 %rest_two.1 = (f32[2,1,64,128]{3,2,1,0:T(8,128)}, f32[64,128]{1,0:T(8,128)S(1)}) custom-call(s32[5]{0:T(128)S(1)} %stack.15.ids_ref, f32[2,8,72,256]{3,2,1,0:T(8,128)S(1)} %get-tuple-element.78.cur_ref, f32[8,64,256]{2,1,0:T(8,128)S(1)} %get-tuple-element.80.east_ref, f32[8,72,128]{2,1,0:T(8,128)S(1)} %get-tuple-element.81.north_ref, ...), custom_call_target="tpu_custom_call" | custom-call | tf_op jit(solution)/shard_map/rest_two/pallas_call | solution.py:23
  91.0 0.2 collective-permute-done.24.t3
  91.1 3.3 %collective-permute-done.23.t2 = f32[2,64,128]{2,1,0:T(8,128)S(1)} collective-permute-done((f32[2,64,128]{2,1,0:T(8,128)S(1)}, f32[2,64,128]{2,1,0:T(8,128)S(1)}, u32[]{:S(2)}, u32[]{:S(2)}) %collective-permute-start.23) | collective-permute-done | bytes 65568 | tf_op jit(solution)/shard_map/ppermute | solution.py:474
  94.4 0.7 collective-permute-done.22.t1
  95.1 1.8 %biology_two.1 = (f32[3,8,64,128]{3,2,1,0:T(8,128)}, f32[1,64,128]{2,1,0:T(8,128)}) custom-call(s32[5]{0:T(128)S(1)} %stack.15.ids_ref, f32[3,8,128]{2,1,0:T(8,128)S(1)} %get-tuple-element.69.rate_ref, f32[8,64,128]{2,1,0:T(8,128)S(1)} %other_two.2.refs_4_.n_ref, f32[8,64,128]{2,1,0:T(8,128)S(1)} %get-tuple-element.82.p_ref, ...), custom_call_target="tpu_custom_call" | custom-call | tf_op jit(solution)/shard_map/biology_two/pallas_call | solution.py:23
  (27 shorter events, 0.1 us)
Async XLA Ops:
  0.6 13.8 %collective-permute-start = (f32[2,1,64,128]{3,2,1,0:T(8,128)}, f32[2,1,64,128]{3,2,1,0:T(8,128)S(1)}, u32[]{:S(2)}, u32[]{:S(2)}) collective-permute-start(f32[2,1,64,128]{3,2,1,0:T(8,128)} %flow_ref.3), channel_id=1, source_target_pairs={{0,4},{1,5},{2,6},{3,7},{4,0},{5,1},{6,2},{7,3},{8,12},{9,13},{10,... | collective-permute-start | bytes 196616 | tf_op jit(solution)/shard_map/ppermute | solution.py:470
  7.9 0.9 copy-start.4
  8.8 5.6 %copy-start.5 = (f32[2,1,64,128]{3,2,1,0:T(8,128)S(1)}, f32[2,1,64,128]{3,2,1,0:T(8,128)}, u32[]{:S(2)}) copy-start(f32[2,1,64,128]{3,2,1,0:T(8,128)} %flow_ref.3) | copy-start | bytes 196612
  8.9 1.1 %copy-start = (f32[3,8,64,128]{3,2,1,0:T(8,128)S(1)}, f32[3,8,64,128]{3,2,1,0:T(8,128)}, u32[]{:S(2)}) copy-start(f32[3,8,64,128]{3,2,1,0:T(8,128)} %c_ref.7) | copy-start | bytes 2359300
  10.0 0.9 copy-start.2
  11.0 0.8 copy-start.6
  11.7 0.8 copy-start.7
  12.5 0.8 copy-start.8
  13.2 0.8 copy-start.9
  14.0 22.0 %copy-start.1 = (f32[3,8,64,128]{3,2,1,0:T(8,128)S(1)}, f32[3,8,64,128]{3,2,1,0:T(8,128)}, u32[]{:S(2)}) copy-start(f32[3,8,64,128]{3,2,1,0:T(8,128)} %c_ref.7) | copy-start | bytes 2359300
  14.0 22.0 %copy-start.3 = (f32[8,64,128]{2,1,0:T(8,128)S(1)}, f32[8,64,128]{2,1,0:T(8,128)}, u32[]{:S(2)}) copy-start(f32[8,64,128]{2,1,0:T(8,128)} %dif_ref.3) | copy-start | bytes 786436
  14.5 6.8 %collective-permute-start.5 = (f32[3,64,128]{2,1,0:T(8,128)S(1)}, f32[3,64,128]{2,1,0:T(8,128)S(1)}, u32[]{:S(2)}, u32[]{:S(2)}) collective-permute-start(f32[3,64,128]{2,1,0:T(8,128)S(1)} %get-tuple-element.54), channel_id=1, source_target_pairs={{64,0},{65,1},{66,2},{67,3},{68,4},{69,5},{70,6},{71,7},{128,64},{... | collective-permute-start | bytes 294920 | tf_op jit(solution)/shard_map/ppermute | solution.py:455
  15.2 6.2 %collective-permute-start.4 = (f32[3,64,128]{2,1,0:T(8,128)S(1)}, f32[3,64,128]{2,1,0:T(8,128)S(1)}, u32[]{:S(2)}, u32[]{:S(2)}) collective-permute-start(f32[3,64,128]{2,1,0:T(8,128)S(1)} %get-tuple-element.54), channel_id=1, source_target_pairs={{0,64},{1,65},{2,66},{3,67},{4,68},{5,69},{6,70},{7,71},{64,128},{... | collective-permute-start | bytes 294920 | tf_op jit(solution)/shard_map/ppermute | solution.py:455
  16.6 13.9 %collective-permute-start.3 = (f32[2,128,128]{2,1,0:T(8,128)S(1)}, f32[2,128,128]{2,1,0:T(8,128)S(1)}, u32[]{:S(2)}, u32[]{:S(2)}) collective-permute-start(f32[2,128,128]{2,1,0:T(8,128)S(1)} %get-tuple-element.53.g0), channel_id=1, source_target_pairs={{0,3},{1,0},{2,1},{3,2},{4,7},{5,4},{6,5},{7,6},{8,11},{9,8},{10,9... | collective-permute-start | bytes 393224 | tf_op jit(solution)/shard_map/ppermute | solution.py:474
  19.6 11.2 %collective-permute-start.2 = (f32[2,128,128]{2,1,0:T(8,128)S(1)}, f32[2,128,128]{2,1,0:T(8,128)S(1)}, u32[]{:S(2)}, u32[]{:S(2)}) collective-permute-start(f32[2,128,128]{2,1,0:T(8,128)S(1)} %get-tuple-element.53.g0), channel_id=1, source_target_pairs={{0,2},{1,3},{2,0},{3,1},{4,6},{5,7},{6,4},{7,5},{8,10},{9,11},{10,... | collective-permute-start | bytes 393224 | tf_op jit(solution)/shard_map/ppermute | solution.py:474
  20.3 10.6 %collective-permute-start.1 = (f32[2,128,128]{2,1,0:T(8,128)S(1)}, f32[2,128,128]{2,1,0:T(8,128)S(1)}, u32[]{:S(2)}, u32[]{:S(2)}) collective-permute-start(f32[2,128,128]{2,1,0:T(8,128)S(1)} %get-tuple-element.53.g0), channel_id=1, source_target_pairs={{0,1},{1,2},{2,3},{3,0},{4,5},{5,6},{6,7},{7,4},{8,9},{9,10},{10,1... | collective-permute-start | bytes 393224 | tf_op jit(solution)/shard_map/ppermute | solution.py:474
  21.9 4.0 %collective-permute-start.6 = (f32[176,128]{1,0:T(8,128)S(1)}, f32[176,128]{1,0:T(8,128)S(1)}, u32[]{:S(2)}, u32[]{:S(2)}) collective-permute-start(f32[176,128]{1,0:T(8,128)S(1)} %get-tuple-element.58), channel_id=1, source_target_pairs={{0,8},{8,16},{16,24},{24,32},{32,40},{40,48},{48,56},{56,0},{1,9},... | collective-permute-start | bytes 270344 | tf_op jit(solution)/shard_map/ppermute | solution.py:462
  21.9 3.9 %collective-permute-start.7 = (f32[176,128]{1,0:T(8,128)S(1)}, f32[176,128]{1,0:T(8,128)S(1)}, u32[]{:S(2)}, u32[]{:S(2)}) collective-permute-start(f32[176,128]{1,0:T(8,128)S(1)} %get-tuple-element.59), channel_id=1, source_target_pairs={{8,0},{16,8},{24,16},{32,24},{40,32},{48,40},{56,48},{0,56},{9,1},... | collective-permute-start | bytes 270344 | tf_op jit(solution)/shard_map/ppermute | solution.py:462
  26.5 4.4 %collective-permute-start.10 = (f32[2,32,128]{2,1,0:T(8,128)S(1)}, f32[2,32,128]{2,1,0:T(8,128)S(1)}, u32[]{:S(2)}, u32[]{:S(2)}) collective-permute-start(f32[2,32,128]{2,1,0:T(8,128)S(1)} %get-tuple-element.60.e0), channel_id=1, source_target_pairs={{0,3},{1,0},{2,1},{3,2},{4,7},{5,4},{6,5},{7,6},{8,11},{9,8},{10,9... | collective-permute-start | bytes 98312 | tf_op jit(solution)/shard_map/ppermute | solution.py:474
  29.3 5.4 %collective-permute-start.9 = (f32[2,32,128]{2,1,0:T(8,128)S(1)}, f32[2,32,128]{2,1,0:T(8,128)S(1)}, u32[]{:S(2)}, u32[]{:S(2)}) collective-permute-start(f32[2,32,128]{2,1,0:T(8,128)S(1)} %get-tuple-element.60.e0), channel_id=1, source_target_pairs={{0,2},{1,3},{2,0},{3,1},{4,6},{5,7},{6,4},{7,5},{8,10},{9,11},{10,... | collective-permute-start | bytes 98312 | tf_op jit(solution)/shard_map/ppermute | solution.py:474
  30.5 5.5 %collective-permute-start.8 = (f32[2,32,128]{2,1,0:T(8,128)S(1)}, f32[2,32,128]{2,1,0:T(8,128)S(1)}, u32[]{:S(2)}, u32[]{:S(2)}) collective-permute-start(f32[2,32,128]{2,1,0:T(8,128)S(1)} %get-tuple-element.60.e0), channel_id=1, source_target_pairs={{0,1},{1,2},{2,3},{3,0},{4,5},{5,6},{6,7},{7,4},{8,9},{9,10},{10,1... | collective-permute-start | bytes 98312 | tf_op jit(solution)/shard_map/ppermute | solution.py:474
  39.8 7.2 %collective-permute-start.11 = (f32[144,128]{1,0:T(8,128)S(1)}, f32[144,128]{1,0:T(8,128)S(1)}, u32[]{:S(2)}, u32[]{:S(2)}) collective-permute-start(f32[144,128]{1,0:T(8,128)S(1)} %get-tuple-element.73), channel_id=1, source_target_pairs={{0,1},{1,2},{2,3},{3,0},{4,5},{5,6},{6,7},{7,4},{8,9},{9,10},{10,1... | collective-permute-start | bytes 221192 | tf_op jit(solution)/shard_map/ppermute | solution.py:486
  39.9 7.1 %collective-permute-start.12 = (f32[144,128]{1,0:T(8,128)S(1)}, f32[144,128]{1,0:T(8,128)S(1)}, u32[]{:S(2)}, u32[]{:S(2)}) collective-permute-start(f32[144,128]{1,0:T(8,128)S(1)} %get-tuple-element.74), channel_id=1, source_target_pairs={{0,2},{1,3},{2,0},{3,1},{4,6},{5,7},{6,4},{7,5},{8,10},{9,11},{10,... | collective-permute-start | bytes 221192 | tf_op jit(solution)/shard_map/ppermute | solution.py:486
  41.3 6.3 %collective-permute-start.13 = (f32[144,128]{1,0:T(8,128)S(1)}, f32[144,128]{1,0:T(8,128)S(1)}, u32[]{:S(2)}, u32[]{:S(2)}) collective-permute-start(f32[144,128]{1,0:T(8,128)S(1)} %get-tuple-element.75), channel_id=1, source_target_pairs={{0,3},{1,0},{2,1},{3,2},{4,7},{5,4},{6,5},{7,6},{8,11},{9,8},{10,9... | collective-permute-start | bytes 221192 | tf_op jit(solution)/shard_map/ppermute | solution.py:486
  47.6 13.4 %copy-start.10 = (f32[3]{0:T(128)S(1)}, f32[3]{0:T(128)}, u32[]{:S(2)}) copy-start(f32[3]{0:T(128)} %rate_ref.1) | copy-start | bytes 40
  47.6 8.3 %collective-permute-start.14 = (f32[144,128]{1,0:T(8,128)S(1)}, f32[144,128]{1,0:T(8,128)S(1)}, u32[]{:S(2)}, u32[]{:S(2)}) collective-permute-start(f32[144,128]{1,0:T(8,128)S(1)} %add_y.2.refs_0_), channel_id=1, source_target_pairs={{0,4},{1,5},{2,6},{3,7},{4,0},{5,1},{6,2},{7,3},{8,12},{9,13},{10,... | collective-permute-start | bytes 221192 | tf_op jit(solution)/shard_map/ppermute | solution.py:470
  55.9 6.9 %collective-permute-start.17 = (f32[144,128]{1,0:T(8,128)S(1)}, f32[144,128]{1,0:T(8,128)S(1)}, u32[]{:S(2)}, u32[]{:S(2)}) collective-permute-start(f32[144,128]{1,0:T(8,128)S(1)} %add_z.2.t0), channel_id=1, source_target_pairs={{0,3},{1,0},{2,1},{3,2},{4,7},{5,4},{6,5},{7,6},{8,11},{9,8},{10,9... | collective-permute-start | bytes 221192 | tf_op jit(solution)/shard_map/ppermute | solution.py:474
  60.0 6.0 %collective-permute-start.16 = (f32[144,128]{1,0:T(8,128)S(1)}, f32[144,128]{1,0:T(8,128)S(1)}, u32[]{:S(2)}, u32[]{:S(2)}) collective-permute-start(f32[144,128]{1,0:T(8,128)S(1)} %add_z.2.t0), channel_id=1, source_target_pairs={{0,2},{1,3},{2,0},{3,1},{4,6},{5,7},{6,4},{7,5},{8,10},{9,11},{10,... | collective-permute-start | bytes 221192 | tf_op jit(solution)/shard_map/ppermute | solution.py:474
  60.0 6.4 %collective-permute-start.15 = (f32[144,128]{1,0:T(8,128)S(1)}, f32[144,128]{1,0:T(8,128)S(1)}, u32[]{:S(2)}, u32[]{:S(2)}) collective-permute-start(f32[144,128]{1,0:T(8,128)S(1)} %add_z.2.t0), channel_id=1, source_target_pairs={{0,1},{1,2},{2,3},{3,0},{4,5},{5,6},{6,7},{7,4},{8,9},{9,10},{10,1... | collective-permute-start | bytes 221192 | tf_op jit(solution)/shard_map/ppermute | solution.py:474
  69.6 6.2 %collective-permute-start.18 = (f32[2,64,128]{2,1,0:T(8,128)S(1)}, f32[2,64,128]{2,1,0:T(8,128)S(1)}, u32[]{:S(2)}, u32[]{:S(2)}) collective-permute-start(f32[2,64,128]{2,1,0:T(8,128)S(1)} %get-tuple-element.85), channel_id=1, source_target_pairs={{0,1},{1,2},{2,3},{3,0},{4,5},{5,6},{6,7},{7,4},{8,9},{9,10},{10,1... | collective-permute-start | bytes 196616 | tf_op jit(solution)/shard_map/ppermute | solution.py:486
  69.6 6.2 %collective-permute-start.19 = (f32[2,64,128]{2,1,0:T(8,128)S(1)}, f32[2,64,128]{2,1,0:T(8,128)S(1)}, u32[]{:S(2)}, u32[]{:S(2)}) collective-permute-start(f32[2,64,128]{2,1,0:T(8,128)S(1)} %get-tuple-element.86), channel_id=1, source_target_pairs={{0,2},{1,3},{2,0},{3,1},{4,6},{5,7},{6,4},{7,5},{8,10},{9,11},{10,... | collective-permute-start | bytes 196616 | tf_op jit(solution)/shard_map/ppermute | solution.py:486
  71.9 4.7 %collective-permute-start.20 = (f32[2,64,128]{2,1,0:T(8,128)S(1)}, f32[2,64,128]{2,1,0:T(8,128)S(1)}, u32[]{:S(2)}, u32[]{:S(2)}) collective-permute-start(f32[2,64,128]{2,1,0:T(8,128)S(1)} %get-tuple-element.87), channel_id=1, source_target_pairs={{0,3},{1,0},{2,1},{3,2},{4,7},{5,4},{6,5},{7,6},{8,11},{9,8},{10,9... | collective-permute-start | bytes 196616 | tf_op jit(solution)/shard_map/ppermute | solution.py:486
  76.7 9.2 %collective-permute-start.21 = (f32[2,64,128]{2,1,0:T(8,128)S(1)}, f32[2,64,128]{2,1,0:T(8,128)S(1)}, u32[]{:S(2)}, u32[]{:S(2)}) collective-permute-start(f32[2,64,128]{2,1,0:T(8,128)S(1)} %add_y.3.refs_0_), channel_id=1, source_target_pairs={{0,4},{1,5},{2,6},{3,7},{4,0},{5,1},{6,2},{7,3},{8,12},{9,13},{10,... | collective-permute-start | bytes 196616 | tf_op jit(solution)/shard_map/ppermute | solution.py:470
  85.9 5.3 %collective-permute-start.24 = (f32[2,64,128]{2,1,0:T(8,128)S(1)}, f32[2,64,128]{2,1,0:T(8,128)S(1)}, u32[]{:S(2)}, u32[]{:S(2)}) collective-permute-start(f32[2,64,128]{2,1,0:T(8,128)S(1)} %add_z.3.t0), channel_id=1, source_target_pairs={{0,3},{1,0},{2,1},{3,2},{4,7},{5,4},{6,5},{7,6},{8,11},{9,8},{10,9... | collective-permute-start | bytes 196616 | tf_op jit(solution)/shard_map/ppermute | solution.py:474
  88.6 5.8 %collective-permute-start.23 = (f32[2,64,128]{2,1,0:T(8,128)S(1)}, f32[2,64,128]{2,1,0:T(8,128)S(1)}, u32[]{:S(2)}, u32[]{:S(2)}) collective-permute-start(f32[2,64,128]{2,1,0:T(8,128)S(1)} %add_z.3.t0), channel_id=1, source_target_pairs={{0,2},{1,3},{2,0},{3,1},{4,6},{5,7},{6,4},{7,5},{8,10},{9,11},{10,... | collective-permute-start | bytes 196616 | tf_op jit(solution)/shard_map/ppermute | solution.py:474
  89.3 5.8 %collective-permute-start.22 = (f32[2,64,128]{2,1,0:T(8,128)S(1)}, f32[2,64,128]{2,1,0:T(8,128)S(1)}, u32[]{:S(2)}, u32[]{:S(2)}) collective-permute-start(f32[2,64,128]{2,1,0:T(8,128)S(1)} %add_z.3.t0), channel_id=1, source_target_pairs={{0,1},{1,2},{2,3},{3,0},{4,5},{5,6},{6,7},{7,4},{8,9},{9,10},{10,1... | collective-permute-start | bytes 196616 | tf_op jit(solution)/shard_map/ppermute | solution.py:474

commit v4 on v3

--- a/solution.py
+++ b/solution.py
@@ -371,9 +371,20 @@
     out_ref[1, 0] = new_v[:R, :W]
 
 
-def biology(ids_ref, rate_ref, mixes, absorb, solar, wx, tadv_ref, outs, tau_ref, a_ref):
+def exchanges(rate_ref, n_ref, p_ref, d_ref, grow_ref, n_out, p_out, d_out):
+    mu, mortal, recycle = (rate_ref[t, 0:1, 0:1] for t in range(NT))
+    for l in range(NL):
+        n, p, d = n_ref[l], p_ref[l], d_ref[l]
+        dead = mortal * p
+        back = recycle * d
+        grow_ref[l] = mu * p * n / (jnp.abs(n) + 0.5)
+        n_out[l] = n + back
+        p_out[l] = p - dead
+        d_out[l] = d + dead - back
+
+
+def biology(ids_ref, mixes, absorb, solar, wx, tadv_ref, outs, tau_ref, a_ref):
     sea, depth = wx
-    mu, mortal, recycle = (rate_ref[t, 0:1, 0:1] for t in range(NT))
     tau = jnp.zeros(solar.shape, f32)
     for l in range(NL):
         a = 0.04 + 0.03 * absorb(l)
@@ -381,13 +392,10 @@
         tau_ref[l] = tau
         a_ref[l] = a
         wet = jnp.where(float(l) < depth, sea, 0.0)
-        n, p, d = mixes[0][l], mixes[1][l], mixes[2][l]
-        uptake = mu * (light / (light + 0.3)) * p * n / (jnp.abs(n) + 0.5)
-        dead = mortal * p
-        back = recycle * d
-        outs[0][l] = wet * (n - uptake + back)
-        outs[1][l] = wet * (p + uptake - dead)
-        outs[2][l] = wet * (d + dead - back)
+        uptake = light / (light + 0.3) * mixes[0][l]
+        outs[0][l] = wet * (mixes[1][l] - uptake)
+        outs[1][l] = wet * (mixes[2][l] + uptake)
+        outs[2][l] = wet * mixes[3][l]
         tau = tau + a
     own = ids_ref[0]
     tau, a = tau_ref[own], a_ref[own]
@@ -397,7 +405,7 @@
 
 
 def biology_one(
-    ids_ref, rate_ref, n_ref, p_ref, d_ref, t0, t1, t2, t3, sun_ref, wx_ref, tadv_ref, cur_ref,
+    ids_ref, grow_ref, n_ref, p_ref, d_ref, t0, t1, t2, t3, sun_ref, wx_ref, tadv_ref, cur_ref,
     kv_ref, n_out, p_out, d_out, temp_ref, mix_ref, a0, a1, a2, a3, east_ref, north_ref,
     sum_ref, cols_ref, turn_ref, slot_ref, tau_ref, a_ref, adv_ref,
 ):
@@ -420,7 +428,7 @@
         return slot[...]
 
     temp_ref[...] = biology(
-        ids_ref, rate_ref, (n_ref, p_ref, d_ref), absorb, sun_ref[...], (wx_ref[0], wx_ref[1]),
+        ids_ref, (grow_ref, n_ref, p_ref, d_ref), absorb, sun_ref[...], (wx_ref[0], wx_ref[1]),
         tadv_ref, (n_out, p_out, d_out), tau_ref, a_ref,
     )
     plankton_two(
@@ -430,7 +438,7 @@
 
 
 def biology_two(
-    ids_ref, rate_ref, n_ref, p_ref, d_ref, t0, t1, t2, t3, sun_ref, wx_ref, tadv_ref,
+    ids_ref, grow_ref, n_ref, p_ref, d_ref, t0, t1, t2, t3, sun_ref, wx_ref, tadv_ref,
     c_ref, temp_ref, sum_ref, tau_ref, a_ref,
 ):
     y = ids_ref[0] & 3
@@ -438,7 +446,7 @@
         sum_ref[pl.ds(2 * ((y + 4 - k) & 3), 2)] = ref[...]
     wx = (wx_ref[0, 0:R, 0:W], wx_ref[1, 0:R, 0:W])
     temp_ref[0] = biology(
-        ids_ref, rate_ref, (n_ref, p_ref, d_ref), lambda l: sum_ref[l], sun_ref[0:R, 0:W], wx,
+        ids_ref, (grow_ref, n_ref, p_ref, d_ref), lambda l: sum_ref[l], sun_ref[0:R, 0:W], wx,
         tadv_ref, [c_ref.at[t] for t in range(NT)], tau_ref, a_ref,
     )
 
@@ -542,12 +550,13 @@
         rest_one, "rest_one", [(2, NL, ER, EW), ext, ext, (NT, 8, W)], 2, [ext]
     )(ids, rates, masks, u, v, east, north, wx, hx, los, his)
     sums = total((a0, a1, a2, a3), nutri, detri)
+    ready = call(exchanges, "exchange_one", [deep] * 4, 0)(pace, nutri, plank, detri)
     half = (2, R, W)
     n, p, d, heated, plank, a0, a1, a2, a3, east, north = call(
         biology_one, "biology_one",
         [deep, deep, deep, ext, col, half, half, half, half, (NL, R, EW), (NL, ER, W)], 1,
         [(4, PART, W), (4 * NL, W), (ER, W), deep, deep, deep, col],
-    )(ids, pace, nutri, plank, detri, *sums, sun, wx, tadv, cur, kv)
+    )(ids, *ready, *sums, sun, wx, tadv, cur, kv)
     nutri, detri = (
         call(other_two, "other_two", [col], 0, [col])(q, east, north, kv, wx)[0] for q in (n, d)
     )
@@ -555,9 +564,10 @@
         ids, cur, east, north, wx, heated
     )
     sums = total((a0, a1, a2, a3), nutri, detri)
+    ready = call(exchanges, "exchange_two", [col] * 4, 0)(pace, nutri, plank, detri)
     c, last_temp = call(
         biology_two, "biology_two", [(NT, NL, R, W), (1, R, W)], 1, [col, col, col]
-    )(ids, pace, nutri, plank, detri, *sums, sun, wx, tadv)
+    )(ids, *ready, *sums, sun, wx, tadv)
     return c, currents, last_temp
 
 

time: 97.3 us -> 97.3 us (level)
    pallas_call x18 -> x20, Pallas kernels: 20.6 us -> 21.2 us  [run(): pl.pallas_call(body, name=name, out_shape=[jax.ShapeDtypeStruct(s, f32) f...]
  transfers between devices with their start and end apart: 25 -> 25, of which waited for: 14 -> 13; matrix products, arithmetic and copies ran while one was open for 0% -> 0% of each run, Pallas kernels for 12% -> 13%
where the time goes in v4:
time: 97.3 us; the launch traced here: 96.9 us
  starting transfers between devices  43.9 us (45%)
  waiting for transfers between devices  24.9 us (26%)
  Pallas kernels  21.2 us (22%)
  local copies, waits for them, and re-layouts  6.08 us (6%)
    pallas_call x20, Pallas kernels, run(): pl.pallas_call(body, name=name, out_shape=[jax.ShapeDtypeStruct(s, f32) f...  21.2 us
    ppermute x12, starting transfers between devices, spread_y(): return [value] + [lax.ppermute(value, 'tracer', by_y(k)) for k in (1, 2, 3)]  17.7 us
    ppermute x3, starting transfers between devices, over_z(): return lax.ppermute(value, 'tracer', [(i, i ^ 4) for i in range(8)])  14.3 us
    ppermute x12, waiting for transfers between devices, spread_y(): return [value] + [lax.ppermute(value, 'tracer', by_y(k)) for k in (1, 2, 3)]  12.2 us
    ppermute x6, starting transfers between devices, total(): lax.ppermute(parts[k], 'tracer', by_y(k))  8.02 us
    ppermute x3, waiting for transfers between devices, over_z(): return lax.ppermute(value, 'tracer', [(i, i ^ 4) for i in range(8)])  7.15 us
    unnamed x22, local copies, waits for them, and re-layouts  6 us
    ppermute x6, waiting for transfers between devices, total(): lax.ppermute(parts[k], 'tracer', by_y(k))  3.38 us
  transfers between devices with their start and end apart: 25, of which 13 were waited for; matrix products, arithmetic and copies ran while one was open for 0% of the time, Pallas kernels for 13%

profile of v4, /device:TPU:2, one launch (start us, length us, event | category | flops | bytes accessed | tf_op | source)
XLA Modules:
  0.0 96.9 jit_solution(8838302524912179090)
XLA Ops:
  0.6 7.3 %collective-permute-start = (f32[2,1,64,128]{3,2,1,0:T(8,128)}, f32[2,1,64,128]{3,2,1,0:T(8,128)S(1)}, u32[]{:S(2)}, u32[]{:S(2)}) collective-permute-start(f32[2,1,64,128]{3,2,1,0:T(8,128)} %flow_ref.3), channel_id=1, source_target_pairs={{0,4},{1,5},{2,6},{3,7},{4,0},{5,1},{6,2},{7,3},{8,12},{9,13},{10,... | collective-permute-start | bytes 196616 | tf_op jit(solution)/shard_map/ppermute | solution.py:478
  7.9 0.9 copy-done.4
  8.8 0.1 pack_flow.1
  8.9 0.0 copy-start
  8.9 1.1 %copy-done = f32[3,8,64,128]{3,2,1,0:T(8,128)S(1)} copy-done((f32[3,8,64,128]{3,2,1,0:T(8,128)S(1)}, f32[3,8,64,128]{3,2,1,0:T(8,128)}, u32[]{:S(2)}) %copy-start) | copy-done | bytes 786456
  10.0 0.9 copy-done.2
  11.0 0.8 copy-done.6
  11.7 0.8 copy-done.7
  12.5 0.8 copy-done.8
  13.2 0.8 copy-done.9
  14.0 0.4 pack_one.1
  14.4 0.0 collective-permute-done.other_ref
  14.4 0.1 pack_two.1
  14.5 0.6 collective-permute-start.5
  15.2 1.5 %collective-permute-start.4 = (f32[3,64,128]{2,1,0:T(8,128)S(1)}, f32[3,64,128]{2,1,0:T(8,128)S(1)}, u32[]{:S(2)}, u32[]{:S(2)}) collective-permute-start(f32[3,64,128]{2,1,0:T(8,128)S(1)} %get-tuple-element.62), channel_id=1, source_target_pairs={{0,64},{1,65},{2,66},{3,67},{4,68},{5,69},{6,70},{7,71},{64,128},{... | collective-permute-start | bytes 294920 | tf_op jit(solution)/shard_map/ppermute | solution.py:463
  16.6 3.0 %collective-permute-start.3 = (f32[2,128,128]{2,1,0:T(8,128)S(1)}, f32[2,128,128]{2,1,0:T(8,128)S(1)}, u32[]{:S(2)}, u32[]{:S(2)}) collective-permute-start(f32[2,128,128]{2,1,0:T(8,128)S(1)} %get-tuple-element.61.g0), channel_id=1, source_target_pairs={{0,3},{1,0},{2,1},{3,2},{4,7},{5,4},{6,5},{7,6},{8,11},{9,8},{10,9... | collective-permute-start | bytes 393224 | tf_op jit(solution)/shard_map/ppermute | solution.py:482
  19.6 0.6 collective-permute-start.2
  20.3 1.0 %collective-permute-start.1 = (f32[2,128,128]{2,1,0:T(8,128)S(1)}, f32[2,128,128]{2,1,0:T(8,128)S(1)}, u32[]{:S(2)}, u32[]{:S(2)}) collective-permute-start(f32[2,128,128]{2,1,0:T(8,128)S(1)} %get-tuple-element.61.g0), channel_id=1, source_target_pairs={{0,1},{1,2},{2,3},{3,0},{4,5},{5,6},{6,7},{7,4},{8,9},{9,10},{10,1... | collective-permute-start | bytes 393224 | tf_op jit(solution)/shard_map/ppermute | solution.py:482
  21.2 0.1 stack.15.ids_ref
  21.3 0.6 pack_y.1
  21.9 0.0 collective-permute-start.6
  21.9 1.7 %collective-permute-start.7 = (f32[176,128]{1,0:T(8,128)S(1)}, f32[176,128]{1,0:T(8,128)S(1)}, u32[]{:S(2)}, u32[]{:S(2)}) collective-permute-start(f32[176,128]{1,0:T(8,128)S(1)} %get-tuple-element.67), channel_id=1, source_target_pairs={{8,0},{16,8},{24,16},{32,24},{40,32},{48,40},{56,48},{0,56},{9,1},... | collective-permute-start | bytes 270344 | tf_op jit(solution)/shard_map/ppermute | solution.py:470
  23.7 2.2 %collective-permute-done.6.lo_ref = f32[176,128]{1,0:T(8,128)S(1)} collective-permute-done((f32[176,128]{1,0:T(8,128)S(1)}, f32[176,128]{1,0:T(8,128)S(1)}, u32[]{:S(2)}, u32[]{:S(2)}) %collective-permute-start.6) | collective-permute-done | bytes 90144 | tf_op jit(solution)/shard_map/ppermute | solution.py:470
  25.9 0.6 extend.1
  26.5 2.8 %collective-permute-start.10 = (f32[2,32,128]{2,1,0:T(8,128)S(1)}, f32[2,32,128]{2,1,0:T(8,128)S(1)}, u32[]{:S(2)}, u32[]{:S(2)}) collective-permute-start(f32[2,32,128]{2,1,0:T(8,128)S(1)} %get-tuple-element.68.e0), channel_id=1, source_target_pairs={{0,3},{1,0},{2,1},{3,2},{4,7},{5,4},{6,5},{7,6},{8,11},{9,8},{10,9... | collective-permute-start | bytes 98312 | tf_op jit(solution)/shard_map/ppermute | solution.py:482
  29.3 1.3 %collective-permute-start.9 = (f32[2,32,128]{2,1,0:T(8,128)S(1)}, f32[2,32,128]{2,1,0:T(8,128)S(1)}, u32[]{:S(2)}, u32[]{:S(2)}) collective-permute-start(f32[2,32,128]{2,1,0:T(8,128)S(1)} %get-tuple-element.68.e0), channel_id=1, source_target_pairs={{0,2},{1,3},{2,0},{3,1},{4,6},{5,7},{6,4},{7,5},{8,10},{9,11},{10,... | collective-permute-start | bytes 98312 | tf_op jit(solution)/shard_map/ppermute | solution.py:482
  30.5 0.3 collective-permute-start.8
  30.9 3.8 %collective-permute-done.9.e2 = f32[2,32,128]{2,1,0:T(8,128)S(1)} collective-permute-done((f32[2,32,128]{2,1,0:T(8,128)S(1)}, f32[2,32,128]{2,1,0:T(8,128)S(1)}, u32[]{:S(2)}, u32[]{:S(2)}) %collective-permute-start.9) | collective-permute-done | bytes 32800 | tf_op jit(solution)/shard_map/ppermute | solution.py:482
  34.7 1.3 %collective-permute-done.8.e1 = f32[2,32,128]{2,1,0:T(8,128)S(1)} collective-permute-done((f32[2,32,128]{2,1,0:T(8,128)S(1)}, f32[2,32,128]{2,1,0:T(8,128)S(1)}, u32[]{:S(2)}, u32[]{:S(2)}) %collective-permute-start.8) | collective-permute-done | bytes 32800 | tf_op jit(solution)/shard_map/ppermute | solution.py:482
  36.0 3.8 %plankton_one.1 = (f32[8,72,256]{2,1,0:T(8,128)S(1)}, f32[144,128]{1,0:T(8,128)S(1)}, f32[144,128]{1,0:T(8,128)S(1)}, f32[144,128]{1,0:T(8,128)S(1)}, f32[144,12...) custom-call(s32[5]{0:T(128)S(1)} %stack.15.ids_ref, ...), custom_call_target="tpu_custom_call" | custom-call | tf_op jit(solution)/shard_map/plankton_one/pallas_call | solution.py:23
  39.8 0.1 collective-permute-start.11
  39.9 1.4 %collective-permute-start.12 = (f32[144,128]{1,0:T(8,128)S(1)}, f32[144,128]{1,0:T(8,128)S(1)}, u32[]{:S(2)}, u32[]{:S(2)}) collective-permute-start(f32[144,128]{1,0:T(8,128)S(1)} %get-tuple-element.86), channel_id=1, source_target_pairs={{0,2},{1,3},{2,0},{3,1},{4,6},{5,7},{6,4},{7,5},{8,10},{9,11},{10,... | collective-permute-start | bytes 221192 | tf_op jit(solution)/shard_map/ppermute | solution.py:494
  41.3 2.4 %collective-permute-start.13 = (f32[144,128]{1,0:T(8,128)S(1)}, f32[144,128]{1,0:T(8,128)S(1)}, u32[]{:S(2)}, u32[]{:S(2)}) collective-permute-start(f32[144,128]{1,0:T(8,128)S(1)} %get-tuple-element.87), channel_id=1, source_target_pairs={{0,3},{1,0},{2,1},{3,2},{4,7},{5,4},{6,5},{7,6},{8,11},{9,8},{10,9... | collective-permute-start | bytes 221192 | tf_op jit(solution)/shard_map/ppermute | solution.py:494
  43.7 1.8 %other_one.2.n_ref.refs_4_ = f32[8,72,256]{2,1,0:T(8,128)S(1)} custom-call(f32[3,8,64,128]{3,2,1,0:T(8,128)S(1)} %copy-done.1, f32[3,72,128]{2,1,0:T(8,128)S(1)} %get-tuple-element.69.hx_ref, f32[176,128]{1,0:T(8,128)S(1)} %get-tuple-element.70.los_ref, f32[176,128]{1,0:T(8,128)S(1)} %get-tuple-element.71.his_ref, ...), custom_call_target="tpu_custom_call" | custom-call | tf_op jit(solution)/shard_map/other_one/pallas_call | solution.py:23
  45.5 1.4 %collective-permute-done.11.refs_1_ = f32[144,128]{1,0:T(8,128)S(1)} collective-permute-done((f32[144,128]{1,0:T(8,128)S(1)}, f32[144,128]{1,0:T(8,128)S(1)}, u32[]{:S(2)}, u32[]{:S(2)}) %collective-permute-start.11) | collective-permute-done | bytes 73760 | tf_op jit(solution)/shard_map/ppermute | solution.py:494
  47.0 0.6 collective-permute-done.13.refs_3_
  47.6 0.0 copy-start.10
  47.6 3.8 %collective-permute-start.14 = (f32[144,128]{1,0:T(8,128)S(1)}, f32[144,128]{1,0:T(8,128)S(1)}, u32[]{:S(2)}, u32[]{:S(2)}) collective-permute-start(f32[144,128]{1,0:T(8,128)S(1)} %add_y.2.refs_0_), channel_id=1, source_target_pairs={{0,4},{1,5},{2,6},{3,7},{4,0},{5,1},{6,2},{7,3},{8,12},{9,13},{10,... | collective-permute-start | bytes 221192 | tf_op jit(solution)/shard_map/ppermute | solution.py:478
  51.4 1.8 %other_one.3.d_ref.refs_2_ = f32[8,72,256]{2,1,0:T(8,128)S(1)} custom-call(f32[3,8,64,128]{3,2,1,0:T(8,128)S(1)} %copy-done.1, f32[3,72,128]{2,1,0:T(8,128)S(1)} %get-tuple-element.69.hx_ref, f32[176,128]{1,0:T(8,128)S(1)} %get-tuple-element.70.los_ref, f32[176,128]{1,0:T(8,128)S(1)} %get-tuple-element.71.his_ref, ...), custom_call_target="tpu_custom_call" | custom-call | tf_op jit(solution)/shard_map/other_one/pallas_call | solution.py:23
  53.2 2.7 %collective-permute-done.14.refs_1_ = f32[144,128]{1,0:T(8,128)S(1)} collective-permute-done((f32[144,128]{1,0:T(8,128)S(1)}, f32[144,128]{1,0:T(8,128)S(1)}, u32[]{:S(2)}, u32[]{:S(2)}) %collective-permute-start.14) | collective-permute-done | bytes 73760 | tf_op jit(solution)/shard_map/ppermute | solution.py:478
  55.9 4.0 %collective-permute-start.17 = (f32[144,128]{1,0:T(8,128)S(1)}, f32[144,128]{1,0:T(8,128)S(1)}, u32[]{:S(2)}, u32[]{:S(2)}) collective-permute-start(f32[144,128]{1,0:T(8,128)S(1)} %add_z.2.t0), channel_id=1, source_target_pairs={{0,3},{1,0},{2,1},{3,2},{4,7},{5,4},{6,5},{7,6},{8,11},{9,8},{10,9... | collective-permute-start | bytes 221192 | tf_op jit(solution)/shard_map/ppermute | solution.py:482
  60.0 1.0 collective-permute-start.15
  60.9 1.9 %rest_one.1 = (f32[2,8,72,256]{3,2,1,0:T(8,128)S(1)}, f32[72,256]{1,0:T(8,128)S(1)}, f32[72,256]{1,0:T(8,128)S(1)}, f32[3,8,128]{2,1,0:T(8,128)S(1)}) custom-call(s32[5]{0:T(128)S(1)} %stack.15.ids_ref, f32[3]{0:T(128)S(1)} %copy-done.10, f32[4,64,128]{2,1,0:T(8,128)S(1)} %get-tuple-element.59.mask_ref, f32[8,72,256]{2,1,0:T(8,128)S(1)} %get-tuple-element.72.u_ref, ...), custom_call_target="tpu_custom_call" | custom-call | tf_op jit(solution)/shard_map/rest_one/pallas_call | solution.py:23
  62.9 0.4 exchange_one.1
  63.3 2.7 %collective-permute-done.16.t2 = f32[144,128]{1,0:T(8,128)S(1)} collective-permute-done((f32[144,128]{1,0:T(8,128)S(1)}, f32[144,128]{1,0:T(8,128)S(1)}, u32[]{:S(2)}, u32[]{:S(2)}) %collective-permute-start.16) | collective-permute-done | bytes 73760 | tf_op jit(solution)/shard_map/ppermute | solution.py:482
  65.9 0.4 collective-permute-done.15.t1
  66.3 3.4 %biology_one.1 = (f32[8,72,256]{2,1,0:T(8,128)S(1)}, f32[8,72,256]{2,1,0:T(8,128)}, f32[8,72,256]{2,1,0:T(8,128)S(1)}, f32[72,256]{1,0:T(8,128)S(1)}, f32[8,64,1...) custom-call(s32[5]{0:T(128)S(1)} %stack.15.ids_ref, ...), custom_call_target="tpu_custom_call" | custom-call | tf_op jit(solution)/shard_map/biology_one/pallas_call | solution.py:23
  69.7 2.3 %collective-permute-start.19 = (f32[2,64,128]{2,1,0:T(8,128)S(1)}, f32[2,64,128]{2,1,0:T(8,128)S(1)}, u32[]{:S(2)}, u32[]{:S(2)}) collective-permute-start(f32[2,64,128]{2,1,0:T(8,128)S(1)} %get-tuple-element.102), channel_id=1, source_target_pairs={{0,2},{1,3},{2,0},{3,1},{4,6},{5,7},{6,4},{7,5},{8,10},{9,11},{10,... | collective-permute-start | bytes 196616 | tf_op jit(solution)/shard_map/ppermute | solution.py:494
  72.1 1.8 %collective-permute-start.20 = (f32[2,64,128]{2,1,0:T(8,128)S(1)}, f32[2,64,128]{2,1,0:T(8,128)S(1)}, u32[]{:S(2)}, u32[]{:S(2)}) collective-permute-start(f32[2,64,128]{2,1,0:T(8,128)S(1)} %get-tuple-element.103), channel_id=1, source_target_pairs={{0,3},{1,0},{2,1},{3,2},{4,7},{5,4},{6,5},{7,6},{8,11},{9,8},{10,9... | collective-permute-start | bytes 196616 | tf_op jit(solution)/shard_map/ppermute | solution.py:494
  73.9 1.5 %other_two.2.n_ref.refs_4_ = f32[8,64,128]{2,1,0:T(8,128)S(1)} custom-call(f32[8,72,256]{2,1,0:T(8,128)S(1)} %get-tuple-element.91.c_ref, f32[8,64,256]{2,1,0:T(8,128)S(1)} %get-tuple-element.92.east_ref, f32[8,72,128]{2,1,0:T(8,128)S(1)} %get-tuple-element.93.north_ref, f32[8,72,256]{2,1,0:T(8,128)S(1)} %get-tuple-element.78.kv_ref, ...), custom_call_target="tpu_custom_call" | custom-call | tf_op jit(solution)/shard_map/other_two/pallas_call | solution.py:23
  75.4 0.5 collective-permute-done.18.refs_1_
  75.9 0.9 collective-permute-done.20.refs_3_
  76.8 3.2 %collective-permute-start.21 = (f32[2,64,128]{2,1,0:T(8,128)S(1)}, f32[2,64,128]{2,1,0:T(8,128)S(1)}, u32[]{:S(2)}, u32[]{:S(2)}) collective-permute-start(f32[2,64,128]{2,1,0:T(8,128)S(1)} %add_y.3.refs_0_), channel_id=1, source_target_pairs={{0,4},{1,5},{2,6},{3,7},{4,0},{5,1},{6,2},{7,3},{8,12},{9,13},{10,... | collective-permute-start | bytes 196616 | tf_op jit(solution)/shard_map/ppermute | solution.py:478
  80.0 1.5 %other_two.3.d_ref.refs_2_ = f32[8,64,128]{2,1,0:T(8,128)S(1)} custom-call(f32[8,72,256]{2,1,0:T(8,128)S(1)} %get-tuple-element.95.c_ref, f32[8,64,256]{2,1,0:T(8,128)S(1)} %get-tuple-element.92.east_ref, f32[8,72,128]{2,1,0:T(8,128)S(1)} %get-tuple-element.93.north_ref, f32[8,72,256]{2,1,0:T(8,128)S(1)} %get-tuple-element.78.kv_ref, ...), custom_call_target="tpu_custom_call" | custom-call | tf_op jit(solution)/shard_map/other_two/pallas_call | solution.py:23
  81.5 4.5 %collective-permute-done.21.refs_1_ = f32[2,64,128]{2,1,0:T(8,128)S(1)} collective-permute-done((f32[2,64,128]{2,1,0:T(8,128)S(1)}, f32[2,64,128]{2,1,0:T(8,128)S(1)}, u32[]{:S(2)}, u32[]{:S(2)}) %collective-permute-start.21) | collective-permute-done | bytes 65568 | tf_op jit(solution)/shard_map/ppermute | solution.py:478
  86.0 2.8 %collective-permute-start.24 = (f32[2,64,128]{2,1,0:T(8,128)S(1)}, f32[2,64,128]{2,1,0:T(8,128)S(1)}, u32[]{:S(2)}, u32[]{:S(2)}) collective-permute-start(f32[2,64,128]{2,1,0:T(8,128)S(1)} %add_z.3.t0), channel_id=1, source_target_pairs={{0,3},{1,0},{2,1},{3,2},{4,7},{5,4},{6,5},{7,6},{8,11},{9,8},{10,9... | collective-permute-start | bytes 196616 | tf_op jit(solution)/shard_map/ppermute | solution.py:482
  88.7 0.7 collective-permute-start.23
  89.5 0.2 collective-permute-start.22
  89.7 1.4 %rest_two.1 = (f32[2,1,64,128]{3,2,1,0:T(8,128)}, f32[64,128]{1,0:T(8,128)S(1)}) custom-call(s32[5]{0:T(128)S(1)} %stack.15.ids_ref, f32[2,8,72,256]{3,2,1,0:T(8,128)S(1)} %get-tuple-element.90.cur_ref, f32[8,64,256]{2,1,0:T(8,128)S(1)} %get-tuple-element.92.east_ref, f32[8,72,128]{2,1,0:T(8,128)S(1)} %get-tuple-element.93.north_ref, ...), custom_call_target="tpu_custom_call" | custom-call | tf_op jit(solution)/shard_map/rest_two/pallas_call | solution.py:23
  91.1 0.1 exchange_two.1
  91.2 0.0 collective-permute-done.24.t3
  91.3 3.3 %collective-permute-done.23.t2 = f32[2,64,128]{2,1,0:T(8,128)S(1)} collective-permute-done((f32[2,64,128]{2,1,0:T(8,128)S(1)}, f32[2,64,128]{2,1,0:T(8,128)S(1)}, u32[]{:S(2)}, u32[]{:S(2)}) %collective-permute-start.23) | collective-permute-done | bytes 65568 | tf_op jit(solution)/shard_map/ppermute | solution.py:482
  94.5 0.7 collective-permute-done.22.t1
  95.2 1.7 %biology_two.1 = (f32[3,8,64,128]{3,2,1,0:T(8,128)}, f32[1,64,128]{2,1,0:T(8,128)}) custom-call(s32[5]{0:T(128)S(1)} %stack.15.ids_ref, f32[8,64,128]{2,1,0:T(8,128)S(1)} %get-tuple-element.96.grow_ref, f32[8,64,128]{2,1,0:T(8,128)S(1)} %get-tuple-element.97.n_ref, f32[8,64,128]{2,1,0:T(8,128)S(1)} %get-tuple-element.98.p_ref, ...), custom_call_target="tpu_custom_call" | custom-call | tf_op jit(solution)/shard_map/biology_two/pallas_call | solution.py:23
  (29 shorter events, 0.1 us)
Async XLA Ops:
  0.6 13.8 %collective-permute-start = (f32[2,1,64,128]{3,2,1,0:T(8,128)}, f32[2,1,64,128]{3,2,1,0:T(8,128)S(1)}, u32[]{:S(2)}, u32[]{:S(2)}) collective-permute-start(f32[2,1,64,128]{3,2,1,0:T(8,128)} %flow_ref.3), channel_id=1, source_target_pairs={{0,4},{1,5},{2,6},{3,7},{4,0},{5,1},{6,2},{7,3},{8,12},{9,13},{10,... | collective-permute-start | bytes 196616 | tf_op jit(solution)/shard_map/ppermute | solution.py:478
  7.9 0.9 copy-start.4
  8.8 5.6 %copy-start.5 = (f32[2,1,64,128]{3,2,1,0:T(8,128)S(1)}, f32[2,1,64,128]{3,2,1,0:T(8,128)}, u32[]{:S(2)}) copy-start(f32[2,1,64,128]{3,2,1,0:T(8,128)} %flow_ref.3) | copy-start | bytes 196612
  8.9 1.1 %copy-start = (f32[3,8,64,128]{3,2,1,0:T(8,128)S(1)}, f32[3,8,64,128]{3,2,1,0:T(8,128)}, u32[]{:S(2)}) copy-start(f32[3,8,64,128]{3,2,1,0:T(8,128)} %c_ref.7) | copy-start | bytes 2359300
  10.0 0.9 copy-start.2
  11.0 0.8 copy-start.6
  11.7 0.8 copy-start.7
  12.5 0.8 copy-start.8
  13.2 0.8 copy-start.9
  14.0 22.0 %copy-start.1 = (f32[3,8,64,128]{3,2,1,0:T(8,128)S(1)}, f32[3,8,64,128]{3,2,1,0:T(8,128)}, u32[]{:S(2)}) copy-start(f32[3,8,64,128]{3,2,1,0:T(8,128)} %c_ref.7) | copy-start | bytes 2359300
  14.0 22.0 %copy-start.3 = (f32[8,64,128]{2,1,0:T(8,128)S(1)}, f32[8,64,128]{2,1,0:T(8,128)}, u32[]{:S(2)}) copy-start(f32[8,64,128]{2,1,0:T(8,128)} %dif_ref.3) | copy-start | bytes 786436
  14.5 6.8 %collective-permute-start.5 = (f32[3,64,128]{2,1,0:T(8,128)S(1)}, f32[3,64,128]{2,1,0:T(8,128)S(1)}, u32[]{:S(2)}, u32[]{:S(2)}) collective-permute-start(f32[3,64,128]{2,1,0:T(8,128)S(1)} %get-tuple-element.62), channel_id=1, source_target_pairs={{64,0},{65,1},{66,2},{67,3},{68,4},{69,5},{70,6},{71,7},{128,64},{... | collective-permute-start | bytes 294920 | tf_op jit(solution)/shard_map/ppermute | solution.py:463
  15.2 6.2 %collective-permute-start.4 = (f32[3,64,128]{2,1,0:T(8,128)S(1)}, f32[3,64,128]{2,1,0:T(8,128)S(1)}, u32[]{:S(2)}, u32[]{:S(2)}) collective-permute-start(f32[3,64,128]{2,1,0:T(8,128)S(1)} %get-tuple-element.62), channel_id=1, source_target_pairs={{0,64},{1,65},{2,66},{3,67},{4,68},{5,69},{6,70},{7,71},{64,128},{... | collective-permute-start | bytes 294920 | tf_op jit(solution)/shard_map/ppermute | solution.py:463
  16.6 13.9 %collective-permute-start.3 = (f32[2,128,128]{2,1,0:T(8,128)S(1)}, f32[2,128,128]{2,1,0:T(8,128)S(1)}, u32[]{:S(2)}, u32[]{:S(2)}) collective-permute-start(f32[2,128,128]{2,1,0:T(8,128)S(1)} %get-tuple-element.61.g0), channel_id=1, source_target_pairs={{0,3},{1,0},{2,1},{3,2},{4,7},{5,4},{6,5},{7,6},{8,11},{9,8},{10,9... | collective-permute-start | bytes 393224 | tf_op jit(solution)/shard_map/ppermute | solution.py:482
  19.6 11.2 %collective-permute-start.2 = (f32[2,128,128]{2,1,0:T(8,128)S(1)}, f32[2,128,128]{2,1,0:T(8,128)S(1)}, u32[]{:S(2)}, u32[]{:S(2)}) collective-permute-start(f32[2,128,128]{2,1,0:T(8,128)S(1)} %get-tuple-element.61.g0), channel_id=1, source_target_pairs={{0,2},{1,3},{2,0},{3,1},{4,6},{5,7},{6,4},{7,5},{8,10},{9,11},{10,... | collective-permute-start | bytes 393224 | tf_op jit(solution)/shard_map/ppermute | solution.py:482
  20.3 10.6 %collective-permute-start.1 = (f32[2,128,128]{2,1,0:T(8,128)S(1)}, f32[2,128,128]{2,1,0:T(8,128)S(1)}, u32[]{:S(2)}, u32[]{:S(2)}) collective-permute-start(f32[2,128,128]{2,1,0:T(8,128)S(1)} %get-tuple-element.61.g0), channel_id=1, source_target_pairs={{0,1},{1,2},{2,3},{3,0},{4,5},{5,6},{6,7},{7,4},{8,9},{9,10},{10,1... | collective-permute-start | bytes 393224 | tf_op jit(solution)/shard_map/ppermute | solution.py:482
  21.9 4.0 %collective-permute-start.6 = (f32[176,128]{1,0:T(8,128)S(1)}, f32[176,128]{1,0:T(8,128)S(1)}, u32[]{:S(2)}, u32[]{:S(2)}) collective-permute-start(f32[176,128]{1,0:T(8,128)S(1)} %get-tuple-element.66), channel_id=1, source_target_pairs={{0,8},{8,16},{16,24},{24,32},{32,40},{40,48},{48,56},{56,0},{1,9},... | collective-permute-start | bytes 270344 | tf_op jit(solution)/shard_map/ppermute | solution.py:470
  21.9 3.9 %collective-permute-start.7 = (f32[176,128]{1,0:T(8,128)S(1)}, f32[176,128]{1,0:T(8,128)S(1)}, u32[]{:S(2)}, u32[]{:S(2)}) collective-permute-start(f32[176,128]{1,0:T(8,128)S(1)} %get-tuple-element.67), channel_id=1, source_target_pairs={{8,0},{16,8},{24,16},{32,24},{40,32},{48,40},{56,48},{0,56},{9,1},... | collective-permute-start | bytes 270344 | tf_op jit(solution)/shard_map/ppermute | solution.py:470
  26.5 4.4 %collective-permute-start.10 = (f32[2,32,128]{2,1,0:T(8,128)S(1)}, f32[2,32,128]{2,1,0:T(8,128)S(1)}, u32[]{:S(2)}, u32[]{:S(2)}) collective-permute-start(f32[2,32,128]{2,1,0:T(8,128)S(1)} %get-tuple-element.68.e0), channel_id=1, source_target_pairs={{0,3},{1,0},{2,1},{3,2},{4,7},{5,4},{6,5},{7,6},{8,11},{9,8},{10,9... | collective-permute-start | bytes 98312 | tf_op jit(solution)/shard_map/ppermute | solution.py:482
  29.3 5.4 %collective-permute-start.9 = (f32[2,32,128]{2,1,0:T(8,128)S(1)}, f32[2,32,128]{2,1,0:T(8,128)S(1)}, u32[]{:S(2)}, u32[]{:S(2)}) collective-permute-start(f32[2,32,128]{2,1,0:T(8,128)S(1)} %get-tuple-element.68.e0), channel_id=1, source_target_pairs={{0,2},{1,3},{2,0},{3,1},{4,6},{5,7},{6,4},{7,5},{8,10},{9,11},{10,... | collective-permute-start | bytes 98312 | tf_op jit(solution)/shard_map/ppermute | solution.py:482
  30.5 5.5 %collective-permute-start.8 = (f32[2,32,128]{2,1,0:T(8,128)S(1)}, f32[2,32,128]{2,1,0:T(8,128)S(1)}, u32[]{:S(2)}, u32[]{:S(2)}) collective-permute-start(f32[2,32,128]{2,1,0:T(8,128)S(1)} %get-tuple-element.68.e0), channel_id=1, source_target_pairs={{0,1},{1,2},{2,3},{3,0},{4,5},{5,6},{6,7},{7,4},{8,9},{9,10},{10,1... | collective-permute-start | bytes 98312 | tf_op jit(solution)/shard_map/ppermute | solution.py:482
  39.8 7.2 %collective-permute-start.11 = (f32[144,128]{1,0:T(8,128)S(1)}, f32[144,128]{1,0:T(8,128)S(1)}, u32[]{:S(2)}, u32[]{:S(2)}) collective-permute-start(f32[144,128]{1,0:T(8,128)S(1)} %get-tuple-element.85), channel_id=1, source_target_pairs={{0,1},{1,2},{2,3},{3,0},{4,5},{5,6},{6,7},{7,4},{8,9},{9,10},{10,1... | collective-permute-start | bytes 221192 | tf_op jit(solution)/shard_map/ppermute | solution.py:494
  39.9 7.1 %collective-permute-start.12 = (f32[144,128]{1,0:T(8,128)S(1)}, f32[144,128]{1,0:T(8,128)S(1)}, u32[]{:S(2)}, u32[]{:S(2)}) collective-permute-start(f32[144,128]{1,0:T(8,128)S(1)} %get-tuple-element.86), channel_id=1, source_target_pairs={{0,2},{1,3},{2,0},{3,1},{4,6},{5,7},{6,4},{7,5},{8,10},{9,11},{10,... | collective-permute-start | bytes 221192 | tf_op jit(solution)/shard_map/ppermute | solution.py:494
  41.3 6.3 %collective-permute-start.13 = (f32[144,128]{1,0:T(8,128)S(1)}, f32[144,128]{1,0:T(8,128)S(1)}, u32[]{:S(2)}, u32[]{:S(2)}) collective-permute-start(f32[144,128]{1,0:T(8,128)S(1)} %get-tuple-element.87), channel_id=1, source_target_pairs={{0,3},{1,0},{2,1},{3,2},{4,7},{5,4},{6,5},{7,6},{8,11},{9,8},{10,9... | collective-permute-start | bytes 221192 | tf_op jit(solution)/shard_map/ppermute | solution.py:494
  47.6 13.4 %copy-start.10 = (f32[3]{0:T(128)S(1)}, f32[3]{0:T(128)}, u32[]{:S(2)}) copy-start(f32[3]{0:T(128)} %rate_ref.1) | copy-start | bytes 40
  47.6 8.3 %collective-permute-start.14 = (f32[144,128]{1,0:T(8,128)S(1)}, f32[144,128]{1,0:T(8,128)S(1)}, u32[]{:S(2)}, u32[]{:S(2)}) collective-permute-start(f32[144,128]{1,0:T(8,128)S(1)} %add_y.2.refs_0_), channel_id=1, source_target_pairs={{0,4},{1,5},{2,6},{3,7},{4,0},{5,1},{6,2},{7,3},{8,12},{9,13},{10,... | collective-permute-start | bytes 221192 | tf_op jit(solution)/shard_map/ppermute | solution.py:478
  55.9 7.3 %collective-permute-start.17 = (f32[144,128]{1,0:T(8,128)S(1)}, f32[144,128]{1,0:T(8,128)S(1)}, u32[]{:S(2)}, u32[]{:S(2)}) collective-permute-start(f32[144,128]{1,0:T(8,128)S(1)} %add_z.2.t0), channel_id=1, source_target_pairs={{0,3},{1,0},{2,1},{3,2},{4,7},{5,4},{6,5},{7,6},{8,11},{9,8},{10,9... | collective-permute-start | bytes 221192 | tf_op jit(solution)/shard_map/ppermute | solution.py:482
  60.0 6.0 %collective-permute-start.16 = (f32[144,128]{1,0:T(8,128)S(1)}, f32[144,128]{1,0:T(8,128)S(1)}, u32[]{:S(2)}, u32[]{:S(2)}) collective-permute-start(f32[144,128]{1,0:T(8,128)S(1)} %add_z.2.t0), channel_id=1, source_target_pairs={{0,2},{1,3},{2,0},{3,1},{4,6},{5,7},{6,4},{7,5},{8,10},{9,11},{10,... | collective-permute-start | bytes 221192 | tf_op jit(solution)/shard_map/ppermute | solution.py:482
  60.0 6.4 %collective-permute-start.15 = (f32[144,128]{1,0:T(8,128)S(1)}, f32[144,128]{1,0:T(8,128)S(1)}, u32[]{:S(2)}, u32[]{:S(2)}) collective-permute-start(f32[144,128]{1,0:T(8,128)S(1)} %add_z.2.t0), channel_id=1, source_target_pairs={{0,1},{1,2},{2,3},{3,0},{4,5},{5,6},{6,7},{7,4},{8,9},{9,10},{10,1... | collective-permute-start | bytes 221192 | tf_op jit(solution)/shard_map/ppermute | solution.py:482
  69.7 6.2 %collective-permute-start.18 = (f32[2,64,128]{2,1,0:T(8,128)S(1)}, f32[2,64,128]{2,1,0:T(8,128)S(1)}, u32[]{:S(2)}, u32[]{:S(2)}) collective-permute-start(f32[2,64,128]{2,1,0:T(8,128)S(1)} %get-tuple-element.101), channel_id=1, source_target_pairs={{0,1},{1,2},{2,3},{3,0},{4,5},{5,6},{6,7},{7,4},{8,9},{9,10},{10,1... | collective-permute-start | bytes 196616 | tf_op jit(solution)/shard_map/ppermute | solution.py:494
  69.7 6.2 %collective-permute-start.19 = (f32[2,64,128]{2,1,0:T(8,128)S(1)}, f32[2,64,128]{2,1,0:T(8,128)S(1)}, u32[]{:S(2)}, u32[]{:S(2)}) collective-permute-start(f32[2,64,128]{2,1,0:T(8,128)S(1)} %get-tuple-element.102), channel_id=1, source_target_pairs={{0,2},{1,3},{2,0},{3,1},{4,6},{5,7},{6,4},{7,5},{8,10},{9,11},{10,... | collective-permute-start | bytes 196616 | tf_op jit(solution)/shard_map/ppermute | solution.py:494
  72.1 4.7 %collective-permute-start.20 = (f32[2,64,128]{2,1,0:T(8,128)S(1)}, f32[2,64,128]{2,1,0:T(8,128)S(1)}, u32[]{:S(2)}, u32[]{:S(2)}) collective-permute-start(f32[2,64,128]{2,1,0:T(8,128)S(1)} %get-tuple-element.103), channel_id=1, source_target_pairs={{0,3},{1,0},{2,1},{3,2},{4,7},{5,4},{6,5},{7,6},{8,11},{9,8},{10,9... | collective-permute-start | bytes 196616 | tf_op jit(solution)/shard_map/ppermute | solution.py:494
  76.8 9.2 %collective-permute-start.21 = (f32[2,64,128]{2,1,0:T(8,128)S(1)}, f32[2,64,128]{2,1,0:T(8,128)S(1)}, u32[]{:S(2)}, u32[]{:S(2)}) collective-permute-start(f32[2,64,128]{2,1,0:T(8,128)S(1)} %add_y.3.refs_0_), channel_id=1, source_target_pairs={{0,4},{1,5},{2,6},{3,7},{4,0},{5,1},{6,2},{7,3},{8,12},{9,13},{10,... | collective-permute-start | bytes 196616 | tf_op jit(solution)/shard_map/ppermute | solution.py:478
  86.0 5.3 %collective-permute-start.24 = (f32[2,64,128]{2,1,0:T(8,128)S(1)}, f32[2,64,128]{2,1,0:T(8,128)S(1)}, u32[]{:S(2)}, u32[]{:S(2)}) collective-permute-start(f32[2,64,128]{2,1,0:T(8,128)S(1)} %add_z.3.t0), channel_id=1, source_target_pairs={{0,3},{1,0},{2,1},{3,2},{4,7},{5,4},{6,5},{7,6},{8,11},{9,8},{10,9... | collective-permute-start | bytes 196616 | tf_op jit(solution)/shard_map/ppermute | solution.py:482
  88.7 5.8 %collective-permute-start.23 = (f32[2,64,128]{2,1,0:T(8,128)S(1)}, f32[2,64,128]{2,1,0:T(8,128)S(1)}, u32[]{:S(2)}, u32[]{:S(2)}) collective-permute-start(f32[2,64,128]{2,1,0:T(8,128)S(1)} %add_z.3.t0), channel_id=1, source_target_pairs={{0,2},{1,3},{2,0},{3,1},{4,6},{5,7},{6,4},{7,5},{8,10},{9,11},{10,... | collective-permute-start | bytes 196616 | tf_op jit(solution)/shard_map/ppermute | solution.py:482
  89.5 5.8 %collective-permute-start.22 = (f32[2,64,128]{2,1,0:T(8,128)S(1)}, f32[2,64,128]{2,1,0:T(8,128)S(1)}, u32[]{:S(2)}, u32[]{:S(2)}) collective-permute-start(f32[2,64,128]{2,1,0:T(8,128)S(1)} %add_z.3.t0), channel_id=1, source_target_pairs={{0,1},{1,2},{2,3},{3,0},{4,5},{5,6},{6,7},{7,4},{8,9},{9,10},{10,1... | collective-permute-start | bytes 196616 | tf_op jit(solution)/shard_map/ppermute | solution.py:482
